TPU v7x, 256 devices: a whole 4x4x8 slice. The times are simulated.
256 devices in a mesh: member: 2 (over core), tp: 128 (over x, z, y).
Axes of the slice: x: 4, y: 4, z: 8, core: 2. Of those that a mesh axis runs over, the one named last changes fastest.
Arguments:
- stream_in: bfloat16 [512, 4096], P(('member', 'tp')), may hold values from -6 to 6
- kv_cache: bfloat16 [512, 512, 2048], P(('member', 'tp')), may hold values from -400 to 400
- lengths: int32 [128], replicated, may hold values from 1 to 512
- targets: int32 [128], replicated, may hold values from 0 to 65535
- norm_gains: float32 [3, 4096], replicated, may hold values from 0.1 to 1.9
- w_qkv: bfloat16 [4096, 6144], P(None, 'tp'), may hold values from -0.09375 to 0.09375
- w_out: bfloat16 [4096, 4096], P('tp'), may hold values from -0.09375 to 0.09375
- w_gate_up: bfloat16 [2, 4096, 14336], P(None, None, 'tp'), may hold values from -0.09375 to 0.09375
- w_down: bfloat16 [14336, 4096], P('tp'), may hold values from -0.046875 to 0.046875
- lm_head: bfloat16 [4096, 65536], P(None, 'tp'), may hold values from -300 to 300
- fast_in: float32 [4, 2, 4096], P('member'), may hold values from 0.1 to 1.9
- fast_hidden: float32 [4, 3, 14336], P('member', None, 'tp'), may hold values from 0.1 to 1.9
- fast_out: float32 [4, 4096], P('member'), may hold values from 0.1 to 1.9
Outputs:
- mean_logits: bfloat16 [128, 65536], P(None, 'tp')
- token_logprob: float32 [128], replicated
Inputs may be any that keep to these rules, and one draw needn't show every extreme that they name: lengths is the same for all members.
All inputs are finite; a program needn't handle non-finite values.
Results may differ from a plain program's by a relative error of at most 0.02.
Values may be sent and summed in bfloat16 or wider, within the bound.
A program may use at most 128 MiB of HBM per device.

v0:
```python
import jax
import jax.numpy as jnp
from jax import lax
from jax.sharding import Mesh
from jax.sharding import PartitionSpec as P

HEADS = 32
KV = 8
HD = 128
CACHE = 512
TP = ("tp_0", "tp_1", "tp_2")
MEMBER_TP = ("member", "tp_0", "tp_1", "tp_2")


ROPE_BASE = 500000.0


def from_everyone(array, axis):
    copies = jnp.broadcast_to(array, (lax.axis_size(axis), *array.shape))
    return lax.all_to_all(copies, axis, split_axis=0, concat_axis=0, tiled=True)


def in_order(blocks, dim):
    lengths = list(blocks.shape[1:])
    lengths[dim] *= blocks.shape[0]
    return jnp.moveaxis(blocks, 0, dim).reshape(lengths)


def gather_axes(array, axes, dim):
    far, near = axes
    blocks = from_everyone(from_everyone(array, far), near)
    return in_order(blocks.swapaxes(0, 1).reshape(-1, *array.shape), dim)


def rows_for(lines, length):
    spare = -lines.shape[0] % length
    if not spare:
        return lines
    return jnp.concatenate([lines, jnp.zeros((spare, *lines.shape[1:]), lines.dtype)])


def cut_along(array, dim, length):
    before, after = (array.shape[:dim], array.shape[dim + 1 :])
    return jnp.moveaxis(array.reshape(*before, length, -1, *after), dim, 0)


def summed_on_arrival(array, axis, dim):
    length = lax.axis_size(axis)
    blocks = lax.all_to_all(cut_along(array, dim, length), axis, 0, 0, tiled=True)
    return jnp.sum(blocks, axis=0)


def sum_by_axis(array, axes, dim):
    far, near = axes
    own = summed_on_arrival(cut_along(array, dim, lax.axis_size(far)), near, dim + 1)
    return jnp.sum(lax.all_to_all(own, far, 0, 0, tiled=True), axis=0)


def nested_sum(array, axes):
    lines = array.reshape(-1, array.shape[-1])
    padded = rows_for(lines, lax.axis_size(axes[0]) * lax.axis_size(axes[1]))
    whole = gather_axes(sum_by_axis(padded, axes, 0), axes, 0)
    return lax.slice_in_dim(whole, 0, len(lines)).reshape(array.shape)


def sent_and_summed(array, axis, dim):
    length = lax.axis_size(axis)
    blocks = lax.all_to_all(cut_along(array, dim, length), axis, 0, 0, tiled=True)
    return jnp.sum(blocks.astype(jnp.float32), axis=0)


def sum_in_two_steps(array, axes, dim):
    far, near = axes
    own = sent_and_summed(cut_along(array, dim, lax.axis_size(far)), near, dim + 1)
    return jnp.sum(
        lax.all_to_all(own.astype(jnp.bfloat16), far, 0, 0, tiled=True).astype(jnp.float32), axis=0
    )


def nested_sum_2(array, axes):
    lines = array.reshape(-1, array.shape[-1])
    own = sum_in_two_steps(
        rows_for(lines, lax.axis_size(axes[0]) * lax.axis_size(axes[1])), axes, 0
    )
    whole = gather_axes(own.astype(jnp.bfloat16), axes, 0)
    return whole[: len(lines)].reshape(array.shape).astype(jnp.float32)


def taken_together(array, axis):
    everything = from_everyone(array, axis)
    return jnp.sum(everything.astype(jnp.float32), axis=0)


def collected_together(array, axis):
    leaves = jax.tree.leaves(array)
    sequence = sorted(range(len(leaves)), key=lambda k: -leaves[k].size)
    width = (1, *leaves[sequence[0]].shape)[-1]
    lines = [
        jnp.pad(leaves[k].reshape(-1), (0, -leaves[k].size % width)).reshape(-1, width)
        for k in sequence
    ]
    both, at, found = (lax.all_gather(jnp.concatenate(lines), axis), 0, {})
    for k, line in zip(sequence, lines):
        section = both[:, at : at + len(line)].reshape(len(both), -1)
        found[k] = section[:, : leaves[k].size].reshape(-1, *leaves[k].shape)
        at += len(line)
    numbers = iter(range(len(leaves)))
    return jax.tree.map(lambda _: found[next(numbers)], array)


def combined_by_axis(array, axes, combine):
    for axis in axes:
        pieces = collected_together(array, axis)
        array = jax.tree.map(lambda part: part[0], pieces)
        for k in range(1, lax.axis_size(axis)):
            array = combine(array, jax.tree.map(lambda part: part[k], pieces))
    return array


def rms_norm(values_in, gain):
    return (
        values_in
        * lax.rsqrt(jnp.mean(values_in * values_in, axis=-1, keepdims=True) + 1e-05)
        * gain
    )


def rotate(values_in, positions):
    half_dim = values_in.shape[-1] // 2
    frequency = ROPE_BASE ** (-jnp.arange(half_dim, dtype=jnp.float32) * 2.0 / values_in.shape[-1])
    angles = positions.astype(jnp.float32)[:, None, None] * frequency[None, None, :]
    lower_half = values_in[..., :half_dim]
    upper_half = values_in[..., half_dim:]
    return jnp.concatenate(
        [
            lower_half * jnp.cos(angles) - upper_half * jnp.sin(angles),
            upper_half * jnp.cos(angles) + lower_half * jnp.sin(angles),
        ],
        axis=-1,
    )


def attend(projected, cache_rows, positions):
    row_count = projected.shape[0]
    head_cols = HEADS * HD
    kv_cols = KV * HD
    queries = rotate(
        projected[:, :head_cols].astype(jnp.float32).reshape(row_count, HEADS, HD), positions
    ).astype(jnp.bfloat16)
    new_key = rotate(
        projected[:, head_cols : head_cols + kv_cols]
        .astype(jnp.float32)
        .reshape(row_count, KV, HD),
        positions,
    ).astype(jnp.bfloat16)
    new_value = projected[:, head_cols + kv_cols :].reshape(row_count, KV, HD)
    cache_keys = cache_rows[:, :, :kv_cols].reshape(row_count, CACHE, KV, HD)
    cache_values = cache_rows[:, :, kv_cols:].reshape(row_count, CACHE, KV, HD)
    grouped = queries.reshape(row_count, KV, HEADS // KV, HD)
    inv_root = HD ** (-0.5)
    cached = (
        jnp.einsum("rkgd,rckd->rkgc", grouped, cache_keys, preferred_element_type=jnp.float32)
        * inv_root
    )
    fresh = (
        jnp.einsum("rkgd,rkd->rkg", grouped, new_key, preferred_element_type=jnp.float32) * inv_root
    )
    in_cache = jnp.arange(CACHE)[None, :] < positions[:, None]
    cached = jnp.where(in_cache[:, None, None, :], cached, -1e30)
    peak = jnp.maximum(jnp.max(cached, axis=-1), fresh)
    weights = jnp.exp(cached - peak[..., None])
    fresh_w = jnp.exp(fresh - peak)
    total_sum = jnp.sum(weights, axis=-1) + fresh_w
    probs = (weights / total_sum[..., None]).astype(jnp.bfloat16)
    fresh_p = (fresh_w / total_sum).astype(jnp.bfloat16)
    result = jnp.einsum("rkgc,rckd->rkgd", probs, cache_values, preferred_element_type=jnp.float32)
    result = (
        result
        + fresh_p.astype(jnp.float32)[..., None] * new_value.astype(jnp.float32)[:, :, None, :]
    )
    return result.reshape(row_count, HEADS * HD).astype(jnp.bfloat16)


def combine_soft(earlier, later):
    peak = jnp.maximum(earlier[0], later[0])
    total_sum = earlier[1] * jnp.exp(earlier[0] - peak) + later[1] * jnp.exp(later[0] - peak)
    return (peak, total_sum, earlier[2] + later[2])


def body(
    stream_in,
    kv_cache,
    lengths,
    targets,
    norm_gains,
    w_qkv,
    w_out,
    w_gate_up,
    w_down,
    lm_head,
    fast_in,
    fast_hidden,
    fast_out,
):
    tp_count = lax.axis_size(TP)
    tp_rank = lax.axis_index(TP)
    mem_dev = fast_in.shape[0]
    batch_rows = lengths.shape[0]
    own_rows = stream_in.shape[0]
    all_rows = own_rows * tp_count
    width = stream_in.shape[1]
    first_row = tp_rank * own_rows
    positions = lax.dynamic_slice_in_dim(lengths, first_row % batch_rows, own_rows, 0)
    stream_all = gather_axes(stream_in, (("tp_0", "tp_1"), "tp_2"), 0)
    attn_in = rms_norm(stream_all.astype(jnp.float32), norm_gains[0]).astype(jnp.bfloat16)
    projected = jnp.dot(attn_in, w_qkv, preferred_element_type=jnp.float32).astype(jnp.bfloat16)
    row_major = lax.all_to_all(projected, TP, split_axis=0, concat_axis=1, tiled=True)
    attended = attend(row_major, kv_cache, positions)
    head_major = lax.all_to_all(attended, TP, split_axis=1, concat_axis=0, tiled=True)
    attn_sum = nested_sum(
        jnp.dot(head_major, w_out, preferred_element_type=jnp.float32), (("tp_0", "tp_1"), "tp_2")
    )
    middle = (stream_all.astype(jnp.float32) + attn_sum).astype(jnp.bfloat16)
    ffn_in = rms_norm(middle.astype(jnp.float32), norm_gains[1]).astype(jnp.bfloat16)
    grouped = ffn_in.astype(jnp.float32).reshape(mem_dev, batch_rows, width)
    gate_in = (grouped * fast_in[:, 0][:, None, :]).astype(jnp.bfloat16).reshape(all_rows, width)
    up_in = (grouped * fast_in[:, 1][:, None, :]).astype(jnp.bfloat16).reshape(all_rows, width)
    hidden_cols = w_gate_up.shape[2]
    gate_act = (
        jnp.dot(gate_in, w_gate_up[0], preferred_element_type=jnp.float32).reshape(
            mem_dev, batch_rows, hidden_cols
        )
        * fast_hidden[:, 0][:, None, :]
    )
    up_act = (
        jnp.dot(up_in, w_gate_up[1], preferred_element_type=jnp.float32).reshape(
            mem_dev, batch_rows, hidden_cols
        )
        * fast_hidden[:, 1][:, None, :]
    )
    hidden = (
        (jax.nn.silu(gate_act) * up_act * fast_hidden[:, 2][:, None, :])
        .astype(jnp.bfloat16)
        .reshape(all_rows, hidden_cols)
    )
    down_sum = nested_sum_2(
        jnp.dot(hidden, w_down, preferred_element_type=jnp.float32).astype(jnp.bfloat16),
        (("tp_0", "tp_1"), "tp_2"),
    )
    scaled = down_sum.reshape(mem_dev, batch_rows, width) * fast_out[:, None, :]
    layer_out = (
        (middle.astype(jnp.float32).reshape(mem_dev, batch_rows, width) + scaled)
        .astype(jnp.bfloat16)
        .reshape(all_rows, width)
    )
    final_in = rms_norm(layer_out.astype(jnp.float32), norm_gains[2]).astype(jnp.bfloat16)
    logits = jnp.dot(final_in, lm_head, preferred_element_type=jnp.float32)
    vocab_cols = lm_head.shape[1]
    member_total = jnp.sum(logits.reshape(mem_dev, batch_rows, vocab_cols), axis=0)
    member_count = mem_dev * lax.axis_size("member")
    mean_logit = (
        taken_together(member_total.astype(jnp.bfloat16), "member").astype(jnp.float32)
        / member_count
    )
    column_ids = tp_rank * vocab_cols + jnp.arange(vocab_cols)
    target_part = jnp.sum(
        jnp.where(column_ids[None, :] == targets[:, None], mean_logit, 0.0), axis=-1
    )
    local_peak = jnp.max(mean_logit, axis=-1)
    local_total = jnp.sum(jnp.exp(mean_logit - local_peak[:, None]), axis=-1)
    peak, exp_total, target_logit = combined_by_axis(
        (local_peak, local_total, target_part), TP, combine_soft
    )
    token_logprob = target_logit - (peak + jnp.log(exp_total))
    return (mean_logit.astype(jnp.bfloat16), token_logprob)


def solution(mesh):
    split = Mesh(
        mesh.devices.reshape(mesh.shape["member"], 4, 8, 4), ("member", "tp_0", "tp_1", "tp_2")
    )
    return jax.shard_map(
        body,
        mesh=split,
        in_specs=(
            P(MEMBER_TP, None),
            P(MEMBER_TP, None, None),
            P(),
            P(),
            P(),
            P(None, TP),
            P(TP, None),
            P(None, None, TP),
            P(TP, None),
            P(None, TP),
            P("member", None, None),
            P("member", None, TP),
            P("member", None),
        ),
        out_specs=(P(None, TP), P()),
        check_vma=False,
    )
```

profile of v0, /device:TPU:32, one launch (start us, length us, event | category | flops | bytes accessed | tf_op | source)
XLA Modules:
  0.0 498.8 jit_solution(14742596613530918622)
XLA Ops:
  2.7 11.2 %all-to-all-start = ((bf16[32,2,4096]{2,1,0:T(2,128)(2,1)}), bf16[32,2,4096]{2,1,0:T(2,128)(2,1)S(1)}, u32[]{:S(2)}, u32[]{:S(2)}) async-start(bf16[32,2,4096]{2,1,0:T(2,128)(2,1)} %broadcast_in_dim.29), calls=%async_computation | async-start | bytes 1048576 | tf_op jit(solution)/shard_map/all_to_all | solution.py:20
  14.7 16.9 %all-to-all-done = bf16[32,2,4096]{2,1,0:T(2,128)(2,1)S(1)} async-done(((bf16[32,2,4096]{2,1,0:T(2,128)(2,1)}), bf16[32,2,4096]{2,1,0:T(2,128)(2,1)S(1)}, u32[]{:S(2)}, u32[]{:S(2)}) %all-to-all-start) | async-done | bytes 524320 | tf_op jit(solution)/shard_map/all_to_all | solution.py:20
  44.3 19.3 %all-to-all-done.1 = bf16[4,32,2,4096]{3,2,1,0:T(2,128)(2,1)S(1)} async-done(((bf16[4,32,2,4096]{3,2,1,0:T(2,128)(2,1)}), bf16[4,32,2,4096]{3,2,1,0:T(2,128)(2,1)S(1)}, u32[]{:S(2)}, u32[]{:S(2)}) %all-to-all-start.1) | async-done | bytes 2097184 | tf_op jit(solution)/shard_map/all_to_all | solution.py:20
  70.5 6.1 %reshape.1071 = f32[256,4096]{1,0:T(8,128)} reshape(f32[32,4,2,4096]{3,2,1,0:T(2,128)} %copy.111) | data formatting | bytes 8388608 | tf_op jit(solution)/shard_map/convert_element_type | solution.py:223
  82.8 8.3 %all-to-all-start.2 = ((bf16[128,2,48]{2,1,0:T(2,128)(2,1)}), bf16[128,2,48]{2,1,0:T(2,128)(2,1)S(1)}, u32[]{:S(2)}, u32[]{:S(2)}) async-start(bf16[128,2,48]{2,1,0:T(2,128)(2,1)} %bitcast.3), calls=%async_computation.2 | async-start | bytes 131072 | tf_op jit(solution)/shard_map/all_to_all | solution.py:217
  107.8 21.7 %all_to_all.87 = bf16[2,128,32]{2,0,1:T(2,128)(2,1)S(1)} all-to-all(bf16[2,128,32]{2,0,1:T(2,128)(2,1)S(1)} %copy.121), channel_id=1, replica_groups=mesh['member'=2,'tp_0'=4,'tp_1'=8,'tp_2'=4] {'tp_0','tp_1','tp_2'}, dimensions={1} | all-to-all | bytes 32768 | tf_op jit(solution)/shard_map/all_to_all | solution.py:219
  130.2 49.4 %all_to_all.88 = f32[4,32,2,4096]{3,1,2,0:T(8,128)} all-to-all(f32[4,32,2,4096]{3,1,2,0:T(8,128)S(1)} %convolution_bitcast_fusion), channel_id=1, replica_groups=mesh['member'=2,'tp_0'=4,'tp_1'=8,'tp_2'=4] {'tp_2'}, dimensions={0} | all-to-all | bytes 8388608 | tf_op jit(solution)/shard_map/all_to_all | solution.py:49
  185.1 29.7 %all_to_all.89 = f32[32,2,4096]{2,1,0:T(2,128)} all-to-all(f32[32,2,4096]{2,1,0:T(2,128)S(1)} %copy.124), channel_id=1, replica_groups=mesh['member'=2,'tp_0'=4,'tp_1'=8,'tp_2'=4] {'tp_0','tp_1'}, dimensions={0} | all-to-all | bytes 2097152 | tf_op jit(solution)/shard_map/all_to_all | solution.py:56
  216.8 29.3 %all_to_all.90 = f32[32,2,4096]{2,1,0:T(2,128)S(1)} all-to-all(f32[32,2,4096]{2,1,0:T(2,128)S(1)} %broadcast_in_dim.34), channel_id=1, replica_groups=mesh['member'=2,'tp_0'=4,'tp_1'=8,'tp_2'=4] {'tp_0','tp_1'}, dimensions={0} | all-to-all | bytes 2097152 | tf_op jit(solution)/shard_map/all_to_all | solution.py:20
  250.1 5.5 %all-to-all-start.7 = ((f32[4,32,2,4096]{3,2,1,0:T(2,128)}), f32[4,32,2,4096]{3,2,1,0:T(2,128)}, u32[]{:S(2)}, u32[]{:S(2)}) async-start(f32[4,32,2,4096]{3,2,1,0:T(2,128)} %broadcast_in_dim.60), calls=%async_computation.7 | async-start | bytes 8388608 | tf_op jit(solution)/shard_map/all_to_all | solution.py:20
  255.8 43.5 %all-to-all-done.7 = f32[4,32,2,4096]{3,2,1,0:T(2,128)} async-done(((f32[4,32,2,4096]{3,2,1,0:T(2,128)}), f32[4,32,2,4096]{3,2,1,0:T(2,128)}, u32[]{:S(2)}, u32[]{:S(2)}) %all-to-all-start.7) | async-done | bytes 4194336 | tf_op jit(solution)/shard_map/all_to_all | solution.py:20
  299.3 7.0 %multiply_reduce_fusion.1 = (f32[32,4,2]{0,2,1:T(2,128)S(1)}, bf16[4,32,2,4096]{3,1,2,0:T(8,128)(2,1)S(1)}) fusion(f32[4,32,2,4096]{3,2,1,0:T(2,128)} %all-to-all-done.7, bf16[4,32,2,4096]{3,2,1,0:T(2,128)(2,1)S(1)} %all-to-all-done.1), kind=kLoop, calls=%fused_computation.23 | loop fusion | flops 6291200 | bytes 8389632 | tf_op jit(solution)/shard_map/reduce_sum | solution.py:123
  334.8 22.8 %all_to_all.91 = bf16[4,32,2,4096]{3,2,1,0:T(2,128)(2,1)S(1)} all-to-all(bf16[4,32,2,4096]{3,2,1,0:T(2,128)(2,1)S(1)} %bitcast.406), channel_id=1, replica_groups=mesh['member'=2,'tp_0'=4,'tp_1'=8,'tp_2'=4] {'tp_2'}, dimensions={0} | all-to-all | bytes 4194304 | tf_op jit(solution)/shard_map/all_to_all | solution.py:68
  360.8 20.0 %all_to_all.92 = bf16[32,2,4096]{2,1,0:T(2,128)(2,1)S(1)} all-to-all(bf16[32,2,4096]{2,1,0:T(2,128)(2,1)S(1)} %reduce_sum.119), channel_id=1, replica_groups=mesh['member'=2,'tp_0'=4,'tp_1'=8,'tp_2'=4] {'tp_0','tp_1'}, dimensions={0} | all-to-all | bytes 1048576 | tf_op jit(solution)/shard_map/all_to_all | solution.py:76
  381.7 18.2 %all_to_all.93 = bf16[32,2,4096]{2,1,0:T(2,128)(2,1)S(1)} all-to-all(bf16[32,2,4096]{2,1,0:T(2,128)(2,1)S(1)} %broadcast_in_dim.61), channel_id=1, replica_groups=mesh['member'=2,'tp_0'=4,'tp_1'=8,'tp_2'=4] {'tp_0','tp_1'}, dimensions={0} | all-to-all | bytes 1048576 | tf_op jit(solution)/shard_map/all_to_all | solution.py:20
  408.3 5.2 %copy.126 = f32[32,4,2,4096]{3,2,1,0:T(2,128)} copy(f32[32,4,2,4096]{3,0,2,1:T(8,128)S(1)} %convert_bitcast_fusion.2) | data formatting | bytes 8388608 | tf_op jit(solution)/shard_map/convert_element_type | solution.py:252
  413.5 6.2 %reshape.1077 = f32[2,128,4096]{2,1,0:T(8,128)} reshape(f32[32,4,2,4096]{3,2,1,0:T(2,128)} %copy.126) | data formatting | bytes 8388608 | tf_op jit(solution)/shard_map/convert_element_type | solution.py:252
  419.8 6.0 %all-to-all-done.11 = bf16[4,32,2,4096]{3,2,1,0:T(2,128)(2,1)} async-done(((bf16[4,32,2,4096]{3,2,1,0:T(2,128)(2,1)}), bf16[4,32,2,4096]{3,2,1,0:T(2,128)(2,1)}, u32[]{:S(2)}, u32[]{:S(2)}) %all-to-all-start.11) | async-done | bytes 2097184 | tf_op jit(solution)/shard_map/all_to_all | solution.py:20
  433.8 5.2 %copy.136 = f32[32,4,2,4096]{3,2,1,0:T(2,128)} copy(f32[32,4,2,4096]{3,0,2,1:T(8,128)S(1)} %convert_bitcast_fusion.1) | data formatting | bytes 8388608 | tf_op jit(solution)/shard_map/convert_element_type | solution.py:86
  439.0 6.0 %reshape.1078 = f32[2,128,4096]{2,1,0:T(8,128)} reshape(f32[32,4,2,4096]{3,2,1,0:T(2,128)} %copy.136) | data formatting | bytes 8388608 | tf_op jit(solution)/shard_map/convert_element_type | solution.py:86
  445.0 6.0 %fusion.15 = bf16[128,512]{1,0:T(8,128)(2,1)S(1)} fusion(bf16[4096,512]{1,0:T(8,128)(2,1)} %param.22, f32[2,128,4096]{2,1,0:T(8,128)} %reshape.1077, f32[2,128,4096]{2,1,0:T(8,128)} %reshape.1078, f32[4096]{0:T(1024)S(1)} %bitcast.414, f32[2,128]{1,0:T(2,128)S(1)} %rsqrt.35, f32[2,4096]{1,0:T(2,128)S(1)} %copy-done.5), kind=kOutput, calls=%fused_computation.32 | convolution fusion | flops 1081147392 | bytes 12764160 | tf_op jit(solution)/shard_map/dot_general | solution.py:257
  455.9 10.4 %all-gather.3 = f32[4,3,128]{2,1,0:T(4,128)S(1)} all-gather(f32[1,3,128]{2,1,0:T(4,128)S(1)} %maximum_bitcast_fusion.1), channel_id=2, replica_groups=mesh['member'=2,'tp_0'=4,'tp_1'=8,'tp_2'=4] {'tp_0'}, dimensions={0}, use_global_device_ids=true | all-gather | bytes 7680 | tf_op jit(solution)/shard_map/all_gather | solution.py:102
  466.4 21.0 %all-gather.4 = f32[8,3,128]{2,1,0:T(4,128)S(1)} all-gather(f32[1,3,128]{2,1,0:T(4,128)S(1)} %maximum_bitcast_fusion.2), channel_id=3, replica_groups=mesh['member'=2,'tp_0'=4,'tp_1'=8,'tp_2'=4] {'tp_1'}, dimensions={0}, use_global_device_ids=true | all-gather | bytes 13824 | tf_op jit(solution)/shard_map/all_gather | solution.py:102
  487.5 10.4 %all-gather.5 = f32[4,3,128]{2,1,0:T(4,128)S(1)} all-gather(f32[1,3,128]{2,1,0:T(4,128)S(1)} %maximum_bitcast_fusion.3), channel_id=4, replica_groups=mesh['member'=2,'tp_0'=4,'tp_1'=8,'tp_2'=4] {'tp_2'}, dimensions={0}, use_global_device_ids=true | all-gather | bytes 7680 | tf_op jit(solution)/shard_map/all_gather | solution.py:102
  (109 shorter events, 111.9 us)
Async XLA Ops:
  0.6 327.2 %copy-start = (bf16[112,4096]{1,0:T(8,128)(2,1)S(1)}, bf16[112,4096]{1,0:T(8,128)(2,1)}, u32[]{:S(2)}) copy-start(bf16[112,4096]{1,0:T(8,128)(2,1)} %param.21) | copy-start | bytes 2752516
  2.7 28.8 %all-to-all-start = ((bf16[32,2,4096]{2,1,0:T(2,128)(2,1)}), bf16[32,2,4096]{2,1,0:T(2,128)(2,1)S(1)}, u32[]{:S(2)}, u32[]{:S(2)}) async-start(bf16[32,2,4096]{2,1,0:T(2,128)(2,1)} %broadcast_in_dim.29), calls=%async_computation | async-start | bytes 1048576 | tf_op jit(solution)/shard_map/all_to_all | solution.py:20
  35.0 28.6 %all-to-all-start.1 = ((bf16[4,32,2,4096]{3,2,1,0:T(2,128)(2,1)}), bf16[4,32,2,4096]{3,2,1,0:T(2,128)(2,1)S(1)}, u32[]{:S(2)}, u32[]{:S(2)}) async-start(bf16[4,32,2,4096]{3,2,1,0:T(2,128)(2,1)} %broadcast_in_dim.30), calls=%async_computation.1 | async-start | bytes 4194304 | tf_op jit(solution)/shard_map/all_to_all | solution.py:20
  39.6 4.7 copy-start.8
  70.5 8.6 %copy-start.4 = (bf16[4096,48]{0,1:T(8,128)(2,1)S(1)}, bf16[4096,48]{0,1:T(8,128)(2,1)}, u32[]{:S(2)}) copy-start(bf16[4096,48]{0,1:T(8,128)(2,1)} %param.18) | copy-start | bytes 1179652
  82.8 19.5 %all-to-all-start.2 = ((bf16[128,2,48]{2,1,0:T(2,128)(2,1)}), bf16[128,2,48]{2,1,0:T(2,128)(2,1)S(1)}, u32[]{:S(2)}, u32[]{:S(2)}) async-start(bf16[128,2,48]{2,1,0:T(2,128)(2,1)} %bitcast.3), calls=%async_computation.2 | async-start | bytes 131072 | tf_op jit(solution)/shard_map/all_to_all | solution.py:217
  95.2 34.3 %copy-start.6 = (bf16[32,4096]{1,0:T(8,128)(2,1)S(1)}, bf16[32,4096]{1,0:T(8,128)(2,1)}, u32[]{:S(2)}) copy-start(bf16[32,4096]{1,0:T(8,128)(2,1)} %param.19) | copy-start | bytes 786436
  250.1 5.5 %copy-start.9 = (f32[2,3,112]{2,0,1:T(2,128)S(1)}, f32[2,3,112]{2,0,1:T(2,128)}, u32[]{:S(2)}) copy-start(f32[2,3,112]{2,0,1:T(2,128)} %param.24) | copy-start | bytes 8068
  250.1 5.5 %copy-start.7 = (f32[2,2,4096]{2,1,0:T(2,128)S(1)}, f32[2,2,4096]{2,1,0:T(2,128)}, u32[]{:S(2)}) copy-start(f32[2,2,4096]{2,1,0:T(2,128)} %param.23) | copy-start | bytes 196612
  250.1 49.1 %all-to-all-start.7 = ((f32[4,32,2,4096]{3,2,1,0:T(2,128)}), f32[4,32,2,4096]{3,2,1,0:T(2,128)}, u32[]{:S(2)}, u32[]{:S(2)}) async-start(f32[4,32,2,4096]{3,2,1,0:T(2,128)} %broadcast_in_dim.60), calls=%async_computation.7 | async-start | bytes 8388608 | tf_op jit(solution)/shard_map/all_to_all | solution.py:20
  306.3 1.4 copy-start.1
  318.8 4.4 copy-start.3
  381.2 26.6 %copy-start.2 = (bf16[4,32,2,4096]{3,1,2,0:T(8,128)(2,1)S(1)}, bf16[4,32,2,4096]{3,1,2,0:T(8,128)(2,1)}, u32[]{:S(2)}) copy-start(bf16[4,32,2,4096]{3,1,2,0:T(8,128)(2,1)} %copy-done.1) | copy-start | bytes 6291460
  403.3 22.5 %all-to-all-start.11 = ((bf16[4,32,2,4096]{3,2,1,0:T(2,128)(2,1)}), bf16[4,32,2,4096]{3,2,1,0:T(2,128)(2,1)}, u32[]{:S(2)}, u32[]{:S(2)}) async-start(bf16[4,32,2,4096]{3,2,1,0:T(2,128)(2,1)} %broadcast_in_dim.62), calls=%async_computation.11 | async-start | bytes 4194304 | tf_op jit(solution)/shard_map/all_to_all | solution.py:20
  413.5 12.3 %copy-start.5 = (f32[2,4096]{1,0:T(2,128)S(1)}, f32[2,4096]{1,0:T(2,128)}, u32[]{:S(2)}) copy-start(f32[2,4096]{1,0:T(2,128)} %param.25) | copy-start | bytes 98308
  445.0 10.1 %copy-start.10 = (s32[128]{0:T(128)S(1)}, s32[128]{0:T(128)}, u32[]{:S(2)}) copy-start(s32[128]{0:T(128)} %param.16) | copy-start | bytes 1540
where the time goes:
time: 509 us; the launch traced here: 499 us
  blocking collectives  237 us (47%)
  waiting for transfers between devices  88.8 us (17%)
  local copies, waits for them, and re-layouts  86.5 us (17%)
  starting transfers between devices  33.9 us (7%)
  other arithmetic  31.6 us (6%)
  matrix products  19.6 us (4%)
    all_to_all x4, waiting for transfers between devices, from_everyone(): return lax.all_to_all(copies, axis, split_axis=0, concat_axis=0, tiled=True)  85.7 us
    all_to_all x3, blocking collectives, from_everyone(): return lax.all_to_all(copies, axis, split_axis=0, concat_axis=0, tiled=True)  51.4 us
    all_to_all x1, blocking collectives, summed_on_arrival(): lax.all_to_all(cut_along(array, dim, length), axis, 0, 0, tiled=True)  49.4 us
    all_gather x3, blocking collectives, collected_together(): both, at, found = (lax.all_gather(jnp.concatenate(lines), axis), 0, {})  41.9 us
    all_to_all x1, blocking collectives, sum_by_axis(): return jnp.sum(lax.all_to_all(own, far, 0, 0, tiled=True), axis=0)  29.7 us
    all_to_all x4, starting transfers between devices, from_everyone(): return lax.all_to_all(copies, axis, split_axis=0, concat_axis=0, tiled=True)  25.6 us
    all_to_all x1, blocking collectives, sent_and_summed(): lax.all_to_all(cut_along(array, dim, length), axis, 0, 0, tiled=True)  22.8 us
    all_to_all x1, blocking collectives, body(): lax.all_to_all(attended, TP, split_axis=1, concat_axis=0, tiled=True)  21.7 us
  transfers between devices with their start and end apart: 5, of which 5 were waited for; matrix products, arithmetic and copies ran while one was open for 5% of the time, Pallas kernels for 0%

commit v1 on v0

v1 whole, which is shorter than its diff:
```python
import jax
import jax.numpy as jnp
import numpy as np
from jax import lax
from jax.experimental import pallas as pl
from jax.experimental.pallas import tpu as pltpu
from jax.sharding import Mesh
from jax.sharding import PartitionSpec as P

MESH = pl.DeviceIdType.MESH
F32 = jnp.float32
BF = jnp.bfloat16
NX, NZ, NY = 4, 8, 4
NP = NX * NY
D, HEADS, KV, HD, CACHE, FFD, VD = 4096, 32, 8, 128, 512, 112, 512
B = 128
QN = 384
ZORDER = (4, 3, 5, 2, 6, 1, 7)
NCH, CW = 4, 512
HALF = D // 2

VM = pltpu.VMEM
DMA = pltpu.SemaphoreType.DMA

SCRATCH = dict(
    st=VM((2, D), BF),
    kvv=VM((2, CACHE, 2 * KV * HD), BF),
    tg=VM((1, B), jnp.int32),
    gn=VM((3, D), F32),
    fi=VM((2, 2, D), F32),
    fh=VM((2, 3, FFD), F32),
    fo=VM((2, D), F32),
    fq=VM((1, 128), F32),
    wq=VM((NZ, 4, 128, 48), BF),
    wo=VM((NP, 32, 256), BF),
    wg=VM((2, NP, 256, FFD), BF),
    wd=VM((FFD, D), BF),
    lm=VM((HALF, VD), BF),
    sc=VM((64, 128), F32),
    s1s=VM((64, 128), F32),
    s1r=VM((64, 128), F32),
    raw=VM((NP, 16, 512), BF),
    p1=VM((3, 256, 128), F32),
    s3s=VM((NZ, 32, QN), BF),
    s3r=VM((NZ, 32, QN), BF),
    q1=VM((3, 32, 128), F32),
    s4s=VM((128, 128), F32),
    s4r=VM((128, 128), F32),
    hs=VM((96, 128), F32),
    osc=VM((64, 128), F32),
    s5s=VM((64, 128), F32),
    s5r=VM((64, 128), F32),
    att=VM((NP, 16, 512), BF),
    s7s=VM((NZ, 32, 256), BF),
    s7r=VM((NZ, 32, 256), BF),
    mid=VM((NP, 256, 256), BF),
    accg=VM((256, FFD), F32),
    accu=VM((256, FFD), F32),
    ssq=VM((256, 128), F32),
    hid=VM((256, FFD), BF),
    p3=VM((NX, NY, 16, D), BF),
    r1a=VM((NX, NY, 16, HALF), BF),
    r1b=VM((NY, NX, 16, HALF), BF),
    s2a=VM((NY, 16, HALF), BF),
    s2b=VM((NX, 16, HALF), BF),
    r2a=VM((NY, 16, HALF), BF),
    r2b=VM((NX, 16, HALF), BF),
    f3=VM((512, 128), F32),
    g3=VM((32, 128), F32),
    s13s=VM((NZ, 64, 128), BF),
    s13r=VM((NZ, 64, 128), BF),
    fs=VM((32, 128), F32),
    fr=VM((16, 128), F32),
    fb=VM((NP, NZ, 16, 128), BF),
    ff=VM((2048, 128), F32),
    lh=VM((B, HALF), BF),
    lp=VM((B, VD), F32),
    lr=VM((B, VD), F32),
    sz=VM((NZ, 8, 128), F32),
    sx=VM((NP, 8, 128), F32),
)
PHASES = dict(
    wq=NZ, wo=NP, s1=NZ, s2=NP, s3=NZ, s4=NP, s5=NZ, s6=NP, s7=NZ, s8=NZ,
    da=NP, fa=NP * 4, fb_=NP * 4, a1=NCH * 4, b1=NCH * 4, a2=NCH * 4, b2=NCH * 4,
    s13=NZ, fx=1, s14=NZ, s15=NP, lx=1, s16=NZ, s17=NP,
)
LOCAL = ("st", "kvv", "tg", "gn", "fi", "fh", "fo", "fq", "wq", "wo", "wg", "wd", "lm")
INPUTS = (
    "stream", "kv", "lengths", "targets", "gains", "wqkv", "wout", "wgu", "wdown", "lmh",
    "fin", "fhid", "fout", "freq",
)


def kernel(names, debug, *refs):
    r = dict(zip(names, refs))
    c, x, z, y = (lax.axis_index(a) for a in ("member", "tp_0", "tp_1", "tp_2"))
    t = x * 32 + z * 4 + y
    n = x * 4 + y
    sends = []

    def rem(v, k):
        return lax.rem(v, k)

    def at_z(zz):
        return (c, x, zz, y)

    def at_xy(xx, yy):
        return (c, xx, z, yy)

    partner = (1 - c, x, z, y)

    def copy(phase, src, dst, slot, dev, sslot=None):
        sslot = slot if sslot is None else sslot
        return pltpu.make_async_remote_copy(
            src_ref=src,
            dst_ref=dst,
            send_sem=r["ss_" + phase].at[sslot],
            recv_sem=r["rs_" + phase].at[slot],
            device_id=dev,
            device_id_type=MESH,
        )

    def send(phase, src, dst, slot, dev, sslot=None):
        k = copy(phase, src, dst, slot, dev, sslot)
        k.start()
        sends.append(k)

    def recv(phase, dst, slot, sslot=None):
        copy(phase, dst, dst, slot, partner, sslot).wait_recv()

    zpeers = [rem(z + d, NZ) for d in ZORDER]
    plane = [
        (rem(x + dx, NX), rem(y + dy, NY))
        for dx, dy in sorted(
            ((a, b) for a in range(NX) for b in range(NY) if a or b),
            key=lambda p: -(min(p[0], 4 - p[0]) + min(p[1], 4 - p[1])),
        )
    ]

    def z_send(phase, src_at, dst):
        for zz in zpeers:
            send(phase, src_at(zz), dst, z, at_z(zz), zz)

    def z_recv(phase, dst_at):
        for zz in zpeers:
            recv(phase, dst_at(zz), zz)

    def xy_send(phase, src_at, dst):
        for xx, yy in plane:
            send(phase, src_at(xx * 4 + yy), dst, n, at_xy(xx, yy), xx * 4 + yy)

    def xy_recv(phase, dst_at):
        for xx, yy in plane:
            recv(phase, dst_at(xx * 4 + yy), xx * 4 + yy)

    bar = pltpu.get_barrier_semaphore()
    peers = [at_z(zz) for zz in zpeers] + [at_xy(*p) for p in plane] + [partner]
    for dev in peers:
        pl.semaphore_signal(bar, inc=1, device_id=dev, device_id_type=MESH)

    local = {}

    def fetch(name, src, dst):
        k = pltpu.make_async_copy(src, dst, r["ls"].at[LOCAL.index(name)])
        k.start()
        local[name] = k

    fetch("st", r["stream"], r["st"])
    fetch("gn", r["gains"], r["gn"])
    fetch("fq", r["freq"], r["fq"])
    fetch("wq", r["wqkv"].at[:, z], r["wq"].at[z])
    fetch("wo", r["wout"].at[:, pl.ds(pl.multiple_of(n * 256, 256), 256)], r["wo"].at[n])
    fetch("kvv", r["kv"], r["kvv"])
    fetch("fi", r["fin"], r["fi"])
    fetch("fh", r["fhid"], r["fh"])
    fetch("fo", r["fout"], r["fo"])
    fetch("tg", r["targets"], r["tg"])
    fetch("wg", r["wgu"], r["wg"])
    fetch("wd", r["wdown"], r["wd"])
    fetch("lm", r["lmh"].at[pl.ds(pl.multiple_of(c * HALF, HALF), HALF)], r["lm"])

    def spread(scratch, dst):
        for zz in range(NZ):
            r[dst][zz * 8 : zz * 8 + 8] = r[scratch][pl.ds(zz, 8, stride=8), :]

    z8 = pl.ds(pl.multiple_of(z * 8, 8), 8)

    def z_then_plane(zphase, pphase, s, rr, buf):
        def piece(zz):
            return pl.ds(pl.multiple_of(zz * 8, 8), 8)

        z_send(zphase, lambda zz: r[s].at[piece(zz)], r[rr].at[z8])
        r[rr][z8, :] = r[s][z8, :]
        z_recv(zphase, lambda zz: r[rr].at[piece(zz)])
        for k in range(4):
            rows = [r[rr][pl.ds(j * 4 + k, 8, stride=8), :] for j in range(2)]
            r[buf][n, :, k * 128 : (k + 1) * 128] = jnp.concatenate(rows, axis=0).astype(BF)
        xy_send(pphase, lambda m: r[buf].at[n], r[buf].at[n])
        return lambda: xy_recv(pphase, lambda m: r[buf].at[m])

    local["st"].wait()
    x32 = r["st"][...].astype(F32)
    rs = lax.rsqrt(jnp.mean(x32 * x32, axis=-1, keepdims=True) + 1e-5)
    for b in range(32):
        for j in range(2):
            r["sc"][j * 32 + b : j * 32 + b + 1, :] = x32[j : j + 1, b * 128 : (b + 1) * 128]
    spread("sc", "s1s")
    r["s4s"][...] = jnp.zeros((128, 128), F32)
    row8 = lax.broadcasted_iota(jnp.int32, (8, 128), 0)
    lane8 = lax.broadcasted_iota(jnp.int32, (8, 128), 1)
    rs8 = jnp.where(row8 < 4, rs[0:1, 0:1], rs[1:2, 0:1])

    pl.semaphore_wait(bar, len(peers))

    finish = z_then_plane("s1", "s2", "s1s", "s1r", "raw")
    z_send("wq", lambda zz: r["wqkv"].at[:, zz], r["wq"].at[z])
    xy_send(
        "wo",
        lambda m: r["wout"].at[:, pl.ds(pl.multiple_of(m * 256, 256), 256)],
        r["wo"].at[n],
    )
    local["fq"].wait()
    local["gn"].wait()
    pos = [r["lengths"][rem(2 * t + j, B)] for j in range(2)]
    ang = jnp.where(row8 < 4, pos[0], pos[1]).astype(F32) * r["fq"][0:1, :]
    cos8 = jnp.cos(ang)
    sin8 = jnp.where(lane8 < 64, -jnp.sin(ang), jnp.sin(ang))
    for b in range(32):
        r["g3"][b : b + 1, :] = r["gn"][2:3, b * 128 : (b + 1) * 128]

    local["wq"].wait()
    z_recv("wq", lambda zz: r["wq"].at[zz])
    wcat = jnp.concatenate([r["wq"][s].reshape(512, 48) for s in range(NZ)], axis=1)
    gq = jnp.concatenate(
        [r["gn"][0:1, pl.ds(pl.multiple_of(k * 1024 + z * 128, 128), 128)] for k in range(4)], axis=1
    )
    finish()
    lhs = (r["raw"][...].reshape(256, 512).astype(F32) * gq).astype(BF)
    prod = jnp.dot(lhs, wcat, preferred_element_type=F32)
    for l in range(3):
        r["p1"][l] = prod[:, l * 128 : (l + 1) * 128]
    for zz in range(NZ):
        for l in range(3):
            r["s3s"][zz, :, l * 128 : (l + 1) * 128] = r["p1"].at[l][
                pl.ds(zz, 32, stride=8), :
            ].astype(BF)
    z_send("s3", lambda zz: r["s3s"].at[zz], r["s3r"].at[z])
    r["s3r"][z] = r["s3s"][z]
    z_recv("s3", lambda zz: r["s3r"].at[zz])
    acc = r["s3r"][0].astype(F32)
    for s in range(1, NZ):
        acc = acc + r["s3r"][s].astype(F32)
    for l in range(3):
        r["q1"][l] = acc[:, l * 128 : (l + 1) * 128]
    for l in range(3):
        for j in range(2):
            r["s4s"][pl.ds(l * 2 + j, 16, stride=8), :] = r["q1"].at[l][pl.ds(j, 16, stride=2), :]

    def tile(m):
        return pl.ds(pl.multiple_of(m * 8, 8), 8)

    xy_send("s4", lambda m: r["s4s"].at[tile(m)], r["s4r"].at[tile(n)])
    r["s4r"][tile(n), :] = r["s4s"][tile(n), :]
    xy_recv("s4", lambda m: r["s4r"].at[tile(m)])

    blocks = {
        (yy, l): jnp.concatenate(
            [r["s4r"][pl.ds(yy * 8 + l * 2 + j, 4, stride=32), :] for j in range(2)], axis=0
        )
        for yy in range(NY)
        for l in range(3)
    }
    for hh in range(12):
        val = jnp.zeros((8, 128), F32)
        lane = 0
        while lane < 128:
            col = hh * 128 + lane
            tt, i = divmod(col, 48)
            at = (tt // 4) * 48 + i
            l, src = divmod(at, 128)
            width = min(48 - i, 128 - src, 128 - lane)
            piece = blocks[(tt % 4, l)]
            shift = (lane - src) % 128
            if shift:
                piece = pltpu.roll(piece, shift, 1)
            val = jnp.where((lane8 >= lane) & (lane8 < lane + width), piece, val)
            lane += width
        val = (val * rs8).astype(BF).astype(F32)
        turned = (val * cos8 + pltpu.roll(val, 64, 1) * sin8).astype(BF).astype(F32)
        if hh >= 4:
            turned = jnp.where(row8 % 4 == 3, val, turned)
        r["hs"][pl.ds(hh, 8, stride=12), :] = turned

    local["kvv"].wait()
    inv_root = HD**-0.5
    group = lax.broadcasted_iota(jnp.int32, (32, 128), 0) // 4
    group8 = (
        lax.broadcasted_iota(jnp.int32, (32, 8), 0) // 4
        == lax.broadcasted_iota(jnp.int32, (32, 8), 1)
    )
    place = lax.broadcasted_iota(jnp.int32, (32, CACHE), 1)
    nt = (((1,), (1,)), ((), ()))
    for j in range(2):
        q = r["hs"][j * 48 : j * 48 + 32, :]
        kn = r["hs"][j * 48 + 32 : j * 48 + 40, :].astype(BF)
        vn = r["hs"][j * 48 + 40 : j * 48 + 48, :].astype(BF)
        qd = jnp.concatenate([jnp.where(group == k, q, 0.0) for k in range(KV)], axis=1).astype(BF)
        scores = (
            lax.dot_general(qd, r["kvv"][j, :, : KV * HD], nt, preferred_element_type=F32) * inv_root
        )
        fresh = lax.dot_general(q.astype(BF), kn, nt, preferred_element_type=F32)
        fresh = jnp.sum(jnp.where(group8, fresh, 0.0), axis=1, keepdims=True) * inv_root
        scores = jnp.where(place < pos[j], scores, -1e30)
        peak = jnp.maximum(jnp.max(scores, axis=1, keepdims=True), fresh)
        weights = jnp.exp(scores - peak)
        fresh_w = jnp.exp(fresh - peak)
        total = jnp.sum(weights, axis=1, keepdims=True) + fresh_w
        probs = (weights / total).astype(BF)
        fresh_p = jnp.where(group8, fresh_w / total, 0.0).astype(BF)
        wide = jnp.dot(probs, r["kvv"][j, :, KV * HD :], preferred_element_type=F32)
        out = jnp.dot(fresh_p, vn, preferred_element_type=F32)
        for k in range(KV):
            out = out + jnp.where(group == k, wide[:, k * 128 : (k + 1) * 128], 0.0)
        r["osc"][j * 32 : j * 32 + 32, :] = out.astype(BF).astype(F32)

    spread("osc", "s5s")
    finish = z_then_plane("s5", "s6", "s5s", "s5r", "att")
    local["wo"].wait()
    xy_recv("wo", lambda m: r["wo"].at[m])
    resid = r["raw"][:, :, pl.ds(pl.multiple_of(x * 128, 128), 128)].reshape(256, 128).astype(F32)
    lo = resid * jnp.where(z == 2 * y, 1.0, 0.0)
    hi = resid * jnp.where(z == 2 * y + 1, 1.0, 0.0)
    finish()
    prod = jnp.dot(
        r["att"][...].reshape(256, 512), r["wo"][...].reshape(512, 256), preferred_element_type=F32
    ) + jnp.concatenate([lo, hi], axis=1)
    for xl in range(2):
        for ys in range(NY):
            for j in range(2):
                at = [((m * 2 + xl) * 4 + ys) * 16 + j * 8 for m in range(2)]
                r["s7s"][xl * 4 + ys, j * 16 : j * 16 + 16, :] = jnp.concatenate(
                    [prod[a : a + 8] for a in at], axis=0
                ).astype(BF)
    z_send("s7", lambda zz: r["s7s"].at[zz], r["s7r"].at[z])
    r["s7r"][z] = r["s7s"][z]
    z_recv("s7", lambda zz: r["s7r"].at[zz])
    acc = r["s7r"][0].astype(F32)
    for s in range(1, NZ):
        acc = acc + r["s7r"][s].astype(F32)

    def z32(zz):
        return pl.ds(pl.multiple_of(zz * 32, 32), 32)

    r["mid"][n, z32(z), :] = acc.astype(BF)
    z_send("s8", lambda zz: r["mid"].at[n, z32(z)], r["mid"].at[n, z32(z)])
    r["accg"][...] = jnp.zeros((256, FFD), F32)
    r["accu"][...] = jnp.zeros((256, FFD), F32)
    r["ssq"][...] = jnp.zeros((256, 128), F32)
    for name in ("fi", "fh", "fo", "wg", "wd"):
        local[name].wait()
    z_recv("s8", lambda zz: r["mid"].at[n, z32(zz)])

    near = (1, 3, 2)
    for d in (2, 1, 3):
        xx, yy = rem(x + d, NX), rem(y + d, NY)
        send("da", r["mid"].at[n], r["mid"].at[n], n, at_xy(xx, y), xx * 4 + y)
        send("da", r["mid"].at[n], r["mid"].at[n], n, at_xy(x, yy), x * 4 + yy)

    def ffn_chunk(m):
        v = r["mid"][m].astype(F32)
        r["ssq"][...] += v[:, :128] * v[:, :128] + v[:, 128:] * v[:, 128:]
        cols = pl.ds(pl.multiple_of(m * 256, 256), 256)
        g = r["gn"][1:2, cols]
        v4 = v.reshape(16, 2, 8, 256)
        for k, name in enumerate(("accg", "accu")):
            f = jnp.concatenate(
                [
                    (r["fi"][i, k : k + 1, cols] * g).reshape(1, 1, 1, 256)
                    for i in range(2)
                ],
                axis=1,
            )
            act = (v4 * f).reshape(256, 256).astype(BF)
            r[name][...] += jnp.dot(act, r["wg"][k, m], preferred_element_type=F32)

    ffn_chunk(n)
    top, low = pl.ds(0, 128), pl.ds(128, 128)
    for d in near:
        xx = rem(x + d, NX)
        m = xx * 4 + y
        recv("da", r["mid"].at[m], m)
        for e in (2, 1, 3):
            yy = rem(y + e, NY)
            send("fa", r["mid"].at[m, top], r["mid"].at[m, top], m, at_xy(x, yy), m * 4 + e)
        yy = rem(y + d, NY)
        m = x * 4 + yy
        recv("da", r["mid"].at[m], m)
        for e in (2, 1, 3):
            xx = rem(x + e, NX)
            send("fb_", r["mid"].at[m, low], r["mid"].at[m, low], m, at_xy(xx, y), m * 4 + e)

    def line_step(i, carry):
        ffn_chunk(rem(x + 1 + i, NX) * 4 + y)
        ffn_chunk(x * 4 + rem(y + 1 + i, NY))
        return carry

    lax.fori_loop(0, 3, line_step, 0)

    def diag_step(i, carry):
        m = rem(x + 1 + i // 3, NX) * 4 + rem(y + 1 + i % 3, NY)
        recv("fa", r["mid"].at[m, top], m)
        recv("fb_", r["mid"].at[m, low], m)
        ffn_chunk(m)
        return carry

    lax.fori_loop(0, 9, diag_step, 0)
    scale = lax.rsqrt(jnp.sum(r["ssq"][...], axis=1, keepdims=True) * (1.0 / D) + 1e-5)

    def by_member(k):
        return jnp.concatenate(
            [r["fh"][i, k : k + 1, :].reshape(1, 1, 1, FFD) for i in range(2)], axis=1
        )

    gate = (r["accg"][...] * scale).reshape(16, 2, 8, FFD) * by_member(0)
    up = (r["accu"][...] * scale).reshape(16, 2, 8, FFD) * by_member(1)
    hidden = gate / (1.0 + jnp.exp(-gate)) * up * by_member(2)
    r["hid"][...] = hidden.reshape(256, FFD).astype(BF)

    def chunk(ch):
        return pl.ds(pl.multiple_of(ch * CW, CW), CW)

    def high(ch):
        return pl.ds(pl.multiple_of(HALF + ch * CW, CW), CW)

    def a1(ch, xx):
        return copy(
            "a1", r["p3"].at[xx, :, :, chunk(ch)], r["r1a"].at[x, :, :, chunk(ch)],
            ch * 4 + x, at_xy(xx, y), ch * 4 + xx,
        )

    def b1(ch, yy):
        return copy(
            "b1", r["p3"].at[:, yy, :, high(ch)], r["r1b"].at[y, :, :, chunk(ch)],
            ch * 4 + y, at_xy(x, yy), ch * 4 + yy,
        )

    def down_step(ch, carry):
        for cols in (chunk(ch), high(ch)):
            v = jnp.dot(r["hid"][...], r["wd"][:, cols], preferred_element_type=F32)
            r["p3"][:, :, :, cols] = v.astype(BF).reshape(NX, NY, 16, CW)
        for d in (2, 1, 3):
            a1(ch, rem(x + d, NX)).start()
            b1(ch, rem(y + d, NY)).start()
        return carry

    lax.fori_loop(0, NCH, down_step, 0)

    def a2(ch, yy):
        return copy(
            "a2", r["s2a"].at[yy, :, chunk(ch)], r["r2a"].at[y, :, chunk(ch)],
            ch * 4 + y, at_xy(x, yy), ch * 4 + yy,
        )

    def b2(ch, xx):
        return copy(
            "b2", r["s2b"].at[xx, :, chunk(ch)], r["r2b"].at[x, :, chunk(ch)],
            ch * 4 + x, at_xy(xx, y), ch * 4 + xx,
        )

    def second_step(ch, carry):
        for d in near:
            xx = rem(x + d, NX)
            recv("a1", r["r1a"].at[xx, :, :, chunk(ch)], ch * 4 + xx)
        v = r["p3"][x, :, :, chunk(ch)].astype(F32)
        for d in near:
            v = v + r["r1a"][rem(x + d, NX), :, :, chunk(ch)].astype(F32)
        r["s2a"][:, :, chunk(ch)] = v.astype(BF)
        for d in (2, 1, 3):
            a2(ch, rem(y + d, NY)).start()
        for d in near:
            yy = rem(y + d, NY)
            recv("b1", r["r1b"].at[yy, :, :, chunk(ch)], ch * 4 + yy)
        v = r["p3"][:, y, :, high(ch)].astype(F32)
        for d in near:
            v = v + r["r1b"][rem(y + d, NY), :, :, chunk(ch)].astype(F32)
        r["s2b"][:, :, chunk(ch)] = v.astype(BF)
        for d in (2, 1, 3):
            b2(ch, rem(x + d, NX)).start()
        return carry

    lax.fori_loop(0, NCH, second_step, 0)
    for ch in range(NCH):
        for d in near:
            yy = rem(y + d, NY)
            recv("a2", r["r2a"].at[yy, :, chunk(ch)], ch * 4 + yy)
            xx = rem(x + d, NX)
            recv("b2", r["r2b"].at[xx, :, chunk(ch)], ch * 4 + xx)

    row16 = lax.broadcasted_iota(jnp.int32, (16, 128), 0)
    own_row = rem(row16, 8) == z
    tile16 = pl.ds(pl.multiple_of(n * 16, 16), 16)
    for b in range(32):
        own, got, me, count = (
            ("s2a", "r2a", y, NY) if b < 16 else ("s2b", "r2b", x, NX)
        )
        cols = slice((b % 16) * 128, (b % 16 + 1) * 128)
        v = r[own][me, :, cols].astype(F32)
        for d in near:
            v = v + r[got][rem(me + d, count), :, cols].astype(F32)
        at = slice(b * 128, (b + 1) * 128)
        v = v * jnp.where(row16 < 8, r["fo"][0:1, at], r["fo"][1:2, at])
        m = r["mid"][b // 2, tile16, (b % 2) * 128 : (b % 2 + 1) * 128].astype(F32)
        r["f3"][b * 16 : (b + 1) * 16, :] = v + jnp.where(own_row, m, 0.0)

    for zz in range(NZ):
        for m in range(2):
            r["s13s"][zz, m * 32 : (m + 1) * 32, :] = r["f3"][
                pl.ds(m * 8 + zz, 32, stride=16), :
            ].astype(BF)
    z_send("s13", lambda zz: r["s13s"].at[zz], r["s13r"].at[z])
    owned = [r["f3"][pl.ds(m * 8 + z, 32, stride=16), :] for m in range(2)]
    z_recv("s13", lambda zz: r["s13r"].at[zz])
    both = jnp.zeros((32, 128), F32)
    for m in range(2):
        v = owned[m]
        for zz in zpeers:
            v = v + r["s13r"][zz, m * 32 : (m + 1) * 32, :].astype(F32)
        v = v.astype(BF).astype(F32)
        mean = jnp.sum(jnp.sum(v * v, axis=1, keepdims=True), axis=0, keepdims=True) * (1.0 / D)
        both = both + (v * lax.rsqrt(mean + 1e-5) * r["g3"][...]).astype(BF).astype(F32)
    r["fs"][...] = both

    def half(k):
        return pl.ds(pl.multiple_of(k * 16, 16), 16)

    send("fx", r["fs"].at[half(1 - c)], r["fr"], 0, partner)
    recv("fx", r["fr"], 0)
    r["fb"][n, z] = ((r["fs"][half(c), :] + r["fr"][...]) * 0.25).astype(BF)
    z_send("s14", lambda zz: r["fb"].at[n, z], r["fb"].at[n, z])
    local["lm"].wait()
    local["tg"].wait()
    wanted = jnp.broadcast_to(r["tg"][...].astype(F32), (B, B)).T[:, 0:1]
    z_recv("s14", lambda zz: r["fb"].at[n, zz])
    xy_send("s15", lambda m: r["fb"].at[n], r["fb"].at[n])
    xy_recv("s15", lambda m: r["fb"].at[m])
    r["ff"][...] = r["fb"][...].reshape(2048, 128).astype(F32)
    for b in range(16):
        rows = [
            r["ff"][pl.ds(xl * 1024 + zz * 16 + b, 8, stride=128), :]
            for xl in range(2)
            for zz in range(NZ)
        ]
        r["lh"][:, b * 128 : (b + 1) * 128] = jnp.concatenate(rows, axis=0).astype(BF)
    r["lp"][...] = jnp.dot(r["lh"][...], r["lm"][...], preferred_element_type=F32)
    send("lx", r["lp"], r["lr"], 0, partner)
    recv("lx", r["lr"], 0)
    mean_f = r["lp"][...] + r["lr"][...]
    r["logits_o"][...] = mean_f.astype(BF)

    ids = (lax.broadcasted_iota(jnp.int32, (B, VD), 1) + t * VD).astype(F32)
    found = jnp.sum(jnp.where(ids == wanted, mean_f, 0.0), axis=1, keepdims=True)
    peak = jnp.max(mean_f, axis=1, keepdims=True)
    total = jnp.sum(jnp.exp(mean_f - peak), axis=1, keepdims=True)
    lane = lax.broadcasted_iota(jnp.int32, (B, B), 1)
    stat = jnp.where(lane == 0, peak, jnp.where(lane == 1, total, jnp.where(lane == 2, found, 0.0)))
    r["sz"][z] = stat.T[:8]

    def combine(ref, count):
        peaks = [ref[k, 0:1, :] for k in range(count)]
        top_ = peaks[0]
        for k in range(1, count):
            top_ = jnp.maximum(top_, peaks[k])
        tot = ref[0, 1:2, :] * jnp.exp(peaks[0] - top_)
        hit = ref[0, 2:3, :]
        for k in range(1, count):
            tot = tot + ref[k, 1:2, :] * jnp.exp(peaks[k] - top_)
            hit = hit + ref[k, 2:3, :]
        return top_, tot, hit

    z_send("s16", lambda zz: r["sz"].at[z], r["sz"].at[z])
    z_recv("s16", lambda zz: r["sz"].at[zz])
    a, b_, h = combine(r["sz"], NZ)
    r["sx"][n] = jnp.concatenate([a, b_, h, jnp.zeros((5, 128), F32)], axis=0)
    xy_send("s17", lambda m: r["sx"].at[n], r["sx"].at[n])
    xy_recv("s17", lambda m: r["sx"].at[m])
    a, b_, h = combine(r["sx"], NP)
    r["lp_o"][...] = h - (a + jnp.log(b_))

    for k in sends:
        k.wait_send()

    def drain(ch, carry):
        for d in near:
            a1(ch, rem(x + d, NX)).wait_send()
            b1(ch, rem(y + d, NY)).wait_send()
            a2(ch, rem(y + d, NY)).wait_send()
            b2(ch, rem(x + d, NX)).wait_send()
        return carry

    lax.fori_loop(0, NCH, drain, 0)
    for name in debug:
        r["dbg_" + name][...] = r[name][...]


def body(
    stream_in, kv_cache, lengths, targets, norm_gains, w_qkv, w_out, w_gate_up, w_down, lm_head,
    fast_in, fast_hidden, fast_out, debug=(),
):
    freq = np.float32(500000.0) ** (-np.arange(64, dtype=np.float32) * 2.0 / 128)
    freq = jnp.asarray(np.concatenate([freq, freq])[None, :], F32)
    args = dict(
        stream=stream_in, kv=kv_cache, lengths=lengths, targets=targets.reshape(1, B),
        gains=norm_gains, wqkv=w_qkv.reshape(4, NZ, 128, 48), wout=w_out,
        wgu=w_gate_up.reshape(2, NP, 256, FFD), wdown=w_down, lmh=lm_head,
        fin=fast_in, fhid=fast_hidden, fout=fast_out, freq=freq,
    )
    outs = ["logits_o", "lp_o"] + ["dbg_" + k for k in debug]
    shapes = [jax.ShapeDtypeStruct((B, VD), BF), jax.ShapeDtypeStruct((1, B), F32)] + [
        jax.ShapeDtypeStruct(SCRATCH[k].shape, SCRATCH[k].dtype) for k in debug
    ]
    sems = {}
    for k, count in PHASES.items():
        sems["ss_" + k] = DMA((count,))
        sems["rs_" + k] = DMA((count,))
    sems["ls"] = DMA((len(LOCAL),))
    names = list(INPUTS) + outs + list(SCRATCH) + list(sems)
    import functools

    got = pl.pallas_call(
        functools.partial(kernel, names, debug),
        out_shape=shapes,
        in_specs=[
            pl.BlockSpec(memory_space=pltpu.SMEM if k == "lengths" else pl.ANY) for k in INPUTS
        ],
        out_specs=[pl.BlockSpec(memory_space=VM)] * len(outs),
        scratch_shapes=list(SCRATCH.values()) + list(sems.values()),
        compiler_params=pltpu.CompilerParams(
            collective_id=0, has_side_effects=True, vmem_limit_bytes=60 * 1024 * 1024
        ),
        name="step",
    )(*(args[k] for k in INPUTS))
    return (got[0], got[1].reshape(B), *got[2:])


MEMBER_TP = ("member", "tp_0", "tp_1", "tp_2")
TP = ("tp_0", "tp_1", "tp_2")
IN_SPECS = (
    P(MEMBER_TP, None), P(MEMBER_TP, None, None), P(), P(), P(), P(None, TP), P(TP, None),
    P(None, None, TP), P(TP, None), P(None, TP), P("member", None, None), P("member", None, TP),
    P("member", None),
)


def solution(mesh):
    split = Mesh(
        mesh.devices.reshape(mesh.shape["member"], NX, NZ, NY), ("member", "tp_0", "tp_1", "tp_2")
    )
    return jax.shard_map(
        body, mesh=split, in_specs=IN_SPECS, out_specs=(P(None, TP), P()), check_vma=False
    )
```

time: 509 us -> 155 us (0.30); the launches traced: 499 us -> 153 us
  blocking collectives: 237 us -> 0 us
  Pallas kernels: 0 us -> 142 us
  waiting for transfers between devices: 88.8 us -> 0 us
  local copies, waits for them, and re-layouts: 86.5 us -> 10.3 us
  starting transfers between devices: 33.9 us -> 0 us
  other arithmetic: 31.6 us -> 0 us
  matrix products: 19.6 us -> 0 us
    all_to_all x8 -> x0, blocking collectives: 195 us -> none  [the longest x3 51.4 us: from_everyone(): return lax.all_to_all(copies, axis, split_axis=0, concat_axis=0, tiled=True)]
    pallas_call x0 -> x1, Pallas kernels: none -> 142 us  [body(): pl.pallas_call(functools.partial(kernel, names, debug), out_shape=shapes,...]
    all_to_all x5 -> x0, waiting for transfers between devices: 88.8 us -> none  [the longest x4 85.7 us: from_everyone(): return lax.all_to_all(copies, axis, split_axis=0, concat_axis=0, tiled=True)]
    convert_element_type x14 -> x0, local copies, waits for them, and re-layouts: 50.5 us -> none  [the longest x2 11.5 us: body(): middle.astype(jnp.float32).reshape(mem_dev, batch_rows, width) + scaled]
    all_gather x3 -> x0, blocking collectives: 41.9 us -> none  [collected_together(): both, at, found = (lax.all_gather(jnp.concatenate(lines), axis), 0, {})]
    all_to_all x5 -> x0, starting transfers between devices: 33.9 us -> none  [the longest x4 25.6 us: from_everyone(): return lax.all_to_all(copies, axis, split_axis=0, concat_axis=0, tiled=True)]
    reduce_sum x10 -> x0, other arithmetic: 23.2 us -> none  [the longest x3 13.6 us: rms_norm(): jnp.mean(values_in * values_in, axis=-1, keepdims=True) + 1e-05]
    dot_general x9 -> x0, matrix products: 19.6 us -> none  [the longest x1 5.98 us: body(): logits = jnp.dot(final_in, lm_head, preferred_element_type=jnp.float32)]
  transfers between devices with their start and end apart: 5 -> 0, of which waited for: 5 -> 0; matrix products, arithmetic and copies ran while one was open for 5% -> 0% of each run, Pallas kernels for 0% -> 0%
where the time goes in v1:
time: 155 us; the launch traced here: 153 us
  Pallas kernels  142 us (92%)
  local copies, waits for them, and re-layouts  10.3 us (7%)
    pallas_call x1, Pallas kernels, body(): pl.pallas_call(functools.partial(kernel, names, debug), out_shape=shapes,...  142 us
    unnamed x5, local copies, waits for them, and re-layouts  10.3 us

profile of v1, /device:TPU:32, one launch (start us, length us, event | category | flops | bytes accessed | tf_op | source)
XLA Modules:
  0.0 153.3 jit_solution(11332955249431597777)
XLA Ops:
  0.6 1.3 copy.18.refs_11_
  1.9 2.3 %copy.16 = bf16[4096,48]{1,0:T(8,128)(2,1)} copy(bf16[4096,48]{0,1:T(8,128)(2,1)} %param.19) | data formatting | bytes 786432 | tf_op args[5]
  4.2 4.0 %copy.17 = bf16[2,4096,112]{2,1,0:T(8,128)(2,1)} copy(bf16[2,4096,112]{1,2,0:T(8,128)(2,1)} %param.21) | data formatting | bytes 3670016 | tf_op args[7]
  8.2 142.4 %step.1 = (bf16[128,512]{1,0:T(8,128)(2,1)}, f32[1,128]{1,0:T(1,128)}) custom-call(bf16[2,4096]{1,0:T(2,128)(2,1)} %refs_0_.1, bf16[2,512,2048]{2,1,0:T(8,128)(2,1)} %refs_1_.1, s32[128]{0:T(128)} %refs_2_.1, s32[1,128]{1,0:T(1,128)} %bitcast.6, f32[3,4096]{1,0:T(4,128)} %refs_4_.1, bf16[4,8,128,48]{3,2,1,0:T(8,128)(2,1)} %bitcast.5, ...), custom_call_target="tpu_custom_call" | custom-call | tf_op jit(solution)/shard_map/step/pallas_call | solution.py:629
  150.6 1.6 %copy.21 = bf16[128,512]{1,0:T(8,128)(2,1)} copy(bf16[128,512]{1,0:T(8,128)(2,1)} %get-tuple-element.8) | data formatting | bytes 262144
  152.2 1.1 copy.22

commit v2 on v1

--- a/solution.py
+++ b/solution.py
@@ -18,6 +18,7 @@
 ZORDER = (4, 3, 5, 2, 6, 1, 7)
 NCH, CW = 4, 512
 HALF = D // 2
+NT = (((1,), (1,)), ((), ()))
 
 VM = pltpu.VMEM
 DMA = pltpu.SemaphoreType.DMA
@@ -28,12 +29,12 @@
     tg=VM((1, B), jnp.int32),
     gn=VM((3, D), F32),
     fi=VM((2, 2, D), F32),
-    fh=VM((2, 3, FFD), F32),
+    fh=VM((3, 2, FFD), F32),
     fo=VM((2, D), F32),
     fq=VM((1, 128), F32),
-    wq=VM((NZ, 4, 128, 48), BF),
+    wq=VM((NZ, 48, 512), BF),
     wo=VM((NP, 32, 256), BF),
-    wg=VM((2, NP, 256, FFD), BF),
+    wg=VM((2, FFD, D), BF),
     wd=VM((FFD, D), BF),
     lm=VM((HALF, VD), BF),
     sc=VM((64, 128), F32),
@@ -80,11 +81,13 @@
     sx=VM((NP, 8, 128), F32),
 )
 PHASES = dict(
-    wq=NZ, wo=NP, s1=NZ, s2=NP, s3=NZ, s4=NP, s5=NZ, s6=NP, s7=NZ, s8=NZ,
+    wq=NZ * 4, wo=NP, s1=NZ, s2=NP, s3=NZ, s4=NP, s5=NZ, s6=NP, s7=NZ, s8=NZ,
     da=NP, fa=NP * 4, fb_=NP * 4, a1=NCH * 4, b1=NCH * 4, a2=NCH * 4, b2=NCH * 4,
     s13=NZ, fx=1, s14=NZ, s15=NP, lx=1, s16=NZ, s17=NP,
 )
-LOCAL = ("st", "kvv", "tg", "gn", "fi", "fh", "fo", "fq", "wq", "wo", "wg", "wd", "lm")
+LOCAL = (
+    "st", "kvv", "tg", "gn", "fi", "fh", "fo", "fq", "wq0", "wq1", "wq2", "wq3", "wo", "wg", "wd", "lm",
+)
 INPUTS = (
     "stream", "kv", "lengths", "targets", "gains", "wqkv", "wout", "wgu", "wdown", "lmh",
     "fin", "fhid", "fout", "freq",
@@ -97,7 +100,16 @@
     t = x * 32 + z * 4 + y
     n = x * 4 + y
     sends = []
-
+    scope = []
+
+    def mark(name):
+        while scope:
+            scope.pop().__exit__(None, None, None)
+        if name:
+            scope.append(jax.named_scope(name))
+            scope[-1].__enter__()
+
+    mark("start")
     def rem(v, k):
         return lax.rem(v, k)
 
@@ -158,6 +170,9 @@
     for dev in peers:
         pl.semaphore_signal(bar, inc=1, device_id=dev, device_id_type=MESH)
 
+    def qcols(zz, k):
+        return r["wqkv"].at[:, pl.ds(pl.multiple_of(k * 1024 + zz * 128, 128), 128)]
+
     local = {}
 
     def fetch(name, src, dst):
@@ -168,7 +183,8 @@
     fetch("st", r["stream"], r["st"])
     fetch("gn", r["gains"], r["gn"])
     fetch("fq", r["freq"], r["fq"])
-    fetch("wq", r["wqkv"].at[:, z], r["wq"].at[z])
+    for k in range(4):
+        fetch("wq%d" % k, qcols(z, k), r["wq"].at[z, :, k * 128 : (k + 1) * 128])
     fetch("wo", r["wout"].at[:, pl.ds(pl.multiple_of(n * 256, 256), 256)], r["wo"].at[n])
     fetch("kvv", r["kv"], r["kvv"])
     fetch("fi", r["fin"], r["fi"])
@@ -210,10 +226,17 @@
     lane8 = lax.broadcasted_iota(jnp.int32, (8, 128), 1)
     rs8 = jnp.where(row8 < 4, rs[0:1, 0:1], rs[1:2, 0:1])
 
+    mark("barrier")
     pl.semaphore_wait(bar, len(peers))
+    mark("s1")
 
     finish = z_then_plane("s1", "s2", "s1s", "s1r", "raw")
-    z_send("wq", lambda zz: r["wqkv"].at[:, zz], r["wq"].at[z])
+    for zz in zpeers:
+        for k in range(4):
+            send(
+                "wq", qcols(zz, k), r["wq"].at[z, :, k * 128 : (k + 1) * 128],
+                z * 4 + k, at_z(zz), zz * 4 + k,
+            )
     xy_send(
         "wo",
         lambda m: r["wout"].at[:, pl.ds(pl.multiple_of(m * 256, 256), 256)],
@@ -228,15 +251,20 @@
     for b in range(32):
         r["g3"][b : b + 1, :] = r["gn"][2:3, b * 128 : (b + 1) * 128]
 
-    local["wq"].wait()
-    z_recv("wq", lambda zz: r["wq"].at[zz])
-    wcat = jnp.concatenate([r["wq"][s].reshape(512, 48) for s in range(NZ)], axis=1)
+    mark("wqwait")
+    for k in range(4):
+        local["wq%d" % k].wait()
+    for zz in zpeers:
+        for k in range(4):
+            recv("wq", r["wq"].at[zz, :, k * 128 : (k + 1) * 128], zz * 4 + k)
     gq = jnp.concatenate(
         [r["gn"][0:1, pl.ds(pl.multiple_of(k * 1024 + z * 128, 128), 128)] for k in range(4)], axis=1
     )
+    mark("s2wait")
     finish()
+    mark("qkv")
     lhs = (r["raw"][...].reshape(256, 512).astype(F32) * gq).astype(BF)
-    prod = jnp.dot(lhs, wcat, preferred_element_type=F32)
+    prod = lax.dot_general(lhs, r["wq"][...].reshape(QN, 512), NT, preferred_element_type=F32)
     for l in range(3):
         r["p1"][l] = prod[:, l * 128 : (l + 1) * 128]
     for zz in range(NZ):
@@ -244,6 +272,7 @@
             r["s3s"][zz, :, l * 128 : (l + 1) * 128] = r["p1"].at[l][
                 pl.ds(zz, 32, stride=8), :
             ].astype(BF)
+    mark("s3")
     z_send("s3", lambda zz: r["s3s"].at[zz], r["s3r"].at[z])
     r["s3r"][z] = r["s3s"][z]
     z_recv("s3", lambda zz: r["s3r"].at[zz])
@@ -259,10 +288,12 @@
     def tile(m):
         return pl.ds(pl.multiple_of(m * 8, 8), 8)
 
+    mark("s4")
     xy_send("s4", lambda m: r["s4s"].at[tile(m)], r["s4r"].at[tile(n)])
     r["s4r"][tile(n), :] = r["s4s"][tile(n), :]
     xy_recv("s4", lambda m: r["s4r"].at[tile(m)])
 
+    mark("heads")
     blocks = {
         (yy, l): jnp.concatenate(
             [r["s4r"][pl.ds(yy * 8 + l * 2 + j, 4, stride=32), :] for j in range(2)], axis=0
@@ -291,6 +322,7 @@
             turned = jnp.where(row8 % 4 == 3, val, turned)
         r["hs"][pl.ds(hh, 8, stride=12), :] = turned
 
+    mark("attn")
     local["kvv"].wait()
     inv_root = HD**-0.5
     group = lax.broadcasted_iota(jnp.int32, (32, 128), 0) // 4
@@ -299,16 +331,15 @@
         == lax.broadcasted_iota(jnp.int32, (32, 8), 1)
     )
     place = lax.broadcasted_iota(jnp.int32, (32, CACHE), 1)
-    nt = (((1,), (1,)), ((), ()))
     for j in range(2):
         q = r["hs"][j * 48 : j * 48 + 32, :]
         kn = r["hs"][j * 48 + 32 : j * 48 + 40, :].astype(BF)
         vn = r["hs"][j * 48 + 40 : j * 48 + 48, :].astype(BF)
         qd = jnp.concatenate([jnp.where(group == k, q, 0.0) for k in range(KV)], axis=1).astype(BF)
         scores = (
-            lax.dot_general(qd, r["kvv"][j, :, : KV * HD], nt, preferred_element_type=F32) * inv_root
-        )
-        fresh = lax.dot_general(q.astype(BF), kn, nt, preferred_element_type=F32)
+            lax.dot_general(qd, r["kvv"][j, :, : KV * HD], NT, preferred_element_type=F32) * inv_root
+        )
+        fresh = lax.dot_general(q.astype(BF), kn, NT, preferred_element_type=F32)
         fresh = jnp.sum(jnp.where(group8, fresh, 0.0), axis=1, keepdims=True) * inv_root
         scores = jnp.where(place < pos[j], scores, -1e30)
         peak = jnp.maximum(jnp.max(scores, axis=1, keepdims=True), fresh)
@@ -323,6 +354,7 @@
             out = out + jnp.where(group == k, wide[:, k * 128 : (k + 1) * 128], 0.0)
         r["osc"][j * 32 : j * 32 + 32, :] = out.astype(BF).astype(F32)
 
+    mark("s5")
     spread("osc", "s5s")
     finish = z_then_plane("s5", "s6", "s5s", "s5r", "att")
     local["wo"].wait()
@@ -330,7 +362,9 @@
     resid = r["raw"][:, :, pl.ds(pl.multiple_of(x * 128, 128), 128)].reshape(256, 128).astype(F32)
     lo = resid * jnp.where(z == 2 * y, 1.0, 0.0)
     hi = resid * jnp.where(z == 2 * y + 1, 1.0, 0.0)
+    mark("s6wait")
     finish()
+    mark("oproj")
     prod = jnp.dot(
         r["att"][...].reshape(256, 512), r["wo"][...].reshape(512, 256), preferred_element_type=F32
     ) + jnp.concatenate([lo, hi], axis=1)
@@ -341,6 +375,7 @@
                 r["s7s"][xl * 4 + ys, j * 16 : j * 16 + 16, :] = jnp.concatenate(
                     [prod[a : a + 8] for a in at], axis=0
                 ).astype(BF)
+    mark("s7")
     z_send("s7", lambda zz: r["s7s"].at[zz], r["s7r"].at[z])
     r["s7r"][z] = r["s7s"][z]
     z_recv("s7", lambda zz: r["s7r"].at[zz])
@@ -352,6 +387,7 @@
         return pl.ds(pl.multiple_of(zz * 32, 32), 32)
 
     r["mid"][n, z32(z), :] = acc.astype(BF)
+    mark("s8")
     z_send("s8", lambda zz: r["mid"].at[n, z32(z)], r["mid"].at[n, z32(z)])
     r["accg"][...] = jnp.zeros((256, FFD), F32)
     r["accu"][...] = jnp.zeros((256, FFD), F32)
@@ -360,6 +396,7 @@
         local[name].wait()
     z_recv("s8", lambda zz: r["mid"].at[n, z32(zz)])
 
+    mark("gather1")
     near = (1, 3, 2)
     for d in (2, 1, 3):
         xx, yy = rem(x + d, NX), rem(y + d, NY)
@@ -381,7 +418,9 @@
                 axis=1,
             )
             act = (v4 * f).reshape(256, 256).astype(BF)
-            r[name][...] += jnp.dot(act, r["wg"][k, m], preferred_element_type=F32)
+            r[name][...] += lax.dot_general(
+                act, r["wg"][k, :, cols], NT, preferred_element_type=F32
+            )
 
     ffn_chunk(n)
     top, low = pl.ds(0, 128), pl.ds(128, 128)
@@ -399,12 +438,16 @@
             xx = rem(x + e, NX)
             send("fb_", r["mid"].at[m, low], r["mid"].at[m, low], m, at_xy(xx, y), m * 4 + e)
 
+    mark("lines")
+
     def line_step(i, carry):
         ffn_chunk(rem(x + 1 + i, NX) * 4 + y)
         ffn_chunk(x * 4 + rem(y + 1 + i, NY))
         return carry
 
     lax.fori_loop(0, 3, line_step, 0)
+
+    mark("diag")
 
     def diag_step(i, carry):
         m = rem(x + 1 + i // 3, NX) * 4 + rem(y + 1 + i % 3, NY)
@@ -414,11 +457,12 @@
         return carry
 
     lax.fori_loop(0, 9, diag_step, 0)
+    mark("act")
     scale = lax.rsqrt(jnp.sum(r["ssq"][...], axis=1, keepdims=True) * (1.0 / D) + 1e-5)
 
     def by_member(k):
         return jnp.concatenate(
-            [r["fh"][i, k : k + 1, :].reshape(1, 1, 1, FFD) for i in range(2)], axis=1
+            [r["fh"][k, i : i + 1, :].reshape(1, 1, 1, FFD) for i in range(2)], axis=1
         )
 
     gate = (r["accg"][...] * scale).reshape(16, 2, 8, FFD) * by_member(0)
@@ -443,6 +487,8 @@
             "b1", r["p3"].at[:, yy, :, high(ch)], r["r1b"].at[y, :, :, chunk(ch)],
             ch * 4 + y, at_xy(x, yy), ch * 4 + yy,
         )
+
+    mark("down")
 
     def down_step(ch, carry):
         for cols in (chunk(ch), high(ch)):
@@ -466,6 +512,8 @@
             "b2", r["s2b"].at[xx, :, chunk(ch)], r["r2b"].at[x, :, chunk(ch)],
             ch * 4 + x, at_xy(xx, y), ch * 4 + xx,
         )
+
+    mark("rs1")
 
     def second_step(ch, carry):
         for d in near:
@@ -489,6 +537,7 @@
         return carry
 
     lax.fori_loop(0, NCH, second_step, 0)
+    mark("rs2wait")
     for ch in range(NCH):
         for d in near:
             yy = rem(y + d, NY)
@@ -496,6 +545,7 @@
             xx = rem(x + d, NX)
             recv("b2", r["r2b"].at[xx, :, chunk(ch)], ch * 4 + xx)
 
+    mark("rs2sum")
     row16 = lax.broadcasted_iota(jnp.int32, (16, 128), 0)
     own_row = rem(row16, 8) == z
     tile16 = pl.ds(pl.multiple_of(n * 16, 16), 16)
@@ -512,6 +562,7 @@
         m = r["mid"][b // 2, tile16, (b % 2) * 128 : (b % 2 + 1) * 128].astype(F32)
         r["f3"][b * 16 : (b + 1) * 16, :] = v + jnp.where(own_row, m, 0.0)
 
+    mark("s13")
     for zz in range(NZ):
         for m in range(2):
             r["s13s"][zz, m * 32 : (m + 1) * 32, :] = r["f3"][
@@ -520,6 +571,7 @@
     z_send("s13", lambda zz: r["s13s"].at[zz], r["s13r"].at[z])
     owned = [r["f3"][pl.ds(m * 8 + z, 32, stride=16), :] for m in range(2)]
     z_recv("s13", lambda zz: r["s13r"].at[zz])
+    mark("finalnorm")
     both = jnp.zeros((32, 128), F32)
     for m in range(2):
         v = owned[m]
@@ -533,16 +585,20 @@
     def half(k):
         return pl.ds(pl.multiple_of(k * 16, 16), 16)
 
+    mark("fx")
     send("fx", r["fs"].at[half(1 - c)], r["fr"], 0, partner)
     recv("fx", r["fr"], 0)
     r["fb"][n, z] = ((r["fs"][half(c), :] + r["fr"][...]) * 0.25).astype(BF)
+    mark("s14")
     z_send("s14", lambda zz: r["fb"].at[n, z], r["fb"].at[n, z])
     local["lm"].wait()
     local["tg"].wait()
     wanted = jnp.broadcast_to(r["tg"][...].astype(F32), (B, B)).T[:, 0:1]
     z_recv("s14", lambda zz: r["fb"].at[n, zz])
+    mark("s15")
     xy_send("s15", lambda m: r["fb"].at[n], r["fb"].at[n])
     xy_recv("s15", lambda m: r["fb"].at[m])
+    mark("lhs")
     r["ff"][...] = r["fb"][...].reshape(2048, 128).astype(F32)
     for b in range(16):
         rows = [
@@ -551,12 +607,15 @@
             for zz in range(NZ)
         ]
         r["lh"][:, b * 128 : (b + 1) * 128] = jnp.concatenate(rows, axis=0).astype(BF)
+    mark("lmdot")
     r["lp"][...] = jnp.dot(r["lh"][...], r["lm"][...], preferred_element_type=F32)
+    mark("lx")
     send("lx", r["lp"], r["lr"], 0, partner)
     recv("lx", r["lr"], 0)
     mean_f = r["lp"][...] + r["lr"][...]
     r["logits_o"][...] = mean_f.astype(BF)
 
+    mark("stats")
     ids = (lax.broadcasted_iota(jnp.int32, (B, VD), 1) + t * VD).astype(F32)
     found = jnp.sum(jnp.where(ids == wanted, mean_f, 0.0), axis=1, keepdims=True)
     peak = jnp.max(mean_f, axis=1, keepdims=True)
@@ -577,15 +636,18 @@
             hit = hit + ref[k, 2:3, :]
         return top_, tot, hit
 
+    mark("s16")
     z_send("s16", lambda zz: r["sz"].at[z], r["sz"].at[z])
     z_recv("s16", lambda zz: r["sz"].at[zz])
     a, b_, h = combine(r["sz"], NZ)
     r["sx"][n] = jnp.concatenate([a, b_, h, jnp.zeros((5, 128), F32)], axis=0)
+    mark("s17")
     xy_send("s17", lambda m: r["sx"].at[n], r["sx"].at[n])
     xy_recv("s17", lambda m: r["sx"].at[m])
     a, b_, h = combine(r["sx"], NP)
     r["lp_o"][...] = h - (a + jnp.log(b_))
 
+    mark("drain")
     for k in sends:
         k.wait_send()
 
@@ -598,6 +660,7 @@
         return carry
 
     lax.fori_loop(0, NCH, drain, 0)
+    mark(None)
     for name in debug:
         r["dbg_" + name][...] = r[name][...]
 
@@ -610,9 +673,9 @@
     freq = jnp.asarray(np.concatenate([freq, freq])[None, :], F32)
     args = dict(
         stream=stream_in, kv=kv_cache, lengths=lengths, targets=targets.reshape(1, B),
-        gains=norm_gains, wqkv=w_qkv.reshape(4, NZ, 128, 48), wout=w_out,
-        wgu=w_gate_up.reshape(2, NP, 256, FFD), wdown=w_down, lmh=lm_head,
-        fin=fast_in, fhid=fast_hidden, fout=fast_out, freq=freq,
+        gains=norm_gains, wqkv=w_qkv.T, wout=w_out,
+        wgu=w_gate_up.swapaxes(1, 2), wdown=w_down, lmh=lm_head,
+        fin=fast_in, fhid=fast_hidden.swapaxes(0, 1), fout=fast_out, freq=freq,
     )
     outs = ["logits_o", "lp_o"] + ["dbg_" + k for k in debug]
     shapes = [jax.ShapeDtypeStruct((B, VD), BF), jax.ShapeDtypeStruct((1, B), F32)] + [

time: 155 us -> 133 us (0.86)
  Pallas kernels: 142 us -> 129 us
  local copies, waits for them, and re-layouts: 10.3 us -> 2.74 us
    pallas_call x1, Pallas kernels: 142 us -> 129 us  [body(): pl.pallas_call(functools.partial(kernel, names, debug), out_shape=shapes,...]
    unnamed x5 -> x2, local copies, waits for them, and re-layouts: 10.3 us -> 2.74 us
where the time goes in v2:
time: 133 us; the launch traced here: 132 us
  Pallas kernels  129 us (97%)
  local copies, waits for them, and re-layouts  2.74 us (2%)
    pallas_call x1, Pallas kernels, body(): pl.pallas_call(functools.partial(kernel, names, debug), out_shape=shapes,...  129 us
    unnamed x2, local copies, waits for them, and re-layouts  2.74 us

profile of v2, /device:TPU:32, one launch (start us, length us, event | category | flops | bytes accessed | tf_op | source)
XLA Modules:
  0.0 132.3 jit_solution(675293393919028005)
XLA Ops:
  0.6 129.0 %step.1 = (bf16[128,512]{1,0:T(8,128)(2,1)}, f32[1,128]{1,0:T(1,128)}) custom-call(bf16[2,4096]{1,0:T(2,128)(2,1)} %refs_0_.1, bf16[2,512,2048]{2,1,0:T(8,128)(2,1)} %refs_1_.1, s32[128]{0:T(128)} %refs_2_.1, s32[1,128]{1,0:T(1,128)} %bitcast.8, f32[3,4096]{1,0:T(4,128)} %refs_4_.1, bf16[48,4096]{1,0:T(8,128)(2,1)} %bitcast.6, bf16[32,4096]{1,0:T(8,128)(2,1)} %refs_6_.1, ...), custom_call_target="tpu_custom_call" | custom-call | tf_op jit(solution)/shard_map/step/pallas_call | solution.py:692
  129.6 1.6 %copy.18 = bf16[128,512]{1,0:T(8,128)(2,1)} copy(bf16[128,512]{1,0:T(8,128)(2,1)} %get-tuple-element.8) | data formatting | bytes 262144
  131.2 1.2 copy.19

commit v3 on v1

v3 whole, which is shorter than its diff:
```python
import functools
from types import SimpleNamespace

import jax
import jax.numpy as jnp
import numpy as np
from jax import lax
from jax.experimental import pallas as pl
from jax.experimental.pallas import tpu as pltpu
from jax.sharding import Mesh
from jax.sharding import PartitionSpec as P

MESH = pl.DeviceIdType.MESH
F32 = jnp.float32
BF = jnp.bfloat16
NX, NZ, NY = 4, 8, 4
NP = NX * NY
D, HEADS, KV, HD, CACHE, FFD, VD = 4096, 32, 8, 128, 512, 112, 512
B = 128
QN = 384
ZORDER = (4, 3, 5, 2, 6, 1, 7)
NCH, CW = 4, 512
HALF = D // 2
NT = (((1,), (1,)), ((), ()))

VM = pltpu.VMEM
DMA = pltpu.SemaphoreType.DMA

SCRATCH = dict(
    st=VM((2, D), BF),
    kvv=VM((2, CACHE, 2 * KV * HD), BF),
    tg=VM((1, B), jnp.int32),
    gn=VM((3, D), F32),
    fi=VM((2, 2, D), F32),
    fh=VM((3, 2, FFD), F32),
    fo=VM((2, D), F32),
    fq=VM((1, 128), F32),
    wq=VM((NZ, 48, 512), BF),
    wo=VM((NP, 32, 256), BF),
    wg=VM((2, FFD, D), BF),
    wd=VM((FFD, D), BF),
    lm=VM((HALF, VD), BF),
    sc=VM((64, 128), F32),
    s1s=VM((64, 128), F32),
    s1r=VM((64, 128), F32),
    raw=VM((NP, 16, 512), BF),
    p1=VM((3, 256, 128), F32),
    s3s=VM((NZ, 32, QN), BF),
    s3r=VM((NZ, 32, QN), BF),
    q1=VM((3, 32, 128), F32),
    s4s=VM((128, 128), F32),
    s4r=VM((128, 128), F32),
    hs=VM((96, 128), F32),
    osc=VM((64, 128), F32),
    s5s=VM((64, 128), F32),
    s5r=VM((64, 128), F32),
    att=VM((NP, 16, 512), BF),
    s7s=VM((NZ, 32, 256), BF),
    s7r=VM((NZ, 32, 256), BF),
    mid=VM((NP, 256, 256), BF),
    accg=VM((256, FFD), F32),
    accu=VM((256, FFD), F32),
    ssq=VM((256, 128), F32),
    hid=VM((256, FFD), BF),
    p3=VM((NX, NY, 16, D), BF),
    r1a=VM((NX, NY, 16, HALF), BF),
    r1b=VM((NY, NX, 16, HALF), BF),
    s2a=VM((NY, 16, HALF), BF),
    s2b=VM((NX, 16, HALF), BF),
    r2a=VM((NY, 16, HALF), BF),
    r2b=VM((NX, 16, HALF), BF),
    f3=VM((512, 128), F32),
    g3=VM((32, 128), F32),
    s13s=VM((NZ, 64, 128), BF),
    s13r=VM((NZ, 64, 128), BF),
    fs=VM((32, 128), F32),
    fr=VM((16, 128), F32),
    fb=VM((NP, NZ, 16, 128), BF),
    ff=VM((2048, 128), F32),
    lh=VM((B, HALF), BF),
    lp=VM((B, VD), F32),
    lr=VM((B, VD), F32),
    sz=VM((NZ, 8, 128), F32),
    sx=VM((NP, 8, 128), F32),
)
PHASES = dict(
    wq=1, wqf=1, wo=1, s1=1, s2=1, s3=1, s4=1, s5=1, s6=1, s7=1, s8=1, da=6, dg=9,
    a1=NCH, b1=NCH, a2=1, b2=1, s13=1, fx=1, s14=1, s15=1, lx=1, s16=1, s17=1,
)
LS = dict(ls=DMA((16,)))
OUTS = dict(
    logits_o=jax.ShapeDtypeStruct((B, VD), BF), lp_o=jax.ShapeDtypeStruct((1, B), F32)
)


def kernel(inputs, *refs):
    names = [*inputs, *OUTS, *SCRATCH, *LS]
    r = SimpleNamespace(**dict(zip(names, refs)))
    sems = iter(refs[len(names) :])
    p = SimpleNamespace(**{k: (next(sems), next(sems)) for k in PHASES})
    c, x, z, y = (lax.axis_index(a) for a in MEMBER_TP)
    t = x * 32 + z * 4 + y
    n = x * 4 + y
    drains = []
    def rem(v, k):
        return lax.rem(v, k)

    def at_z(zz):
        return (c, x, zz, y)

    def at_xy(xx, yy):
        return (c, xx, z, yy)

    partner = (1 - c, x, z, y)

    def copy(phase, src, dst, dev, slot=0):
        return pltpu.make_async_remote_copy(
            src_ref=src,
            dst_ref=dst,
            send_sem=phase[0].at[0],
            recv_sem=phase[1].at[slot],
            device_id=dev,
            device_id_type=MESH,
        )

    def send(phase, src, dst, dev, slot=0):
        copy(phase, src, dst, dev, slot).start()

    def wait_bytes(sem, ref):
        pltpu.make_async_copy(ref, ref, sem).wait()

    def recv(phase, ref, slot=0):
        wait_bytes(phase[1].at[slot], ref)

    def sent(phase, ref):
        drains.append((phase[0].at[0], ref))

    zpeers = [rem(z + d, NZ) for d in ZORDER]
    plane = [
        (rem(x + dx, NX), rem(y + dy, NY))
        for dx, dy in sorted(
            ((a, b) for a in range(NX) for b in range(NY) if a or b),
            key=lambda p: -(min(p[0], 4 - p[0]) + min(p[1], 4 - p[1])),
        )
    ]

    def z_send(phase, src_at, dst):
        for zz in zpeers:
            send(phase, src_at(zz), dst, at_z(zz))

    def xy_send(phase, src_at, dst):
        for xx, yy in plane:
            send(phase, src_at(xx * 4 + yy), dst, at_xy(xx, yy))

    def done(phase, ref):
        recv(phase, ref)
        sent(phase, ref)

    bar = pltpu.get_barrier_semaphore()
    peers = [at_z(zz) for zz in zpeers] + [at_xy(*p) for p in plane] + [partner]
    for dev in peers:
        pl.semaphore_signal(bar, inc=1, device_id=dev, device_id_type=MESH)

    def qcols(zz, k):
        return r.wqkv.at[:, pl.ds(pl.multiple_of(k * 1024 + zz * 128, 128), 128)]

    def half_cols(k):
        return pl.ds(pl.multiple_of((2 * c + k) * 128, 128), 128)

    local = SimpleNamespace()
    begun = []

    def fetch(src, dst):
        k = pltpu.make_async_copy(src, dst, r.ls.at[len(begun)])
        k.start()
        begun.append(k)
        return k

    local.st = fetch(r.stream, r.st)
    local.gn = fetch(r.gains, r.gn)
    local.fq = fetch(r.freq, r.fq)
    local_wq = [fetch(qcols(z, 2 * c + k), r.wq.at[z, :, half_cols(k)]) for k in range(2)]
    local.wo = fetch(r.wout.at[:, pl.ds(pl.multiple_of(n * 256, 256), 256)], r.wo.at[n])
    local.kvv = fetch(r.kv, r.kvv)
    local.fi = fetch(r.fin, r.fi)
    local.fh = fetch(r.fhid, r.fh)
    local.fo = fetch(r.fout, r.fo)
    local.tg = fetch(r.targets, r.tg)
    local.wg = fetch(r.wgu, r.wg)
    local.wd = fetch(r.wdown, r.wd)
    local.lm = fetch(r.lmh.at[pl.ds(pl.multiple_of(c * HALF, HALF), HALF)], r.lm)

    def spread(scratch, dst):
        for zz in range(NZ):
            dst[zz * 8 : zz * 8 + 8] = scratch[pl.ds(zz, 8, stride=8), :]

    z8 = pl.ds(pl.multiple_of(z * 8, 8), 8)

    def z_then_plane(zphase, pphase, s, rr, buf, start=True):
        def piece(zz):
            return pl.ds(pl.multiple_of(zz * 8, 8), 8)

        if start:
            z_send(zphase, lambda zz: s.at[piece(zz)], rr.at[z8])
        rr[z8, :] = s[z8, :]
        done(zphase, rr.at[0:56])
        for k in range(4):
            rows = [rr[pl.ds(j * 4 + k, 8, stride=8), :] for j in range(2)]
            buf[n, :, k * 128 : (k + 1) * 128] = jnp.concatenate(rows, axis=0).astype(BF)
        xy_send(pphase, lambda m: buf.at[n], buf.at[n])
        return lambda: done(pphase, buf.at[0:15])

    local.st.wait()
    x32 = r.st[...].astype(F32)
    rs = lax.rsqrt(jnp.mean(x32 * x32, axis=-1, keepdims=True) + 1e-5)
    for b in range(32):
        for j in range(2):
            r.sc[j * 32 + b : j * 32 + b + 1, :] = x32[j : j + 1, b * 128 : (b + 1) * 128]
    spread(r.sc, r.s1s)
    r.s4s[...] = jnp.zeros((128, 128), F32)
    row8 = lax.broadcasted_iota(jnp.int32, (8, 128), 0)
    lane8 = lax.broadcasted_iota(jnp.int32, (8, 128), 1)
    rs8 = jnp.where(row8 < 4, rs[0:1, 0:1], rs[1:2, 0:1])

    pl.semaphore_wait(bar, len(peers))

    for zz in zpeers:
        send(p.s1, r.s1s.at[pl.ds(pl.multiple_of(zz * 8, 8), 8)], r.s1r.at[z8], at_z(zz))
    for zz in zpeers:
        for k in range(2):
            send(p.wq, qcols(zz, 2 * c + k), r.wq.at[z, :, half_cols(k)], at_z(zz))
    finish = z_then_plane(p.s1, p.s2, r.s1s, r.s1r, r.raw, False)
    xy_send(
        p.wo,
        lambda m: r.wout.at[:, pl.ds(pl.multiple_of(m * 256, 256), 256)],
        r.wo.at[n],
    )
    local.fq.wait()
    local.gn.wait()
    pos = [r.lengths[rem(2 * t + j, B)] for j in range(2)]
    ang = jnp.where(row8 < 4, pos[0], pos[1]).astype(F32) * r.fq[0:1, :]
    cos8 = jnp.cos(ang)
    sin8 = jnp.where(lane8 < 64, -jnp.sin(ang), jnp.sin(ang))
    for b in range(32):
        r.g3[b : b + 1, :] = r.gn[2:3, b * 128 : (b + 1) * 128]

    for k in range(2):
        local_wq[k].wait()
    done(p.wq, r.wq.at[0:7, :, 0:256])
    mine = r.wq.at[:, :, pl.ds(pl.multiple_of(c * 256, 256), 256)]
    send(p.wqf, mine, mine, partner)
    done(p.wqf, mine)
    gq = jnp.concatenate(
        [r.gn[0:1, pl.ds(pl.multiple_of(k * 1024 + z * 128, 128), 128)] for k in range(4)], axis=1
    )
    finish()
    lhs = (r.raw[...].reshape(256, 512).astype(F32) * gq).astype(BF)
    prod = lax.dot_general(lhs, r.wq[...].reshape(QN, 512), NT, preferred_element_type=F32)
    for l in range(3):
        r.p1[l] = prod[:, l * 128 : (l + 1) * 128]
    for zz in range(NZ):
        for l in range(3):
            r.s3s[zz, :, l * 128 : (l + 1) * 128] = r.p1.at[l][
                pl.ds(zz, 32, stride=8), :
            ].astype(BF)
    z_send(p.s3, lambda zz: r.s3s.at[zz], r.s3r.at[z])
    r.s3r[z] = r.s3s[z]
    done(p.s3, r.s3r.at[0:7])
    acc = r.s3r[0].astype(F32)
    for s in range(1, NZ):
        acc = acc + r.s3r[s].astype(F32)
    for l in range(3):
        r.q1[l] = acc[:, l * 128 : (l + 1) * 128]
    for l in range(3):
        for j in range(2):
            r.s4s[pl.ds(l * 2 + j, 16, stride=8), :] = r.q1.at[l][pl.ds(j, 16, stride=2), :]

    def tile(m):
        return pl.ds(pl.multiple_of(m * 8, 8), 8)

    xy_send(p.s4, lambda m: r.s4s.at[tile(m)], r.s4r.at[tile(n)])
    r.s4r[tile(n), :] = r.s4s[tile(n), :]
    done(p.s4, r.s4r.at[0:120])

    blocks = {
        (yy, l): jnp.concatenate(
            [r.s4r[pl.ds(yy * 8 + l * 2 + j, 4, stride=32), :] for j in range(2)], axis=0
        )
        for yy in range(NY)
        for l in range(3)
    }
    for hh in range(12):
        val = jnp.zeros((8, 128), F32)
        lane = 0
        while lane < 128:
            col = hh * 128 + lane
            tt, i = divmod(col, 48)
            at = (tt // 4) * 48 + i
            l, src = divmod(at, 128)
            width = min(48 - i, 128 - src, 128 - lane)
            piece = blocks[(tt % 4, l)]
            shift = (lane - src) % 128
            if shift:
                piece = pltpu.roll(piece, shift, 1)
            val = jnp.where((lane8 >= lane) & (lane8 < lane + width), piece, val)
            lane += width
        val = (val * rs8).astype(BF).astype(F32)
        turned = (val * cos8 + pltpu.roll(val, 64, 1) * sin8).astype(BF).astype(F32)
        if hh >= 4:
            turned = jnp.where(row8 % 4 == 3, val, turned)
        r.hs[pl.ds(hh, 8, stride=12), :] = turned

    local.kvv.wait()
    inv_root = HD**-0.5
    group = lax.broadcasted_iota(jnp.int32, (32, 128), 0) // 4
    group8 = (
        lax.broadcasted_iota(jnp.int32, (32, 8), 0) // 4
        == lax.broadcasted_iota(jnp.int32, (32, 8), 1)
    )
    place = lax.broadcasted_iota(jnp.int32, (32, CACHE), 1)
    for j in range(2):
        q = r.hs[j * 48 : j * 48 + 32, :]
        kn = r.hs[j * 48 + 32 : j * 48 + 40, :].astype(BF)
        vn = r.hs[j * 48 + 40 : j * 48 + 48, :].astype(BF)
        qd = jnp.concatenate([jnp.where(group == k, q, 0.0) for k in range(KV)], axis=1).astype(BF)
        scores = (
            lax.dot_general(qd, r.kvv[j, :, : KV * HD], NT, preferred_element_type=F32) * inv_root
        )
        fresh = lax.dot_general(q.astype(BF), kn, NT, preferred_element_type=F32)
        fresh = jnp.sum(jnp.where(group8, fresh, 0.0), axis=1, keepdims=True) * inv_root
        scores = jnp.where(place < pos[j], scores, -1e30)
        peak = jnp.maximum(jnp.max(scores, axis=1, keepdims=True), fresh)
        weights = jnp.exp(scores - peak)
        fresh_w = jnp.exp(fresh - peak)
        total = jnp.sum(weights, axis=1, keepdims=True) + fresh_w
        probs = (weights / total).astype(BF)
        fresh_p = jnp.where(group8, fresh_w / total, 0.0).astype(BF)
        wide = jnp.dot(probs, r.kvv[j, :, KV * HD :], preferred_element_type=F32)
        out = jnp.dot(fresh_p, vn, preferred_element_type=F32)
        for k in range(KV):
            out = out + jnp.where(group == k, wide[:, k * 128 : (k + 1) * 128], 0.0)
        r.osc[j * 32 : j * 32 + 32, :] = out.astype(BF).astype(F32)

    spread(r.osc, r.s5s)
    finish = z_then_plane(p.s5, p.s6, r.s5s, r.s5r, r.att)
    local.wo.wait()
    done(p.wo, r.wo.at[0:15])
    resid = r.raw[:, :, pl.ds(pl.multiple_of(x * 128, 128), 128)].reshape(256, 128).astype(F32)
    lo = resid * jnp.where(z == 2 * y, 1.0, 0.0)
    hi = resid * jnp.where(z == 2 * y + 1, 1.0, 0.0)
    finish()
    prod = jnp.dot(
        r.att[...].reshape(256, 512), r.wo[...].reshape(512, 256), preferred_element_type=F32
    ) + jnp.concatenate([lo, hi], axis=1)
    for xl in range(2):
        for ys in range(NY):
            for j in range(2):
                at = [((m * 2 + xl) * 4 + ys) * 16 + j * 8 for m in range(2)]
                r.s7s[xl * 4 + ys, j * 16 : j * 16 + 16, :] = jnp.concatenate(
                    [prod[a : a + 8] for a in at], axis=0
                ).astype(BF)
    z_send(p.s7, lambda zz: r.s7s.at[zz], r.s7r.at[z])
    r.s7r[z] = r.s7s[z]
    done(p.s7, r.s7r.at[0:7])
    acc = r.s7r[0].astype(F32)
    for s in range(1, NZ):
        acc = acc + r.s7r[s].astype(F32)

    def z32(zz):
        return pl.ds(pl.multiple_of(zz * 32, 32), 32)

    r.mid[n, z32(z), :] = acc.astype(BF)
    z_send(p.s8, lambda zz: r.mid.at[n, z32(z)], r.mid.at[n, z32(z)])
    r.accg[...] = jnp.zeros((256, FFD), F32)
    r.accu[...] = jnp.zeros((256, FFD), F32)
    r.ssq[...] = jnp.zeros((256, 128), F32)
    for k in (local.fi, local.fh, local.fo, local.wg, local.wd):
        k.wait()
    done(p.s8, r.mid.at[n, 0:224])

    near = (1, 3, 2)
    for d in (2, 1, 3):
        xx, yy = rem(x + d, NX), rem(y + d, NY)
        send(p.da, r.mid.at[n], r.mid.at[n], at_xy(xx, y), 3 - d)
        send(p.da, r.mid.at[n], r.mid.at[n], at_xy(x, yy), 6 - d)
    sent(p.da, r.mid.at[0:6])

    def ffn_chunk(m):
        v = r.mid[m].astype(F32)
        r.ssq[...] += v[:, :128] * v[:, :128] + v[:, 128:] * v[:, 128:]
        cols = pl.ds(pl.multiple_of(m * 256, 256), 256)
        g = r.gn[1:2, cols]
        v4 = v.reshape(16, 2, 8, 256)
        for k, total in enumerate((r.accg, r.accu)):
            f = jnp.concatenate(
                [
                    (r.fi[i, k : k + 1, cols] * g).reshape(1, 1, 1, 256)
                    for i in range(2)
                ],
                axis=1,
            )
            act = (v4 * f).reshape(256, 256).astype(BF)
            total[...] += lax.dot_general(
                act, r.wg[k, :, cols], NT, preferred_element_type=F32
            )

    ffn_chunk(n)
    top, low = pl.ds(0, 128), pl.ds(128, 128)
    for d in near:
        m = rem(x + d, NX) * 4 + y
        recv(p.da, r.mid.at[m], d - 1)
        for e in (2, 1, 3):
            yy = rem(y + e, NY)
            send(p.dg, r.mid.at[m, top], r.mid.at[m, top], at_xy(x, yy), (d - 1) * 3 + 3 - e)
        m = x * 4 + rem(y + d, NY)
        recv(p.da, r.mid.at[m], d + 2)
        for e in (2, 1, 3):
            xx = rem(x + e, NX)
            send(p.dg, r.mid.at[m, low], r.mid.at[m, low], at_xy(xx, y), (3 - e) * 3 + d - 1)
    sent(p.dg, r.mid.at[0:9])

    def line_step(i, carry):
        ffn_chunk(rem(x + 1 + i, NX) * 4 + y)
        ffn_chunk(x * 4 + rem(y + 1 + i, NY))
        return carry

    lax.fori_loop(0, 3, line_step, 0)

    def diag_step(i, carry):
        m = rem(x + 1 + i // 3, NX) * 4 + rem(y + 1 + i % 3, NY)
        recv(p.dg, r.mid.at[m], i)
        ffn_chunk(m)
        return carry

    lax.fori_loop(0, 9, diag_step, 0)
    scale = lax.rsqrt(jnp.sum(r.ssq[...], axis=1, keepdims=True) * (1.0 / D) + 1e-5)

    def by_member(k):
        return jnp.concatenate(
            [r.fh[k, i : i + 1, :].reshape(1, 1, 1, FFD) for i in range(2)], axis=1
        )

    gate = (r.accg[...] * scale).reshape(16, 2, 8, FFD) * by_member(0)
    up = (r.accu[...] * scale).reshape(16, 2, 8, FFD) * by_member(1)
    hidden = gate / (1.0 + jnp.exp(-gate)) * up * by_member(2)
    r.hid[...] = hidden.reshape(256, FFD).astype(BF)

    def chunk(ch):
        return pl.ds(pl.multiple_of(ch * CW, CW), CW)

    def high(ch):
        return pl.ds(pl.multiple_of(HALF + ch * CW, CW), CW)

    def a1(ch, xx):
        at = r.p3.at[xx, :, :, chunk(ch)]
        send(p.a1, at, r.r1a.at[x, :, :, chunk(ch)], at_xy(xx, y), ch)

    def b1(ch, yy):
        at = r.p3.at[:, yy, :, high(ch)]
        send(p.b1, at, r.r1b.at[y, :, :, chunk(ch)], at_xy(x, yy), ch)

    def down_step(ch, carry):
        for cols in (chunk(ch), high(ch)):
            v = jnp.dot(r.hid[...], r.wd[:, cols], preferred_element_type=F32)
            r.p3[:, :, :, cols] = v.astype(BF).reshape(NX, NY, 16, CW)
        for d in (2, 1, 3):
            a1(ch, rem(x + d, NX))
            b1(ch, rem(y + d, NY))
        return carry

    lax.fori_loop(0, NCH, down_step, 0)

    def a2(ch, yy):
        send(p.a2, r.s2a.at[yy, :, chunk(ch)], r.r2a.at[y, :, chunk(ch)], at_xy(x, yy))

    def b2(ch, xx):
        send(p.b2, r.s2b.at[xx, :, chunk(ch)], r.r2b.at[x, :, chunk(ch)], at_xy(xx, y))

    def second_step(ch, carry):
        recv(p.a1, r.r1a.at[0:3, :, :, chunk(ch)], ch)
        v = r.p3[x, :, :, chunk(ch)].astype(F32)
        for d in near:
            v = v + r.r1a[rem(x + d, NX), :, :, chunk(ch)].astype(F32)
        r.s2a[:, :, chunk(ch)] = v.astype(BF)
        for d in (2, 1, 3):
            a2(ch, rem(y + d, NY))
        recv(p.b1, r.r1b.at[0:3, :, :, chunk(ch)], ch)
        v = r.p3[:, y, :, high(ch)].astype(F32)
        for d in near:
            v = v + r.r1b[rem(y + d, NY), :, :, chunk(ch)].astype(F32)
        r.s2b[:, :, chunk(ch)] = v.astype(BF)
        for d in (2, 1, 3):
            b2(ch, rem(x + d, NX))
        return carry

    lax.fori_loop(0, NCH, second_step, 0)
    sent(p.a1, r.r1a.at[0:3])
    sent(p.b1, r.r1b.at[0:3])
    done(p.a2, r.r2a.at[0:3])
    done(p.b2, r.r2b.at[0:3])

    row16 = lax.broadcasted_iota(jnp.int32, (16, 128), 0)
    own_row = rem(row16, 8) == z
    tile16 = pl.ds(pl.multiple_of(n * 16, 16), 16)
    for b in range(32):
        own, got, me, count = (
            (r.s2a, r.r2a, y, NY) if b < 16 else (r.s2b, r.r2b, x, NX)
        )
        cols = slice((b % 16) * 128, (b % 16 + 1) * 128)
        v = own[me, :, cols].astype(F32)
        for d in near:
            v = v + got[rem(me + d, count), :, cols].astype(F32)
        at = slice(b * 128, (b + 1) * 128)
        v = v * jnp.where(row16 < 8, r.fo[0:1, at], r.fo[1:2, at])
        m = r.mid[b // 2, tile16, (b % 2) * 128 : (b % 2 + 1) * 128].astype(F32)
        r.f3[b * 16 : (b + 1) * 16, :] = v + jnp.where(own_row, m, 0.0)

    for zz in range(NZ):
        for m in range(2):
            r.s13s[zz, m * 32 : (m + 1) * 32, :] = r.f3[
                pl.ds(m * 8 + zz, 32, stride=16), :
            ].astype(BF)
    z_send(p.s13, lambda zz: r.s13s.at[zz], r.s13r.at[z])
    owned = [r.f3[pl.ds(m * 8 + z, 32, stride=16), :] for m in range(2)]
    done(p.s13, r.s13r.at[0:7])
    both = jnp.zeros((32, 128), F32)
    for m in range(2):
        v = owned[m]
        for zz in zpeers:
            v = v + r.s13r[zz, m * 32 : (m + 1) * 32, :].astype(F32)
        v = v.astype(BF).astype(F32)
        mean = jnp.sum(jnp.sum(v * v, axis=1, keepdims=True), axis=0, keepdims=True) * (1.0 / D)
        both = both + (v * lax.rsqrt(mean + 1e-5) * r.g3[...]).astype(BF).astype(F32)
    r.fs[...] = both

    def half(k):
        return pl.ds(pl.multiple_of(k * 16, 16), 16)

    send(p.fx, r.fs.at[half(1 - c)], r.fr, partner)
    done(p.fx, r.fr)
    r.fb[n, z] = ((r.fs[half(c), :] + r.fr[...]) * 0.25).astype(BF)
    z_send(p.s14, lambda zz: r.fb.at[n, z], r.fb.at[n, z])
    local.lm.wait()
    local.tg.wait()
    wanted = jnp.broadcast_to(r.tg[...].astype(F32), (B, B)).T[:, 0:1]
    done(p.s14, r.fb.at[n, 0:7])
    xy_send(p.s15, lambda m: r.fb.at[n], r.fb.at[n])
    done(p.s15, r.fb.at[0:15])
    r.ff[...] = r.fb[...].reshape(2048, 128).astype(F32)
    for b in range(16):
        rows = [
            r.ff[pl.ds(xl * 1024 + zz * 16 + b, 8, stride=128), :]
            for xl in range(2)
            for zz in range(NZ)
        ]
        r.lh[:, b * 128 : (b + 1) * 128] = jnp.concatenate(rows, axis=0).astype(BF)
    r.lp[...] = jnp.dot(r.lh[...], r.lm[...], preferred_element_type=F32)
    send(p.lx, r.lp, r.lr, partner)
    done(p.lx, r.lr)
    mean_f = r.lp[...] + r.lr[...]
    r.logits_o[...] = mean_f.astype(BF)

    ids = (lax.broadcasted_iota(jnp.int32, (B, VD), 1) + t * VD).astype(F32)
    found = jnp.sum(jnp.where(ids == wanted, mean_f, 0.0), axis=1, keepdims=True)
    peak = jnp.max(mean_f, axis=1, keepdims=True)
    total = jnp.sum(jnp.exp(mean_f - peak), axis=1, keepdims=True)
    lane = lax.broadcasted_iota(jnp.int32, (B, B), 1)
    stat = jnp.where(lane == 0, peak, jnp.where(lane == 1, total, jnp.where(lane == 2, found, 0.0)))
    r.sz[z] = stat.T[:8]

    def combine(ref, count):
        peaks = [ref[k, 0:1, :] for k in range(count)]
        top_ = peaks[0]
        for k in range(1, count):
            top_ = jnp.maximum(top_, peaks[k])
        tot = ref[0, 1:2, :] * jnp.exp(peaks[0] - top_)
        hit = ref[0, 2:3, :]
        for k in range(1, count):
            tot = tot + ref[k, 1:2, :] * jnp.exp(peaks[k] - top_)
            hit = hit + ref[k, 2:3, :]
        return top_, tot, hit

    z_send(p.s16, lambda zz: r.sz.at[z], r.sz.at[z])
    done(p.s16, r.sz.at[0:7])
    a, b_, h = combine(r.sz, NZ)
    r.sx[n] = jnp.concatenate([a, b_, h, jnp.zeros((5, 128), F32)], axis=0)
    xy_send(p.s17, lambda m: r.sx.at[n], r.sx.at[n])
    done(p.s17, r.sx.at[0:15])
    a, b_, h = combine(r.sx, NP)
    r.lp_o[...] = h - (a + jnp.log(b_))

    for sem, ref in drains:
        wait_bytes(sem, ref)


def body(
    stream_in, kv_cache, lengths, targets, norm_gains, w_qkv, w_out, w_gate_up, w_down, lm_head,
    fast_in, fast_hidden, fast_out,
):
    freq = np.float32(500000.0) ** (-np.arange(64, dtype=np.float32) * 2.0 / 128)
    freq = jnp.asarray(np.concatenate([freq, freq])[None, :], F32)
    args = dict(
        stream=stream_in, kv=kv_cache, lengths=lengths, targets=targets.reshape(1, B),
        gains=norm_gains, wqkv=w_qkv.T, wout=w_out,
        wgu=w_gate_up.swapaxes(1, 2), wdown=w_down, lmh=lm_head,
        fin=fast_in, fhid=fast_hidden.swapaxes(0, 1), fout=fast_out, freq=freq,
    )
    got = pl.pallas_call(
        functools.partial(kernel, list(args)),
        out_shape=list(OUTS.values()),
        in_specs=[
            pl.BlockSpec(memory_space=pltpu.SMEM if v is lengths else pl.ANY)
            for v in args.values()
        ],
        out_specs=[pl.BlockSpec(memory_space=VM)] * len(OUTS),
        scratch_shapes=[
            *SCRATCH.values(),
            *LS.values(),
            *(DMA((count,)) for n in PHASES.values() for count in (1, n)),
        ],
        compiler_params=pltpu.CompilerParams(
            collective_id=0, has_side_effects=True, vmem_limit_bytes=60 * 1024 * 1024
        ),
        name="step",
    )(*args.values())
    return (got[0], got[1].reshape(B))


MEMBER_TP = ("member", "tp_0", "tp_1", "tp_2")
TP = ("tp_0", "tp_1", "tp_2")
IN_SPECS = (
    P(MEMBER_TP, None), P(MEMBER_TP, None, None), P(), P(), P(), P(None, TP), P(TP, None),
    P(None, None, TP), P(TP, None), P(None, TP), P("member", None, None), P("member", None, TP),
    P("member", None),
)


def solution(mesh):
    split = Mesh(
        mesh.devices.reshape(mesh.shape["member"], NX, NZ, NY), MEMBER_TP
    )
    return jax.shard_map(
        body, mesh=split, in_specs=IN_SPECS, out_specs=(P(None, TP), P()), check_vma=False
    )
```

time: 155 us -> 120 us (0.77)
  Pallas kernels: 142 us -> 115 us
  local copies, waits for them, and re-layouts: 10.3 us -> 2.74 us
    pallas_call x1, Pallas kernels: 142 us -> 115 us  [body(): pl.pallas_call(functools.partial(kernel, list(args)), out_shape=list(OUTS...]
    unnamed x5 -> x2, local copies, waits for them, and re-layouts: 10.3 us -> 2.74 us
where the time goes in v3:
time: 120 us; the launch traced here: 119 us
  Pallas kernels  115 us (96%)
  local copies, waits for them, and re-layouts  2.74 us (2%)
    pallas_call x1, Pallas kernels, body(): pl.pallas_call(functools.partial(kernel, list(args)), out_shape=list(OUTS...  115 us
    unnamed x2, local copies, waits for them, and re-layouts  2.74 us

profile of v3, /device:TPU:32, one launch (start us, length us, event | category | flops | bytes accessed | tf_op | source)
XLA Modules:
  0.0 118.5 jit_solution(6480148656838841486)
XLA Ops:
  0.6 115.1 %step.1 = (bf16[128,512]{1,0:T(8,128)(2,1)}, f32[1,128]{1,0:T(1,128)}) custom-call(bf16[2,4096]{1,0:T(2,128)(2,1)} %refs_0_.1, bf16[2,512,2048]{2,1,0:T(8,128)(2,1)} %refs_1_.1, s32[128]{0:T(128)} %refs_2_.1, s32[1,128]{1,0:T(1,128)} %bitcast.8, f32[3,4096]{1,0:T(4,128)} %refs_4_.1, bf16[48,4096]{1,0:T(8,128)(2,1)} %bitcast.6, bf16[32,4096]{1,0:T(8,128)(2,1)} %refs_6_.1, ...), custom_call_target="tpu_custom_call" | custom-call | tf_op jit(solution)/shard_map/step/pallas_call | solution.py:608
  115.8 1.6 %copy.18 = bf16[128,512]{1,0:T(8,128)(2,1)} copy(bf16[128,512]{1,0:T(8,128)(2,1)} %get-tuple-element.8) | data formatting | bytes 262144
  117.3 1.2 copy.19

commit v4 on v3

--- a/solution.py
+++ b/solution.py
@@ -37,8 +37,10 @@
     fq=VM((1, 128), F32),
     wq=VM((NZ, 48, 512), BF),
     wo=VM((NP, 32, 256), BF),
-    wg=VM((2, FFD, D), BF),
-    wd=VM((FFD, D), BF),
+    wg=VM((2, 256, D), BF),
+    wd=VM((256, D), BF),
+    fhx=VM((2, 3, 2, FFD), F32),
+    fhp=VM((3, 2, 256), F32),
     lm=VM((HALF, VD), BF),
     sc=VM((64, 128), F32),
     s1s=VM((64, 128), F32),
@@ -57,18 +59,20 @@
     att=VM((NP, 16, 512), BF),
     s7s=VM((NZ, 32, 256), BF),
     s7r=VM((NZ, 32, 256), BF),
-    mid=VM((NP, 256, 256), BF),
-    accg=VM((256, FFD), F32),
-    accu=VM((256, FFD), F32),
-    ssq=VM((256, 128), F32),
-    hid=VM((256, FFD), BF),
-    p3=VM((NX, NY, 16, D), BF),
-    r1a=VM((NX, NY, 16, HALF), BF),
-    r1b=VM((NY, NX, 16, HALF), BF),
+    mc=VM((2, 128, 256), BF),
+    xb=VM((NY, 64, 256), BF),
+    mid=VM((NP, 128, 256), BF),
+    accg=VM((128, 256), F32),
+    accu=VM((128, 256), F32),
+    ssq=VM((128, 128), F32),
+    hid=VM((128, 256), BF),
+    p3=VM((2, NY, 16, D), BF),
+    r1a=VM((NY, 16, HALF), BF),
+    r1b=VM((NY, 2, 16, HALF), BF),
     s2a=VM((NY, 16, HALF), BF),
-    s2b=VM((NX, 16, HALF), BF),
+    s2b=VM((2, 16, HALF), BF),
     r2a=VM((NY, 16, HALF), BF),
-    r2b=VM((NX, 16, HALF), BF),
+    r2b=VM((16, HALF), BF),
     f3=VM((512, 128), F32),
     g3=VM((32, 128), F32),
     s13s=VM((NZ, 64, 128), BF),
@@ -84,7 +88,8 @@
     sx=VM((NP, 8, 128), F32),
 )
 PHASES = dict(
-    wq=1, wqf=1, wo=1, s1=1, s2=1, s3=1, s4=1, s5=1, s6=1, s7=1, s8=1, da=6, dg=9,
+    wq=1, wqf=1, wo=1, s1=1, s2=1, s3=1, s4=1, s5=1, s6=1, s7=1, s8=1, da=6, db=3, dg=9,
+    xg=2, xd=2, fg=2, fd=2, xh=2,
     a1=NCH, b1=NCH, a2=1, b2=1, s13=1, fx=1, s14=1, s15=1, lx=1, s16=1, s17=1,
 )
 LS = dict(ls=DMA((16,)))
@@ -101,6 +106,8 @@
     c, x, z, y = (lax.axis_index(a) for a in MEMBER_TP)
     t = x * 32 + z * 4 + y
     n = x * 4 + y
+    xl, par = x // 2, lax.rem(x, 2)
+    own = xl * 8 + y * 2 + par
     drains = []
     def rem(v, k):
         return lax.rem(v, k)
@@ -186,9 +193,27 @@
     local.fh = fetch(r.fhid, r.fh)
     local.fo = fetch(r.fout, r.fo)
     local.tg = fetch(r.targets, r.tg)
-    local.wg = fetch(r.wgu, r.wg)
-    local.wd = fetch(r.wdown, r.wd)
+    local.wg = fetch(r.wgu, r.wg.at[:, 0:FFD])
+    local.wd = fetch(r.wdown, r.wd.at[0:FFD])
     local.lm = fetch(r.lmh.at[pl.ds(pl.multiple_of(c * HALF, HALF), HALF)], r.lm)
+
+    right, left = at_xy(rem(x + 1, NX), y), at_xy(rem(x + 3, NX), y)
+
+    def weight_piece(i):
+        cols = pl.ds(pl.multiple_of(c * HALF + i * 256, 256), 256)
+        for dev, a, b in ((right, 0, 64), (left, 64, FFD)):
+            g = r.wg.at[:, 128 + a : 128 + b, cols]
+            send(p.xg, r.wgu.at[:, a:b, cols], g, dev, i // 4)
+            send(p.xd, r.wdown.at[a:b, cols], r.wd.at[128 + a : 128 + b, cols], dev, i // 4)
+
+    def pass_weights(g):
+        cols = pl.ds(pl.multiple_of(c * HALF + g * 1024, 1024), 1024)
+        for came, went, at in (
+            (p.xg, p.fg, r.wg.at[:, 128 : 128 + FFD, cols]),
+            (p.xd, p.fd, r.wd.at[128 : 128 + FFD, cols]),
+        ):
+            recv(came, at, g)
+            send(went, at, at, partner, g)
 
     def spread(scratch, dst):
         for zz in range(NZ):
@@ -196,12 +221,13 @@
 
     z8 = pl.ds(pl.multiple_of(z * 8, 8), 8)
 
-    def z_then_plane(zphase, pphase, s, rr, buf, start=True):
+    def z_then_plane(zphase, pphase, s, rr, buf, start=True, beside=lambda: None):
         def piece(zz):
             return pl.ds(pl.multiple_of(zz * 8, 8), 8)
 
         if start:
             z_send(zphase, lambda zz: s.at[piece(zz)], rr.at[z8])
+        beside()
         rr[z8, :] = s[z8, :]
         done(zphase, rr.at[0:56])
         for k in range(4):
@@ -229,6 +255,10 @@
     for zz in zpeers:
         for k in range(2):
             send(p.wq, qcols(zz, 2 * c + k), r.wq.at[z, :, half_cols(k)], at_z(zz))
+    weight_piece(0)
+    weight_piece(1)
+    send(p.xh, r.fhid, r.fhx.at[0], right, 0)
+    send(p.xh, r.fhid, r.fhx.at[1], left, 1)
     finish = z_then_plane(p.s1, p.s2, r.s1s, r.s1r, r.raw, False)
     xy_send(
         p.wo,
@@ -264,6 +294,8 @@
                 pl.ds(zz, 32, stride=8), :
             ].astype(BF)
     z_send(p.s3, lambda zz: r.s3s.at[zz], r.s3r.at[z])
+    weight_piece(2)
+    weight_piece(3)
     r.s3r[z] = r.s3s[z]
     done(p.s3, r.s3r.at[0:7])
     acc = r.s3r[0].astype(F32)
@@ -342,7 +374,13 @@
         r.osc[j * 32 : j * 32 + 32, :] = out.astype(BF).astype(F32)
 
     spread(r.osc, r.s5s)
-    finish = z_then_plane(p.s5, p.s6, r.s5s, r.s5r, r.att)
+
+    def beside():
+        weight_piece(4)
+        weight_piece(5)
+
+    finish = z_then_plane(p.s5, p.s6, r.s5s, r.s5r, r.att, beside=beside)
+    pass_weights(0)
     local.wo.wait()
     done(p.wo, r.wo.at[0:15])
     resid = r.raw[:, :, pl.ds(pl.multiple_of(x * 128, 128), 128)].reshape(256, 128).astype(F32)
@@ -352,45 +390,72 @@
     prod = jnp.dot(
         r.att[...].reshape(256, 512), r.wo[...].reshape(512, 256), preferred_element_type=F32
     ) + jnp.concatenate([lo, hi], axis=1)
-    for xl in range(2):
+    for h in range(2):
         for ys in range(NY):
             for j in range(2):
-                at = [((m * 2 + xl) * 4 + ys) * 16 + j * 8 for m in range(2)]
-                r.s7s[xl * 4 + ys, j * 16 : j * 16 + 16, :] = jnp.concatenate(
+                at = [((m * 2 + h) * 4 + ys) * 16 + j * 8 for m in range(2)]
+                r.s7s[h * 4 + ys, j * 16 : j * 16 + 16, :] = jnp.concatenate(
                     [prod[a : a + 8] for a in at], axis=0
                 ).astype(BF)
     z_send(p.s7, lambda zz: r.s7s.at[zz], r.s7r.at[z])
+    weight_piece(6)
+    weight_piece(7)
     r.s7r[z] = r.s7s[z]
     done(p.s7, r.s7r.at[0:7])
     acc = r.s7r[0].astype(F32)
     for s in range(1, NZ):
         acc = acc + r.s7r[s].astype(F32)
 
-    def z32(zz):
-        return pl.ds(pl.multiple_of(zz * 32, 32), 32)
-
-    r.mid[n, z32(z), :] = acc.astype(BF)
-    z_send(p.s8, lambda zz: r.mid.at[n, z32(z)], r.mid.at[n, z32(z)])
-    r.accg[...] = jnp.zeros((256, FFD), F32)
-    r.accu[...] = jnp.zeros((256, FFD), F32)
-    r.ssq[...] = jnp.zeros((256, 128), F32)
-    for k in (local.fi, local.fh, local.fo, local.wg, local.wd):
+    z16 = pl.ds(pl.multiple_of(z * 16, 16), 16)
+    for j in range(2):
+        r.mc[j, z16, :] = acc[j * 16 : j * 16 + 16].astype(BF)
+    z_send(p.s8, lambda zz: r.mc.at[:, z16], r.mc.at[:, z16])
+    r.accg[...] = jnp.zeros((128, 256), F32)
+    r.accu[...] = jnp.zeros((128, 256), F32)
+    r.ssq[...] = jnp.zeros((128, 128), F32)
+    for a in (FFD, 128 + FFD):
+        r.wg[:, a : a + 16, :] = jnp.zeros((2, 16, D), BF)
+        r.wd[a : a + 16, :] = jnp.zeros((16, D), BF)
+    recv(p.xh, r.fhx.at[0], 0)
+    recv(p.xh, r.fhx.at[1], 1)
+    sent(p.xh, r.fhx)
+    local.fh.wait()
+    r.fhp[...] = jnp.zeros((3, 2, 256), F32)
+    r.fhp[:, :, 0:FFD] = r.fh[...]
+    lane_h = lax.broadcasted_iota(jnp.int32, (3, 2, FFD), 2)
+    r.fhp[:, :, 128 : 128 + FFD] = jnp.where(lane_h < 64, r.fhx[0], r.fhx[1])
+    pass_weights(1)
+    mine_g = r.wg.at[:, 128 : 128 + FFD, 0:HALF]
+    mine_d = r.wd.at[128 : 128 + FFD, 0:HALF]
+    for k in (p.xg, p.fg):
+        sent(k, mine_g)
+    for k in (p.xd, p.fd):
+        sent(k, mine_d)
+    for k in (local.fi, local.fo, local.wg, local.wd):
         k.wait()
-    done(p.s8, r.mid.at[n, 0:224])
+    done(p.s8, r.mc.at[:, 0:112])
 
     near = (1, 3, 2)
+    top, low = pl.ds(0, 64), pl.ds(64, 64)
     for d in (2, 1, 3):
         xx, yy = rem(x + d, NX), rem(y + d, NY)
-        send(p.da, r.mid.at[n], r.mid.at[n], at_xy(xx, y), 3 - d)
-        send(p.da, r.mid.at[n], r.mid.at[n], at_xy(x, yy), 6 - d)
+        send(p.da, r.mc.at[rem(xx, 2)], r.mid.at[n], at_xy(xx, y), 3 - d)
+        send(p.da, r.mc.at[par], r.mid.at[n], at_xy(x, yy), 6 - d)
+        send(p.db, r.mc.at[1 - par, low], r.xb.at[y], at_xy(x, yy), 3 - d)
     sent(p.da, r.mid.at[0:6])
+    sent(p.db, r.xb.at[0:3])
+    r.mid[n] = r.mc[par]
+    for g in range(2):
+        cols = pl.ds(pl.multiple_of((1 - c) * HALF + g * 1024, 1024), 1024)
+        recv(p.fg, r.wg.at[:, 128 : 128 + FFD, cols], g)
+        recv(p.fd, r.wd.at[128 : 128 + FFD, cols], g)
 
     def ffn_chunk(m):
         v = r.mid[m].astype(F32)
         r.ssq[...] += v[:, :128] * v[:, :128] + v[:, 128:] * v[:, 128:]
         cols = pl.ds(pl.multiple_of(m * 256, 256), 256)
         g = r.gn[1:2, cols]
-        v4 = v.reshape(16, 2, 8, 256)
+        v4 = v.reshape(8, 2, 8, 256)
         for k, total in enumerate((r.accg, r.accu)):
             f = jnp.concatenate(
                 [
@@ -399,24 +464,26 @@
                 ],
                 axis=1,
             )
-            act = (v4 * f).reshape(256, 256).astype(BF)
+            act = (v4 * f).reshape(128, 256).astype(BF)
             total[...] += lax.dot_general(
                 act, r.wg[k, :, cols], NT, preferred_element_type=F32
             )
 
     ffn_chunk(n)
-    top, low = pl.ds(0, 128), pl.ds(128, 128)
     for d in near:
         m = rem(x + d, NX) * 4 + y
         recv(p.da, r.mid.at[m], d - 1)
         for e in (2, 1, 3):
             yy = rem(y + e, NY)
             send(p.dg, r.mid.at[m, top], r.mid.at[m, top], at_xy(x, yy), (d - 1) * 3 + 3 - e)
-        m = x * 4 + rem(y + d, NY)
+        yy = rem(y + d, NY)
+        m = x * 4 + yy
         recv(p.da, r.mid.at[m], d + 2)
+        recv(p.db, r.xb.at[yy], d - 1)
         for e in (2, 1, 3):
             xx = rem(x + e, NX)
-            send(p.dg, r.mid.at[m, low], r.mid.at[m, low], at_xy(xx, y), (3 - e) * 3 + d - 1)
+            at = r.mid.at[m, low] if e == 2 else r.xb.at[yy]
+            send(p.dg, at, r.mid.at[m, low], at_xy(xx, y), (3 - e) * 3 + d - 1)
     sent(p.dg, r.mid.at[0:9])
 
     def line_step(i, carry):
@@ -437,13 +504,13 @@
 
     def by_member(k):
         return jnp.concatenate(
-            [r.fh[k, i : i + 1, :].reshape(1, 1, 1, FFD) for i in range(2)], axis=1
+            [r.fhp[k, i : i + 1, :].reshape(1, 1, 1, 256) for i in range(2)], axis=1
         )
 
-    gate = (r.accg[...] * scale).reshape(16, 2, 8, FFD) * by_member(0)
-    up = (r.accu[...] * scale).reshape(16, 2, 8, FFD) * by_member(1)
+    gate = (r.accg[...] * scale).reshape(8, 2, 8, 256) * by_member(0)
+    up = (r.accu[...] * scale).reshape(8, 2, 8, 256) * by_member(1)
     hidden = gate / (1.0 + jnp.exp(-gate)) * up * by_member(2)
-    r.hid[...] = hidden.reshape(256, FFD).astype(BF)
+    r.hid[...] = hidden.reshape(128, 256).astype(BF)
 
     def chunk(ch):
         return pl.ds(pl.multiple_of(ch * CW, CW), CW)
@@ -451,9 +518,11 @@
     def high(ch):
         return pl.ds(pl.multiple_of(HALF + ch * CW, CW), CW)
 
-    def a1(ch, xx):
-        at = r.p3.at[xx, :, :, chunk(ch)]
-        send(p.a1, at, r.r1a.at[x, :, :, chunk(ch)], at_xy(xx, y), ch)
+    other = 1 - xl
+    opposite = at_xy(rem(x + 2, NX), y)
+
+    def a1(ch):
+        send(p.a1, r.p3.at[other, :, :, chunk(ch)], r.r1a.at[:, :, chunk(ch)], opposite, ch)
 
     def b1(ch, yy):
         at = r.p3.at[:, yy, :, high(ch)]
@@ -462,9 +531,9 @@
     def down_step(ch, carry):
         for cols in (chunk(ch), high(ch)):
             v = jnp.dot(r.hid[...], r.wd[:, cols], preferred_element_type=F32)
-            r.p3[:, :, :, cols] = v.astype(BF).reshape(NX, NY, 16, CW)
+            r.p3[:, :, :, cols] = v.astype(BF).reshape(2, NY, 16, CW)
+        a1(ch)
         for d in (2, 1, 3):
-            a1(ch, rem(x + d, NX))
             b1(ch, rem(y + d, NY))
         return carry
 
@@ -473,14 +542,12 @@
     def a2(ch, yy):
         send(p.a2, r.s2a.at[yy, :, chunk(ch)], r.r2a.at[y, :, chunk(ch)], at_xy(x, yy))
 
-    def b2(ch, xx):
-        send(p.b2, r.s2b.at[xx, :, chunk(ch)], r.r2b.at[x, :, chunk(ch)], at_xy(xx, y))
+    def b2(ch):
+        send(p.b2, r.s2b.at[other, :, chunk(ch)], r.r2b.at[:, chunk(ch)], opposite)
 
     def second_step(ch, carry):
-        recv(p.a1, r.r1a.at[0:3, :, :, chunk(ch)], ch)
-        v = r.p3[x, :, :, chunk(ch)].astype(F32)
-        for d in near:
-            v = v + r.r1a[rem(x + d, NX), :, :, chunk(ch)].astype(F32)
+        recv(p.a1, r.r1a.at[:, :, chunk(ch)], ch)
+        v = r.p3[xl, :, :, chunk(ch)].astype(F32) + r.r1a[:, :, chunk(ch)].astype(F32)
         r.s2a[:, :, chunk(ch)] = v.astype(BF)
         for d in (2, 1, 3):
             a2(ch, rem(y + d, NY))
@@ -489,27 +556,26 @@
         for d in near:
             v = v + r.r1b[rem(y + d, NY), :, :, chunk(ch)].astype(F32)
         r.s2b[:, :, chunk(ch)] = v.astype(BF)
-        for d in (2, 1, 3):
-            b2(ch, rem(x + d, NX))
+        b2(ch)
         return carry
 
     lax.fori_loop(0, NCH, second_step, 0)
-    sent(p.a1, r.r1a.at[0:3])
+    sent(p.a1, r.r1a)
     sent(p.b1, r.r1b.at[0:3])
     done(p.a2, r.r2a.at[0:3])
-    done(p.b2, r.r2b.at[0:3])
+    done(p.b2, r.r2b)
 
     row16 = lax.broadcasted_iota(jnp.int32, (16, 128), 0)
     own_row = rem(row16, 8) == z
-    tile16 = pl.ds(pl.multiple_of(n * 16, 16), 16)
+    tile16 = pl.ds(pl.multiple_of((xl * 4 + y) * 16, 16), 16)
     for b in range(32):
-        own, got, me, count = (
-            (r.s2a, r.r2a, y, NY) if b < 16 else (r.s2b, r.r2b, x, NX)
-        )
         cols = slice((b % 16) * 128, (b % 16 + 1) * 128)
-        v = own[me, :, cols].astype(F32)
-        for d in near:
-            v = v + got[rem(me + d, count), :, cols].astype(F32)
+        if b < 16:
+            v = r.s2a[y, :, cols].astype(F32)
+            for d in near:
+                v = v + r.r2a[rem(y + d, NY), :, cols].astype(F32)
+        else:
+            v = r.s2b[xl, :, cols].astype(F32) + r.r2b[:, cols].astype(F32)
         at = slice(b * 128, (b + 1) * 128)
         v = v * jnp.where(row16 < 8, r.fo[0:1, at], r.fo[1:2, at])
         m = r.mid[b // 2, tile16, (b % 2) * 128 : (b % 2 + 1) * 128].astype(F32)
@@ -538,19 +604,19 @@
 
     send(p.fx, r.fs.at[half(1 - c)], r.fr, partner)
     done(p.fx, r.fr)
-    r.fb[n, z] = ((r.fs[half(c), :] + r.fr[...]) * 0.25).astype(BF)
-    z_send(p.s14, lambda zz: r.fb.at[n, z], r.fb.at[n, z])
+    r.fb[own, z] = ((r.fs[half(c), :] + r.fr[...]) * 0.25).astype(BF)
+    z_send(p.s14, lambda zz: r.fb.at[own, z], r.fb.at[own, z])
     local.lm.wait()
     local.tg.wait()
     wanted = jnp.broadcast_to(r.tg[...].astype(F32), (B, B)).T[:, 0:1]
-    done(p.s14, r.fb.at[n, 0:7])
-    xy_send(p.s15, lambda m: r.fb.at[n], r.fb.at[n])
+    done(p.s14, r.fb.at[own, 0:7])
+    xy_send(p.s15, lambda m: r.fb.at[own], r.fb.at[own])
     done(p.s15, r.fb.at[0:15])
     r.ff[...] = r.fb[...].reshape(2048, 128).astype(F32)
     for b in range(16):
         rows = [
-            r.ff[pl.ds(xl * 1024 + zz * 16 + b, 8, stride=128), :]
-            for xl in range(2)
+            r.ff[pl.ds(h * 1024 + zz * 16 + b, 8, stride=128), :]
+            for h in range(2)
             for zz in range(NZ)
         ]
         r.lh[:, b * 128 : (b + 1) * 128] = jnp.concatenate(rows, axis=0).astype(BF)

time: 120 us -> 114 us (0.950)
  Pallas kernels: 115 us -> 109 us
    pallas_call x1, Pallas kernels: 115 us -> 109 us  [body(): pl.pallas_call(functools.partial(kernel, list(args)), out_shape=list(OUTS...]
where the time goes in v4:
time: 114 us; the launch traced here: 113 us
  Pallas kernels  109 us (96%)
  local copies, waits for them, and re-layouts  2.74 us (2%)
    pallas_call x1, Pallas kernels, body(): pl.pallas_call(functools.partial(kernel, list(args)), out_shape=list(OUTS...  109 us
    unnamed x2, local copies, waits for them, and re-layouts  2.74 us

profile of v4, /device:TPU:32, one launch (start us, length us, event | category | flops | bytes accessed | tf_op | source)
XLA Modules:
  0.0 112.6 jit_solution(5562667452788349223)
XLA Ops:
  0.6 109.2 %step.1 = (bf16[128,512]{1,0:T(8,128)(2,1)}, f32[1,128]{1,0:T(1,128)}) custom-call(bf16[2,4096]{1,0:T(2,128)(2,1)} %refs_0_.1, bf16[2,512,2048]{2,1,0:T(8,128)(2,1)} %refs_1_.1, s32[128]{0:T(128)} %refs_2_.1, s32[1,128]{1,0:T(1,128)} %bitcast.8, f32[3,4096]{1,0:T(4,128)} %refs_4_.1, bf16[48,4096]{1,0:T(8,128)(2,1)} %bitcast.6, bf16[32,4096]{1,0:T(8,128)(2,1)} %refs_6_.1, ...), custom_call_target="tpu_custom_call" | custom-call | tf_op jit(solution)/shard_map/step/pallas_call | solution.py:674
  109.8 1.6 %copy.18 = bf16[128,512]{1,0:T(8,128)(2,1)} copy(bf16[128,512]{1,0:T(8,128)(2,1)} %get-tuple-element.8) | data formatting | bytes 262144
  111.4 1.2 %copy.19 = f32[128]{0:T(128)} copy(f32[128]{0:T(128)} %bitcast.9) | data formatting | bytes 1024

commit v5 on v4

--- a/solution.py
+++ b/solution.py
@@ -40,6 +40,7 @@
     wg=VM((2, 256, D), BF),
     wd=VM((256, D), BF),
     fhx=VM((2, 3, 2, FFD), F32),
+    fhy=VM((2, 3, 2, FFD), F32),
     fhp=VM((3, 2, 256), F32),
     lm=VM((HALF, VD), BF),
     sc=VM((64, 128), F32),
@@ -89,7 +90,7 @@
 )
 PHASES = dict(
     wq=1, wqf=1, wo=1, s1=1, s2=1, s3=1, s4=1, s5=1, s6=1, s7=1, s8=1, da=6, db=3, dg=9,
-    xg=2, xd=2, fg=2, fd=2, xh=2,
+    xg=2, xd=2, fg=2, fd=2, xh=2, fi=1, fh=1, fo=1, fy=1,
     a1=NCH, b1=NCH, a2=1, b2=1, s13=1, fx=1, s14=1, s15=1, lx=1, s16=1, s17=1,
 )
 LS = dict(ls=DMA((16,)))
@@ -120,6 +121,9 @@
 
     partner = (1 - c, x, z, y)
 
+    def across_z(zz):
+        return (1 - c, x, zz, y)
+
     def copy(phase, src, dst, dev, slot=0):
         return pltpu.make_async_remote_copy(
             src_ref=src,
@@ -164,7 +168,8 @@
         sent(phase, ref)
 
     bar = pltpu.get_barrier_semaphore()
-    peers = [at_z(zz) for zz in zpeers] + [at_xy(*p) for p in plane] + [partner]
+    peers = [at_z(zz) for zz in zpeers] + [at_xy(*k) for k in plane] + [partner]
+    peers += [across_z(zz) for zz in zpeers]
     for dev in peers:
         pl.semaphore_signal(bar, inc=1, device_id=dev, device_id_type=MESH)
 
@@ -189,9 +194,6 @@
     local_wq = [fetch(qcols(z, 2 * c + k), r.wq.at[z, :, half_cols(k)]) for k in range(2)]
     local.wo = fetch(r.wout.at[:, pl.ds(pl.multiple_of(n * 256, 256), 256)], r.wo.at[n])
     local.kvv = fetch(r.kv, r.kvv)
-    local.fi = fetch(r.fin, r.fi)
-    local.fh = fetch(r.fhid, r.fh)
-    local.fo = fetch(r.fout, r.fo)
     local.tg = fetch(r.targets, r.tg)
     local.wg = fetch(r.wgu, r.wg.at[:, 0:FFD])
     local.wd = fetch(r.wdown, r.wd.at[0:FFD])
@@ -257,6 +259,9 @@
             send(p.wq, qcols(zz, 2 * c + k), r.wq.at[z, :, half_cols(k)], at_z(zz))
     weight_piece(0)
     weight_piece(1)
+    send(p.fi, r.fin, r.fi, partner)
+    send(p.fh, r.fhid, r.fh, partner)
+    send(p.fo, r.fout, r.fo, partner)
     send(p.xh, r.fhid, r.fhx.at[0], right, 0)
     send(p.xh, r.fhid, r.fhx.at[1], left, 1)
     finish = z_then_plane(p.s1, p.s2, r.s1s, r.s1r, r.raw, False)
@@ -397,11 +402,16 @@
                 r.s7s[h * 4 + ys, j * 16 : j * 16 + 16, :] = jnp.concatenate(
                     [prod[a : a + 8] for a in at], axis=0
                 ).astype(BF)
-    z_send(p.s7, lambda zz: r.s7s.at[zz], r.s7r.at[z])
+    for zz in zpeers:
+        send(p.s7, r.s7s.at[zz], r.s7r.at[z], across_z(zz))
+    send(p.s7, r.s7s.at[z], r.s7r.at[z], partner)
     weight_piece(6)
     weight_piece(7)
-    r.s7r[z] = r.s7s[z]
-    done(p.s7, r.s7r.at[0:7])
+    recv(p.xh, r.fhx.at[0], 0)
+    recv(p.xh, r.fhx.at[1], 1)
+    sent(p.xh, r.fhx)
+    send(p.fy, r.fhx, r.fhy, partner)
+    done(p.s7, r.s7r)
     acc = r.s7r[0].astype(F32)
     for s in range(1, NZ):
         acc = acc + r.s7r[s].astype(F32)
@@ -416,14 +426,14 @@
     for a in (FFD, 128 + FFD):
         r.wg[:, a : a + 16, :] = jnp.zeros((2, 16, D), BF)
         r.wd[a : a + 16, :] = jnp.zeros((16, D), BF)
-    recv(p.xh, r.fhx.at[0], 0)
-    recv(p.xh, r.fhx.at[1], 1)
-    sent(p.xh, r.fhx)
-    local.fh.wait()
+    done(p.fi, r.fi)
+    done(p.fh, r.fh)
+    done(p.fo, r.fo)
+    done(p.fy, r.fhy)
     r.fhp[...] = jnp.zeros((3, 2, 256), F32)
     r.fhp[:, :, 0:FFD] = r.fh[...]
     lane_h = lax.broadcasted_iota(jnp.int32, (3, 2, FFD), 2)
-    r.fhp[:, :, 128 : 128 + FFD] = jnp.where(lane_h < 64, r.fhx[0], r.fhx[1])
+    r.fhp[:, :, 128 : 128 + FFD] = jnp.where(lane_h < 64, r.fhy[0], r.fhy[1])
     pass_weights(1)
     mine_g = r.wg.at[:, 128 : 128 + FFD, 0:HALF]
     mine_d = r.wd.at[128 : 128 + FFD, 0:HALF]
@@ -431,7 +441,7 @@
         sent(k, mine_g)
     for k in (p.xd, p.fd):
         sent(k, mine_d)
-    for k in (local.fi, local.fo, local.wg, local.wd):
+    for k in (local.wg, local.wd):
         k.wait()
     done(p.s8, r.mc.at[:, 0:112])
 
@@ -657,6 +667,11 @@
 
     for sem, ref in drains:
         wait_bytes(sem, ref)
+
+
+def hand_on(logits, logprob, logits_o, logprob_o):
+    logits_o[...] = logits[...]
+    logprob_o[...] = logprob[...]
 
 
 def body(
@@ -689,6 +704,7 @@
         ),
         name="step",
     )(*args.values())
+    got = pl.pallas_call(hand_on, out_shape=list(OUTS.values()), name="result")(*got)
     return (got[0], got[1].reshape(B))
 
 

time: 114 us -> 112 us (0.982)
  local copies, waits for them, and re-layouts: 2.74 us -> 0 us
    unnamed x2 -> x0, local copies, waits for them, and re-layouts: 2.74 us -> none
    pallas_call x0 -> x1, Pallas kernels: none -> 1.57 us  [body(): pl.pallas_call(hand_on, out_shape=list(OUTS.values()), name='result')(*got)]
where the time goes in v5:
time: 112 us; the launch traced here: 111 us
  Pallas kernels  110 us (98%)
    pallas_call x1, Pallas kernels, body(): pl.pallas_call(functools.partial(kernel, list(args)), out_shape=list(OUTS...  109 us

profile of v5, /device:TPU:32, one launch (start us, length us, event | category | flops | bytes accessed | tf_op | source)
XLA Modules:
  0.0 110.9 jit_solution(14948316975839824457)
XLA Ops:
  0.6 108.7 %step.1 = (bf16[128,512]{1,0:T(8,128)(2,1)}, f32[1,128]{1,0:T(1,128)}) custom-call(bf16[2,4096]{1,0:T(2,128)(2,1)} %refs_0_.1, bf16[2,512,2048]{2,1,0:T(8,128)(2,1)} %refs_1_.1, s32[128]{0:T(128)} %refs_2_.1, s32[1,128]{1,0:T(1,128)} %bitcast.8, f32[3,4096]{1,0:T(4,128)} %refs_4_.1, bf16[48,4096]{1,0:T(8,128)(2,1)} %bitcast.6, bf16[32,4096]{1,0:T(8,128)(2,1)} %refs_6_.1, ...), custom_call_target="tpu_custom_call" | custom-call | tf_op jit(solution)/shard_map/step/pallas_call | solution.py:689
  109.3 1.6 %result.1 = (bf16[128,512]{1,0:T(8,128)(2,1)}, f32[1,128]{1,0:T(1,128)}) custom-call(bf16[128,512]{1,0:T(8,128)(2,1)} %get-tuple-element.6.logits, f32[1,128]{1,0:T(1,128)} %get-tuple-element.7.logprob), custom_call_target="tpu_custom_call" | custom-call | tf_op jit(solution)/shard_map/result/pallas_call | solution.py:707

commit v6 on v5

--- a/solution.py
+++ b/solution.py
@@ -61,7 +61,7 @@
     s7s=VM((NZ, 32, 256), BF),
     s7r=VM((NZ, 32, 256), BF),
     mc=VM((2, 128, 256), BF),
-    xb=VM((NY, 64, 256), BF),
+    xb=VM((NY, 128, 128), BF),
     mid=VM((NP, 128, 256), BF),
     accg=VM((128, 256), F32),
     accu=VM((128, 256), F32),
@@ -76,8 +76,9 @@
     r2b=VM((16, HALF), BF),
     f3=VM((512, 128), F32),
     g3=VM((32, 128), F32),
-    s13s=VM((NZ, 64, 128), BF),
-    s13r=VM((NZ, 64, 128), BF),
+    s13s=VM((NZ, NCH, 16, 128), BF),
+    s13r=VM((NZ, NCH, 16, 128), BF),
+    vs=VM((64, 128), F32),
     fs=VM((32, 128), F32),
     fr=VM((16, 128), F32),
     fb=VM((NP, NZ, 16, 128), BF),
@@ -89,9 +90,9 @@
     sx=VM((NP, 8, 128), F32),
 )
 PHASES = dict(
-    wq=1, wqf=1, wo=1, s1=1, s2=1, s3=1, s4=1, s5=1, s6=1, s7=1, s8=1, da=6, db=3, dg=9,
+    wq=1, wqf=1, wo=1, s1=1, s2=1, s3=1, s4=1, s5=1, s6=1, s7=1, s8=7, da=6, db=3, dg=9,
     xg=2, xd=2, fg=2, fd=2, xh=2, fi=1, fh=1, fo=1, fy=1,
-    a1=NCH, b1=NCH, a2=1, b2=1, s13=1, fx=1, s14=1, s15=1, lx=1, s16=1, s17=1,
+    a1=NCH, b1=NCH, a2=NCH, b2=NCH, s13=NCH, fx=1, s14=1, s15=1, lx=2, s16=1, s17=1,
 )
 LS = dict(ls=DMA((16,)))
 OUTS = dict(
@@ -265,11 +266,6 @@
     send(p.xh, r.fhid, r.fhx.at[0], right, 0)
     send(p.xh, r.fhid, r.fhx.at[1], left, 1)
     finish = z_then_plane(p.s1, p.s2, r.s1s, r.s1r, r.raw, False)
-    xy_send(
-        p.wo,
-        lambda m: r.wout.at[:, pl.ds(pl.multiple_of(m * 256, 256), 256)],
-        r.wo.at[n],
-    )
     local.fq.wait()
     local.gn.wait()
     pos = [r.lengths[rem(2 * t + j, B)] for j in range(2)]
@@ -299,6 +295,11 @@
                 pl.ds(zz, 32, stride=8), :
             ].astype(BF)
     z_send(p.s3, lambda zz: r.s3s.at[zz], r.s3r.at[z])
+    xy_send(
+        p.wo,
+        lambda m: r.wout.at[:, pl.ds(pl.multiple_of(m * 256, 256), 256)],
+        r.wo.at[n],
+    )
     weight_piece(2)
     weight_piece(3)
     r.s3r[z] = r.s3s[z]
@@ -419,7 +420,20 @@
     z16 = pl.ds(pl.multiple_of(z * 16, 16), 16)
     for j in range(2):
         r.mc[j, z16, :] = acc[j * 16 : j * 16 + 16].astype(BF)
-    z_send(p.s8, lambda zz: r.mc.at[:, z16], r.mc.at[:, z16])
+    for d in ZORDER:
+        send(p.s8, r.mc.at[:, z16], r.mc.at[:, z16], at_z(rem(z + d, NZ)), 7 - d)
+
+    def tile_on(zz):
+        rows = pl.ds(pl.multiple_of(zz * 16, 16), 16)
+        for d in (2, 1, 3):
+            xx, yy = rem(x + d, NX), rem(y + d, NY)
+            send(p.da, r.mc.at[par, rows], r.mid.at[n, rows], at_xy(x, yy), 6 - d)
+            send(p.da, r.mc.at[rem(xx, 2), rows], r.mid.at[n, rows], at_xy(xx, y), 3 - d)
+            send(p.db, r.mc.at[1 - par, rows, right_cols], r.xb.at[y, rows], at_xy(x, yy), 3 - d)
+
+    left_cols, right_cols = pl.ds(0, 128), pl.ds(128, 128)
+    tile_on(z)
+    pass_weights(1)
     r.accg[...] = jnp.zeros((128, 256), F32)
     r.accu[...] = jnp.zeros((128, 256), F32)
     r.ssq[...] = jnp.zeros((128, 128), F32)
@@ -434,7 +448,6 @@
     r.fhp[:, :, 0:FFD] = r.fh[...]
     lane_h = lax.broadcasted_iota(jnp.int32, (3, 2, FFD), 2)
     r.fhp[:, :, 128 : 128 + FFD] = jnp.where(lane_h < 64, r.fhy[0], r.fhy[1])
-    pass_weights(1)
     mine_g = r.wg.at[:, 128 : 128 + FFD, 0:HALF]
     mine_d = r.wd.at[128 : 128 + FFD, 0:HALF]
     for k in (p.xg, p.fg):
@@ -443,15 +456,12 @@
         sent(k, mine_d)
     for k in (local.wg, local.wd):
         k.wait()
-    done(p.s8, r.mc.at[:, 0:112])
+    for d in (1, 7, 2, 6, 3, 5, 4):
+        recv(p.s8, r.mc.at[:, 0:16], d - 1)
+        tile_on(rem(z + d, NZ))
+    sent(p.s8, r.mc.at[:, 0:112])
 
     near = (1, 3, 2)
-    top, low = pl.ds(0, 64), pl.ds(64, 64)
-    for d in (2, 1, 3):
-        xx, yy = rem(x + d, NX), rem(y + d, NY)
-        send(p.da, r.mc.at[rem(xx, 2)], r.mid.at[n], at_xy(xx, y), 3 - d)
-        send(p.da, r.mc.at[par], r.mid.at[n], at_xy(x, yy), 6 - d)
-        send(p.db, r.mc.at[1 - par, low], r.xb.at[y], at_xy(x, yy), 3 - d)
     sent(p.da, r.mid.at[0:6])
     sent(p.db, r.xb.at[0:3])
     r.mid[n] = r.mc[par]
@@ -485,15 +495,17 @@
         recv(p.da, r.mid.at[m], d - 1)
         for e in (2, 1, 3):
             yy = rem(y + e, NY)
-            send(p.dg, r.mid.at[m, top], r.mid.at[m, top], at_xy(x, yy), (d - 1) * 3 + 3 - e)
+            at = r.mid.at[m, :, left_cols]
+            send(p.dg, at, at, at_xy(x, yy), (d - 1) * 3 + 3 - e)
         yy = rem(y + d, NY)
         m = x * 4 + yy
         recv(p.da, r.mid.at[m], d + 2)
         recv(p.db, r.xb.at[yy], d - 1)
         for e in (2, 1, 3):
             xx = rem(x + e, NX)
-            at = r.mid.at[m, low] if e == 2 else r.xb.at[yy]
-            send(p.dg, at, r.mid.at[m, low], at_xy(xx, y), (3 - e) * 3 + d - 1)
+            to = r.mid.at[m, :, right_cols]
+            at = to if e == 2 else r.xb.at[yy]
+            send(p.dg, at, to, at_xy(xx, y), (3 - e) * 3 + d - 1)
     sent(p.dg, r.mid.at[0:9])
 
     def line_step(i, carry):
@@ -550,10 +562,10 @@
     lax.fori_loop(0, NCH, down_step, 0)
 
     def a2(ch, yy):
-        send(p.a2, r.s2a.at[yy, :, chunk(ch)], r.r2a.at[y, :, chunk(ch)], at_xy(x, yy))
+        send(p.a2, r.s2a.at[yy, :, chunk(ch)], r.r2a.at[y, :, chunk(ch)], at_xy(x, yy), ch)
 
     def b2(ch):
-        send(p.b2, r.s2b.at[other, :, chunk(ch)], r.r2b.at[:, chunk(ch)], opposite)
+        send(p.b2, r.s2b.at[other, :, chunk(ch)], r.r2b.at[:, chunk(ch)], opposite, ch)
 
     def second_step(ch, carry):
         recv(p.a1, r.r1a.at[:, :, chunk(ch)], ch)
@@ -572,38 +584,58 @@
     lax.fori_loop(0, NCH, second_step, 0)
     sent(p.a1, r.r1a)
     sent(p.b1, r.r1b.at[0:3])
-    done(p.a2, r.r2a.at[0:3])
-    done(p.b2, r.r2b)
+    sent(p.a2, r.r2a.at[0:3])
+    sent(p.b2, r.r2b)
 
     row16 = lax.broadcasted_iota(jnp.int32, (16, 128), 0)
     own_row = rem(row16, 8) == z
     tile16 = pl.ds(pl.multiple_of((xl * 4 + y) * 16, 16), 16)
-    for b in range(32):
-        cols = slice((b % 16) * 128, (b % 16 + 1) * 128)
-        if b < 16:
-            v = r.s2a[y, :, cols].astype(F32)
-            for d in near:
-                v = v + r.r2a[rem(y + d, NY), :, cols].astype(F32)
-        else:
-            v = r.s2b[xl, :, cols].astype(F32) + r.r2b[:, cols].astype(F32)
-        at = slice(b * 128, (b + 1) * 128)
-        v = v * jnp.where(row16 < 8, r.fo[0:1, at], r.fo[1:2, at])
-        m = r.mid[b // 2, tile16, (b % 2) * 128 : (b % 2 + 1) * 128].astype(F32)
-        r.f3[b * 16 : (b + 1) * 16, :] = v + jnp.where(own_row, m, 0.0)
-
-    for zz in range(NZ):
+
+    def last_step(ch):
+        recv(p.a2, r.r2a.at[0:3, :, chunk(ch)], ch)
+        recv(p.b2, r.r2b.at[:, chunk(ch)], ch)
+        for b in [*range(ch * 4, ch * 4 + 4), *range(16 + ch * 4, 20 + ch * 4)]:
+            cols = slice((b % 16) * 128, (b % 16 + 1) * 128)
+            if b < 16:
+                v = r.s2a[y, :, cols].astype(F32)
+                for d in near:
+                    v = v + r.r2a[rem(y + d, NY), :, cols].astype(F32)
+            else:
+                v = r.s2b[xl, :, cols].astype(F32) + r.r2b[:, cols].astype(F32)
+            at = slice(b * 128, (b + 1) * 128)
+            v = v * jnp.where(row16 < 8, r.fo[0:1, at], r.fo[1:2, at])
+            m = r.mid[b // 2, tile16, (b % 2) * 128 : (b % 2 + 1) * 128].astype(F32)
+            r.f3[b * 16 : (b + 1) * 16, :] = v + jnp.where(own_row, m, 0.0)
+        for zz in range(NZ):
+            r.s13s[zz, ch] = chunk_rows(zz, ch).astype(BF)
+        for zz in zpeers:
+            send(p.s13, r.s13s.at[zz, ch], r.s13r.at[z, ch], at_z(zz), ch)
+
+    def chunk_rows(zz, ch):
+        return jnp.concatenate(
+            [
+                r.f3[pl.ds(h * 256 + ch * 64 + m * 8 + zz, 4, stride=16), :]
+                for m in range(2)
+                for h in range(2)
+            ],
+            axis=0,
+        )
+
+    for ch in range(NCH):
+        last_step(ch)
+    for ch in range(NCH):
+        v = chunk_rows(z, ch)
+        recv(p.s13, r.s13r.at[0:7, ch], ch)
+        for zz in zpeers:
+            v = v + r.s13r[zz, ch].astype(F32)
         for m in range(2):
-            r.s13s[zz, m * 32 : (m + 1) * 32, :] = r.f3[
-                pl.ds(m * 8 + zz, 32, stride=16), :
-            ].astype(BF)
-    z_send(p.s13, lambda zz: r.s13s.at[zz], r.s13r.at[z])
-    owned = [r.f3[pl.ds(m * 8 + z, 32, stride=16), :] for m in range(2)]
-    done(p.s13, r.s13r.at[0:7])
+            for h in range(2):
+                at = m * 32 + h * 16 + ch * 4
+                r.vs[at : at + 4, :] = v[m * 8 + h * 4 : m * 8 + h * 4 + 4]
+    sent(p.s13, r.s13r.at[0:7])
     both = jnp.zeros((32, 128), F32)
     for m in range(2):
-        v = owned[m]
-        for zz in zpeers:
-            v = v + r.s13r[zz, m * 32 : (m + 1) * 32, :].astype(F32)
+        v = r.vs[m * 32 : m * 32 + 32, :]
         v = v.astype(BF).astype(F32)
         mean = jnp.sum(jnp.sum(v * v, axis=1, keepdims=True), axis=0, keepdims=True) * (1.0 / D)
         both = both + (v * lax.rsqrt(mean + 1e-5) * r.g3[...]).astype(BF).astype(F32)
@@ -630,9 +662,13 @@
             for zz in range(NZ)
         ]
         r.lh[:, b * 128 : (b + 1) * 128] = jnp.concatenate(rows, axis=0).astype(BF)
-    r.lp[...] = jnp.dot(r.lh[...], r.lm[...], preferred_element_type=F32)
-    send(p.lx, r.lp, r.lr, partner)
-    done(p.lx, r.lr)
+    for h in range(2):
+        at = slice(h * 256, (h + 1) * 256)
+        r.lp[:, at] = jnp.dot(r.lh[...], r.lm[:, at], preferred_element_type=F32)
+        send(p.lx, r.lp.at[:, at], r.lr.at[:, at], partner, h)
+    for h in range(2):
+        recv(p.lx, r.lr.at[:, h * 256 : (h + 1) * 256], h)
+    sent(p.lx, r.lr)
     mean_f = r.lp[...] + r.lr[...]
     r.logits_o[...] = mean_f.astype(BF)
 

time: 112 us -> 110 us (0.982)
  Pallas kernels: 110 us -> 108 us
    pallas_call x1, Pallas kernels: 109 us -> 107 us  [body(): pl.pallas_call(functools.partial(kernel, list(args)), out_shape=list(OUTS...]
where the time goes in v6:
time: 110 us; the launch traced here: 109 us
  Pallas kernels  108 us (98%)
    pallas_call x1, Pallas kernels, body(): pl.pallas_call(functools.partial(kernel, list(args)), out_shape=list(OUTS...  107 us

profile of v6, /device:TPU:32, one launch (start us, length us, event | category | flops | bytes accessed | tf_op | source)
XLA Modules:
  0.0 109.1 jit_solution(2366256213440285350)
XLA Ops:
  0.6 106.9 %step.1 = (bf16[128,512]{1,0:T(8,128)(2,1)}, f32[1,128]{1,0:T(1,128)}) custom-call(bf16[2,4096]{1,0:T(2,128)(2,1)} %refs_0_.1, bf16[2,512,2048]{2,1,0:T(8,128)(2,1)} %refs_1_.1, s32[128]{0:T(128)} %refs_2_.1, s32[1,128]{1,0:T(1,128)} %bitcast.8, f32[3,4096]{1,0:T(4,128)} %refs_4_.1, bf16[48,4096]{1,0:T(8,128)(2,1)} %bitcast.6, bf16[32,4096]{1,0:T(8,128)(2,1)} %refs_6_.1, ...), custom_call_target="tpu_custom_call" | custom-call | tf_op jit(solution)/shard_map/step/pallas_call | solution.py:725
  107.6 1.6 %result.1 = (bf16[128,512]{1,0:T(8,128)(2,1)}, f32[1,128]{1,0:T(1,128)}) custom-call(bf16[128,512]{1,0:T(8,128)(2,1)} %get-tuple-element.6.logits, f32[1,128]{1,0:T(1,128)} %get-tuple-element.7.logprob), custom_call_target="tpu_custom_call" | custom-call | tf_op jit(solution)/shard_map/result/pallas_call | solution.py:743

commit v7 on v6

--- a/solution.py
+++ b/solution.py
@@ -19,7 +19,9 @@
 B = 128
 QN = 384
 ZORDER = (4, 3, 5, 2, 6, 1, 7)
-NCH, CW = 4, 512
+NCH, CA, CB = 4, 640, 384
+WA, WB = NCH * CA, NCH * CB
+BA, BB = CA // 128, CB // 128
 HALF = D // 2
 NT = (((1,), (1,)), ((), ()))
 
@@ -68,12 +70,12 @@
     ssq=VM((128, 128), F32),
     hid=VM((128, 256), BF),
     p3=VM((2, NY, 16, D), BF),
-    r1a=VM((NY, 16, HALF), BF),
-    r1b=VM((NY, 2, 16, HALF), BF),
-    s2a=VM((NY, 16, HALF), BF),
-    s2b=VM((2, 16, HALF), BF),
-    r2a=VM((NY, 16, HALF), BF),
-    r2b=VM((16, HALF), BF),
+    r1a=VM((NY, 16, WA), BF),
+    r1b=VM((NY, 2, 16, WB), BF),
+    s2a=VM((NY, 16, WA), BF),
+    s2b=VM((2, 16, WB), BF),
+    r2a=VM((NY, 16, WA), BF),
+    r2b=VM((16, WB), BF),
     f3=VM((512, 128), F32),
     g3=VM((32, 128), F32),
     s13s=VM((NZ, NCH, 16, 128), BF),
@@ -92,7 +94,7 @@
 PHASES = dict(
     wq=1, wqf=1, wo=1, s1=1, s2=1, s3=1, s4=1, s5=1, s6=1, s7=1, s8=7, da=6, db=3, dg=9,
     xg=2, xd=2, fg=2, fd=2, xh=2, fi=1, fh=1, fo=1, fy=1,
-    a1=NCH, b1=NCH, a2=NCH, b2=NCH, s13=NCH, fx=1, s14=1, s15=1, lx=2, s16=1, s17=1,
+    a1=NCH, b1=NCH, a2=NCH, b2=NCH, s13=NCH, fx=1, s14=7, s15=1, lx=2, s16=1, s17=1,
 )
 LS = dict(ls=DMA((16,)))
 OUTS = dict(
@@ -295,11 +297,6 @@
                 pl.ds(zz, 32, stride=8), :
             ].astype(BF)
     z_send(p.s3, lambda zz: r.s3s.at[zz], r.s3r.at[z])
-    xy_send(
-        p.wo,
-        lambda m: r.wout.at[:, pl.ds(pl.multiple_of(m * 256, 256), 256)],
-        r.wo.at[n],
-    )
     weight_piece(2)
     weight_piece(3)
     r.s3r[z] = r.s3s[z]
@@ -317,6 +314,11 @@
         return pl.ds(pl.multiple_of(m * 8, 8), 8)
 
     xy_send(p.s4, lambda m: r.s4s.at[tile(m)], r.s4r.at[tile(n)])
+    xy_send(
+        p.wo,
+        lambda m: r.wout.at[:, pl.ds(pl.multiple_of(m * 256, 256), 256)],
+        r.wo.at[n],
+    )
     r.s4r[tile(n), :] = r.s4s[tile(n), :]
     done(p.s4, r.s4r.at[0:120])
 
@@ -535,10 +537,13 @@
     r.hid[...] = hidden.reshape(128, 256).astype(BF)
 
     def chunk(ch):
-        return pl.ds(pl.multiple_of(ch * CW, CW), CW)
+        return pl.ds(pl.multiple_of(ch * CA, CA), CA)
+
+    def chunk_b(ch):
+        return pl.ds(pl.multiple_of(ch * CB, CB), CB)
 
     def high(ch):
-        return pl.ds(pl.multiple_of(HALF + ch * CW, CW), CW)
+        return pl.ds(pl.multiple_of(WA + ch * CB, 128), CB)
 
     other = 1 - xl
     opposite = at_xy(rem(x + 2, NX), y)
@@ -548,12 +553,12 @@
 
     def b1(ch, yy):
         at = r.p3.at[:, yy, :, high(ch)]
-        send(p.b1, at, r.r1b.at[y, :, :, chunk(ch)], at_xy(x, yy), ch)
+        send(p.b1, at, r.r1b.at[y, :, :, chunk_b(ch)], at_xy(x, yy), ch)
 
     def down_step(ch, carry):
-        for cols in (chunk(ch), high(ch)):
+        for cols, width in ((chunk(ch), CA), (high(ch), CB)):
             v = jnp.dot(r.hid[...], r.wd[:, cols], preferred_element_type=F32)
-            r.p3[:, :, :, cols] = v.astype(BF).reshape(2, NY, 16, CW)
+            r.p3[:, :, :, cols] = v.astype(BF).reshape(2, NY, 16, width)
         a1(ch)
         for d in (2, 1, 3):
             b1(ch, rem(y + d, NY))
@@ -565,7 +570,7 @@
         send(p.a2, r.s2a.at[yy, :, chunk(ch)], r.r2a.at[y, :, chunk(ch)], at_xy(x, yy), ch)
 
     def b2(ch):
-        send(p.b2, r.s2b.at[other, :, chunk(ch)], r.r2b.at[:, chunk(ch)], opposite, ch)
+        send(p.b2, r.s2b.at[other, :, chunk_b(ch)], r.r2b.at[:, chunk_b(ch)], opposite, ch)
 
     def second_step(ch, carry):
         recv(p.a1, r.r1a.at[:, :, chunk(ch)], ch)
@@ -573,11 +578,11 @@
         r.s2a[:, :, chunk(ch)] = v.astype(BF)
         for d in (2, 1, 3):
             a2(ch, rem(y + d, NY))
-        recv(p.b1, r.r1b.at[0:3, :, :, chunk(ch)], ch)
+        recv(p.b1, r.r1b.at[0:3, :, :, chunk_b(ch)], ch)
         v = r.p3[:, y, :, high(ch)].astype(F32)
         for d in near:
-            v = v + r.r1b[rem(y + d, NY), :, :, chunk(ch)].astype(F32)
-        r.s2b[:, :, chunk(ch)] = v.astype(BF)
+            v = v + r.r1b[rem(y + d, NY), :, :, chunk_b(ch)].astype(F32)
+        r.s2b[:, :, chunk_b(ch)] = v.astype(BF)
         b2(ch)
         return carry
 
@@ -591,16 +596,20 @@
     own_row = rem(row16, 8) == z
     tile16 = pl.ds(pl.multiple_of((xl * 4 + y) * 16, 16), 16)
 
+    def parts(ch):
+        return (ch * BA, BA), (NCH * BA + ch * BB, BB)
+
     def last_step(ch):
         recv(p.a2, r.r2a.at[0:3, :, chunk(ch)], ch)
-        recv(p.b2, r.r2b.at[:, chunk(ch)], ch)
-        for b in [*range(ch * 4, ch * 4 + 4), *range(16 + ch * 4, 20 + ch * 4)]:
-            cols = slice((b % 16) * 128, (b % 16 + 1) * 128)
-            if b < 16:
+        recv(p.b2, r.r2b.at[:, chunk_b(ch)], ch)
+        for b in [b for start, length in parts(ch) for b in range(start, start + length)]:
+            if b < NCH * BA:
+                cols = slice(b * 128, (b + 1) * 128)
                 v = r.s2a[y, :, cols].astype(F32)
                 for d in near:
                     v = v + r.r2a[rem(y + d, NY), :, cols].astype(F32)
             else:
+                cols = slice((b - NCH * BA) * 128, (b - NCH * BA + 1) * 128)
                 v = r.s2b[xl, :, cols].astype(F32) + r.r2b[:, cols].astype(F32)
             at = slice(b * 128, (b + 1) * 128)
             v = v * jnp.where(row16 < 8, r.fo[0:1, at], r.fo[1:2, at])
@@ -614,9 +623,9 @@
     def chunk_rows(zz, ch):
         return jnp.concatenate(
             [
-                r.f3[pl.ds(h * 256 + ch * 64 + m * 8 + zz, 4, stride=16), :]
+                r.f3[pl.ds(start * 16 + m * 8 + zz, length, stride=16), :]
                 for m in range(2)
-                for h in range(2)
+                for start, length in parts(ch)
             ],
             axis=0,
         )
@@ -629,9 +638,11 @@
         for zz in zpeers:
             v = v + r.s13r[zz, ch].astype(F32)
         for m in range(2):
-            for h in range(2):
-                at = m * 32 + h * 16 + ch * 4
-                r.vs[at : at + 4, :] = v[m * 8 + h * 4 : m * 8 + h * 4 + 4]
+            row = m * 8
+            for start, length in parts(ch):
+                at = m * 32 + start
+                r.vs[at : at + length, :] = v[row : row + length]
+                row += length
     sent(p.s13, r.s13r.at[0:7])
     both = jnp.zeros((32, 128), F32)
     for m in range(2):
@@ -647,12 +658,17 @@
     send(p.fx, r.fs.at[half(1 - c)], r.fr, partner)
     done(p.fx, r.fr)
     r.fb[own, z] = ((r.fs[half(c), :] + r.fr[...]) * 0.25).astype(BF)
-    z_send(p.s14, lambda zz: r.fb.at[own, z], r.fb.at[own, z])
+    for d in ZORDER:
+        send(p.s14, r.fb.at[own, z], r.fb.at[own, z], at_z(rem(z + d, NZ)), 7 - d)
+    xy_send(p.s15, lambda m: r.fb.at[own, z], r.fb.at[own, z])
     local.lm.wait()
     local.tg.wait()
     wanted = jnp.broadcast_to(r.tg[...].astype(F32), (B, B)).T[:, 0:1]
-    done(p.s14, r.fb.at[own, 0:7])
-    xy_send(p.s15, lambda m: r.fb.at[own], r.fb.at[own])
+    for d in (1, 7, 2, 6, 3, 5, 4):
+        zz = rem(z + d, NZ)
+        recv(p.s14, r.fb.at[own, zz], d - 1)
+        xy_send(p.s15, lambda m: r.fb.at[own, zz], r.fb.at[own, zz])
+    sent(p.s14, r.fb.at[own, 0:7])
     done(p.s15, r.fb.at[0:15])
     r.ff[...] = r.fb[...].reshape(2048, 128).astype(F32)
     for b in range(16):
@@ -724,7 +740,7 @@
     )
     got = pl.pallas_call(
         functools.partial(kernel, list(args)),
-        out_shape=list(OUTS.values()),
+        out_shape=[VM(k.shape, k.dtype) for k in OUTS.values()],
         in_specs=[
             pl.BlockSpec(memory_space=pltpu.SMEM if v is lengths else pl.ANY)
             for v in args.values()
@@ -740,7 +756,13 @@
         ),
         name="step",
     )(*args.values())
-    got = pl.pallas_call(hand_on, out_shape=list(OUTS.values()), name="result")(*got)
+    got = [pltpu.with_memory_space_constraint(k, VM) for k in got]
+    got = pl.pallas_call(
+        hand_on,
+        out_shape=list(OUTS.values()),
+        in_specs=[pl.BlockSpec(memory_space=VM)] * 2,
+        name="result",
+    )(*got)
     return (got[0], got[1].reshape(B))
 
 

time: 110 us -> 109 us (level)
    pallas_call x2, Pallas kernels: 108 us -> 107 us  [the longest x1 107 us: body(): pl.pallas_call(functools.partial(kernel, list(args)), out_shape=[VM(k.sha...]
where the time goes in v7:
time: 109 us; the launch traced here: 108 us
  Pallas kernels  107 us (98%)
    pallas_call x1, Pallas kernels, body(): pl.pallas_call(functools.partial(kernel, list(args)), out_shape=[VM(k.sha...  107 us

profile of v7, /device:TPU:32, one launch (start us, length us, event | category | flops | bytes accessed | tf_op | source)
XLA Modules:
  0.0 107.8 jit_solution(14192600033406976131)
XLA Ops:
  0.6 106.5 %step.1 = (bf16[128,512]{1,0:T(8,128)(2,1)S(1)}, f32[1,128]{1,0:T(1,128)S(1)}) custom-call(bf16[2,4096]{1,0:T(2,128)(2,1)} %refs_0_.1, bf16[2,512,2048]{2,1,0:T(8,128)(2,1)} %refs_1_.1, s32[128]{0:T(128)} %refs_2_.1, s32[1,128]{1,0:T(1,128)} %bitcast.8, f32[3,4096]{1,0:T(4,128)} %refs_4_.1, bf16[48,4096]{1,0:T(8,128)(2,1)} %bitcast.6, ...), custom_call_target="tpu_custom_call" | custom-call | tf_op jit(solution)/shard_map/step/pallas_call | solution.py:741
  107.2 0.7 result.1

commit v8 on v7

--- a/solution.py
+++ b/solution.py
@@ -19,7 +19,8 @@
 B = 128
 QN = 384
 ZORDER = (4, 3, 5, 2, 6, 1, 7)
-NCH, CA, CB = 4, 640, 384
+NEAR_Z = (7, 0, 1)
+NCH, CA, CB = 4, 512, 512
 WA, WB = NCH * CA, NCH * CB
 BA, BB = CA // 128, CB // 128
 HALF = D // 2
@@ -69,7 +70,7 @@
     accu=VM((128, 256), F32),
     ssq=VM((128, 128), F32),
     hid=VM((128, 256), BF),
-    p3=VM((2, NY, 16, D), BF),
+    p3=VM((8, 16, D), BF),
     r1a=VM((NY, 16, WA), BF),
     r1b=VM((NY, 2, 16, WB), BF),
     s2a=VM((NY, 16, WA), BF),
@@ -92,9 +93,9 @@
     sx=VM((NP, 8, 128), F32),
 )
 PHASES = dict(
-    wq=1, wqf=1, wo=1, s1=1, s2=1, s3=1, s4=1, s5=1, s6=1, s7=1, s8=7, da=6, db=3, dg=9,
+    wq=1, wqf=1, wo=1, s1=1, s2=1, s3=1, s4=1, s5=1, s6=1, s7=1, s8=7, da=12, db=6, dg=9,
     xg=2, xd=2, fg=2, fd=2, xh=2, fi=1, fh=1, fo=1, fy=1,
-    a1=NCH, b1=NCH, a2=NCH, b2=NCH, s13=NCH, fx=1, s14=7, s15=1, lx=2, s16=1, s17=1,
+    a1=NCH, b1=NCH, a2=NCH, b2=NCH, s13=NCH, fx=1, s14=7, s15=8, lx=1, s16=1, s17=1,
 )
 LS = dict(ls=DMA((16,)))
 OUTS = dict(
@@ -162,9 +163,9 @@
         for zz in zpeers:
             send(phase, src_at(zz), dst, at_z(zz))
 
-    def xy_send(phase, src_at, dst):
+    def xy_send(phase, src_at, dst, slot=0):
         for xx, yy in plane:
-            send(phase, src_at(xx * 4 + yy), dst, at_xy(xx, yy))
+            send(phase, src_at(xx * 4 + yy), dst, at_xy(xx, yy), slot)
 
     def done(phase, ref):
         recv(phase, ref)
@@ -419,22 +420,28 @@
     for s in range(1, NZ):
         acc = acc + r.s7r[s].astype(F32)
 
-    z16 = pl.ds(pl.multiple_of(z * 16, 16), 16)
+    def tile_rows(d):
+        return pl.ds((d + 1) % NZ * 16, 16)
+
     for j in range(2):
-        r.mc[j, z16, :] = acc[j * 16 : j * 16 + 16].astype(BF)
+        r.mc[j, tile_rows(0), :] = acc[j * 16 : j * 16 + 16].astype(BF)
     for d in ZORDER:
-        send(p.s8, r.mc.at[:, z16], r.mc.at[:, z16], at_z(rem(z + d, NZ)), 7 - d)
-
-    def tile_on(zz):
-        rows = pl.ds(pl.multiple_of(zz * 16, 16), 16)
+        at = r.mc.at[:, tile_rows(0)]
+        send(p.s8, at, r.mc.at[:, tile_rows(-d)], at_z(rem(z + d, NZ)), 7 - d)
+
+    def tile_on(k):
+        rows = tile_rows(k)
+        late = 0 if k in NEAR_Z else 1
         for d in (2, 1, 3):
             xx, yy = rem(x + d, NX), rem(y + d, NY)
-            send(p.da, r.mc.at[par, rows], r.mid.at[n, rows], at_xy(x, yy), 6 - d)
-            send(p.da, r.mc.at[rem(xx, 2), rows], r.mid.at[n, rows], at_xy(xx, y), 3 - d)
-            send(p.db, r.mc.at[1 - par, rows, right_cols], r.xb.at[y, rows], at_xy(x, yy), 3 - d)
+            at = r.mid.at[n, rows]
+            send(p.da, r.mc.at[par, rows], at, at_xy(x, yy), 6 - d + 6 * late)
+            send(p.da, r.mc.at[rem(xx, 2), rows], at, at_xy(xx, y), 3 - d + 6 * late)
+            at = r.mc.at[1 - par, rows, right_cols]
+            send(p.db, at, r.xb.at[y, rows], at_xy(x, yy), 3 - d + 3 * late)
 
     left_cols, right_cols = pl.ds(0, 128), pl.ds(128, 128)
-    tile_on(z)
+    tile_on(0)
     pass_weights(1)
     r.accg[...] = jnp.zeros((128, 256), F32)
     r.accu[...] = jnp.zeros((128, 256), F32)
@@ -460,7 +467,7 @@
         k.wait()
     for d in (1, 7, 2, 6, 3, 5, 4):
         recv(p.s8, r.mc.at[:, 0:16], d - 1)
-        tile_on(rem(z + d, NZ))
+        tile_on(d)
     sent(p.s8, r.mc.at[:, 0:112])
 
     near = (1, 3, 2)
@@ -492,22 +499,23 @@
             )
 
     ffn_chunk(n)
-    for d in near:
-        m = rem(x + d, NX) * 4 + y
-        recv(p.da, r.mid.at[m], d - 1)
-        for e in (2, 1, 3):
-            yy = rem(y + e, NY)
-            at = r.mid.at[m, :, left_cols]
-            send(p.dg, at, at, at_xy(x, yy), (d - 1) * 3 + 3 - e)
-        yy = rem(y + d, NY)
-        m = x * 4 + yy
-        recv(p.da, r.mid.at[m], d + 2)
-        recv(p.db, r.xb.at[yy], d - 1)
-        for e in (2, 1, 3):
-            xx = rem(x + e, NX)
-            to = r.mid.at[m, :, right_cols]
-            at = to if e == 2 else r.xb.at[yy]
-            send(p.dg, at, to, at_xy(xx, y), (3 - e) * 3 + d - 1)
+    for late, rows in enumerate((pl.ds(0, 48), pl.ds(48, 80))):
+        for d in near:
+            m = rem(x + d, NX) * 4 + y
+            recv(p.da, r.mid.at[m, rows], d - 1 + 6 * late)
+            at = r.mid.at[m, rows, left_cols]
+            for e in (2, 1, 3):
+                yy = rem(y + e, NY)
+                send(p.dg, at, at, at_xy(x, yy), (d - 1) * 3 + 3 - e)
+            yy = rem(y + d, NY)
+            m = x * 4 + yy
+            recv(p.da, r.mid.at[m, rows], d + 2 + 6 * late)
+            recv(p.db, r.xb.at[yy, rows], d - 1 + 3 * late)
+            to = r.mid.at[m, rows, right_cols]
+            for e in (2, 1, 3):
+                xx = rem(x + e, NX)
+                at = to if e == 2 else r.xb.at[yy, rows]
+                send(p.dg, at, to, at_xy(xx, y), (3 - e) * 3 + d - 1)
     sent(p.dg, r.mid.at[0:9])
 
     def line_step(i, carry):
@@ -549,16 +557,18 @@
     opposite = at_xy(rem(x + 2, NX), y)
 
     def a1(ch):
-        send(p.a1, r.p3.at[other, :, :, chunk(ch)], r.r1a.at[:, :, chunk(ch)], opposite, ch)
+        send(p.a1, r.p3.at[pl.ds(other * 4, 4), :, chunk(ch)], r.r1a.at[:, :, chunk(ch)], opposite, ch)
 
     def b1(ch, yy):
-        at = r.p3.at[:, yy, :, high(ch)]
-        send(p.b1, at, r.r1b.at[y, :, :, chunk_b(ch)], at_xy(x, yy), ch)
+        for h in range(2):
+            at = r.p3.at[h * 4 + yy, :, high(ch)]
+            send(p.b1, at, r.r1b.at[y, h, :, chunk_b(ch)], at_xy(x, yy), ch)
 
     def down_step(ch, carry):
-        for cols, width in ((chunk(ch), CA), (high(ch), CB)):
+        for cols in (chunk(ch), high(ch)):
             v = jnp.dot(r.hid[...], r.wd[:, cols], preferred_element_type=F32)
-            r.p3[:, :, :, cols] = v.astype(BF).reshape(2, NY, 16, width)
+            for k in range(NZ):
+                r.p3[rem(z + k + NZ - 1, NZ), :, cols] = v[k * 16 : k * 16 + 16].astype(BF)
         a1(ch)
         for d in (2, 1, 3):
             b1(ch, rem(y + d, NY))
@@ -574,12 +584,14 @@
 
     def second_step(ch, carry):
         recv(p.a1, r.r1a.at[:, :, chunk(ch)], ch)
-        v = r.p3[xl, :, :, chunk(ch)].astype(F32) + r.r1a[:, :, chunk(ch)].astype(F32)
+        v = r.p3[pl.ds(xl * 4, 4), :, chunk(ch)].astype(F32) + r.r1a[:, :, chunk(ch)].astype(F32)
         r.s2a[:, :, chunk(ch)] = v.astype(BF)
         for d in (2, 1, 3):
             a2(ch, rem(y + d, NY))
         recv(p.b1, r.r1b.at[0:3, :, :, chunk_b(ch)], ch)
-        v = r.p3[:, y, :, high(ch)].astype(F32)
+        v = jnp.concatenate(
+            [r.p3[pl.ds(h * 4 + y, 1), :, high(ch)].astype(F32) for h in range(2)], axis=0
+        )
         for d in near:
             v = v + r.r1b[rem(y + d, NY), :, :, chunk_b(ch)].astype(F32)
         r.s2b[:, :, chunk_b(ch)] = v.astype(BF)
@@ -594,7 +606,7 @@
 
     row16 = lax.broadcasted_iota(jnp.int32, (16, 128), 0)
     own_row = rem(row16, 8) == z
-    tile16 = pl.ds(pl.multiple_of((xl * 4 + y) * 16, 16), 16)
+    tile16 = pl.ds(pl.multiple_of(rem(xl * 4 + y - z + NZ + 1, NZ) * 16, 16), 16)
 
     def parts(ch):
         return (ch * BA, BA), (NCH * BA + ch * BB, BB)
@@ -660,17 +672,22 @@
     r.fb[own, z] = ((r.fs[half(c), :] + r.fr[...]) * 0.25).astype(BF)
     for d in ZORDER:
         send(p.s14, r.fb.at[own, z], r.fb.at[own, z], at_z(rem(z + d, NZ)), 7 - d)
-    xy_send(p.s15, lambda m: r.fb.at[own, z], r.fb.at[own, z])
+    xy_send(p.s15, lambda m: r.fb.at[own, z], r.fb.at[own, z], 0)
     local.lm.wait()
     local.tg.wait()
     wanted = jnp.broadcast_to(r.tg[...].astype(F32), (B, B)).T[:, 0:1]
     for d in (1, 7, 2, 6, 3, 5, 4):
         zz = rem(z + d, NZ)
         recv(p.s14, r.fb.at[own, zz], d - 1)
-        xy_send(p.s15, lambda m: r.fb.at[own, zz], r.fb.at[own, zz])
+        xy_send(p.s15, lambda m: r.fb.at[own, zz], r.fb.at[own, zz], d)
     sent(p.s14, r.fb.at[own, 0:7])
-    done(p.s15, r.fb.at[0:15])
-    r.ff[...] = r.fb[...].reshape(2048, 128).astype(F32)
+    for d in (0, 1, 7, 2, 6, 3, 5, 4):
+        zz = rem(z + d, NZ)
+        recv(p.s15, r.fb.at[0:15, zz], d)
+        for k in range(NP):
+            at = pl.ds(pl.multiple_of(k * 128 + zz * 16, 16), 16)
+            r.ff[at, :] = r.fb[k, zz].astype(F32)
+    sent(p.s15, r.fb.at[0:15])
     for b in range(16):
         rows = [
             r.ff[pl.ds(h * 1024 + zz * 16 + b, 8, stride=128), :]
@@ -678,13 +695,9 @@
             for zz in range(NZ)
         ]
         r.lh[:, b * 128 : (b + 1) * 128] = jnp.concatenate(rows, axis=0).astype(BF)
-    for h in range(2):
-        at = slice(h * 256, (h + 1) * 256)
-        r.lp[:, at] = jnp.dot(r.lh[...], r.lm[:, at], preferred_element_type=F32)
-        send(p.lx, r.lp.at[:, at], r.lr.at[:, at], partner, h)
-    for h in range(2):
-        recv(p.lx, r.lr.at[:, h * 256 : (h + 1) * 256], h)
-    sent(p.lx, r.lr)
+    r.lp[...] = jnp.dot(r.lh[...], r.lm[...], preferred_element_type=F32)
+    send(p.lx, r.lp, r.lr, partner)
+    done(p.lx, r.lr)
     mean_f = r.lp[...] + r.lr[...]
     r.logits_o[...] = mean_f.astype(BF)
 

time: 109 us -> 106 us (0.972)
  Pallas kernels: 107 us -> 104 us
    pallas_call x1, Pallas kernels: 107 us -> 103 us  [body(): pl.pallas_call(functools.partial(kernel, list(args)), out_shape=[VM(k.sha...]
where the time goes in v8:
time: 106 us; the launch traced here: 104 us
  Pallas kernels  104 us (98%)
    pallas_call x1, Pallas kernels, body(): pl.pallas_call(functools.partial(kernel, list(args)), out_shape=[VM(k.sha...  103 us

profile of v8, /device:TPU:32, one launch (start us, length us, event | category | flops | bytes accessed | tf_op | source)
XLA Modules:
  0.0 104.4 jit_solution(12472884024269002492)
XLA Ops:
  0.6 103.1 %step.1 = (bf16[128,512]{1,0:T(8,128)(2,1)S(1)}, f32[1,128]{1,0:T(1,128)S(1)}) custom-call(bf16[2,4096]{1,0:T(2,128)(2,1)} %refs_0_.1, bf16[2,512,2048]{2,1,0:T(8,128)(2,1)} %refs_1_.1, s32[128]{0:T(128)} %refs_2_.1, s32[1,128]{1,0:T(1,128)} %bitcast.8, f32[3,4096]{1,0:T(4,128)} %refs_4_.1, bf16[48,4096]{1,0:T(8,128)(2,1)} %bitcast.6, ...), custom_call_target="tpu_custom_call" | custom-call | tf_op jit(solution)/shard_map/step/pallas_call | solution.py:754
  103.7 0.7 result.1

commit v9 on v8

--- a/solution.py
+++ b/solution.py
@@ -19,7 +19,8 @@
 B = 128
 QN = 384
 ZORDER = (4, 3, 5, 2, 6, 1, 7)
-NEAR_Z = (7, 0, 1)
+ARRIVAL = (0, 1, 7, 2, 6, 3, 5, 4)
+GROUPS = ((0, 3), (3, 2), (5, 3))
 NCH, CA, CB = 4, 512, 512
 WA, WB = NCH * CA, NCH * CB
 BA, BB = CA // 128, CB // 128
@@ -86,14 +87,14 @@
     fr=VM((16, 128), F32),
     fb=VM((NP, NZ, 16, 128), BF),
     ff=VM((2048, 128), F32),
-    lh=VM((B, HALF), BF),
+    lh=VM((B, HALF), F32),
     lp=VM((B, VD), F32),
     lr=VM((B, VD), F32),
     sz=VM((NZ, 8, 128), F32),
     sx=VM((NP, 8, 128), F32),
 )
 PHASES = dict(
-    wq=1, wqf=1, wo=1, s1=1, s2=1, s3=1, s4=1, s5=1, s6=1, s7=1, s8=7, da=12, db=6, dg=9,
+    wq=1, wqf=1, wo=1, s1=1, s2=1, s3=1, s4=1, s5=1, s6=1, s7=1, s8=7, da=18, db=9, dg=9,
     xg=2, xd=2, fg=2, fd=2, xh=2, fi=1, fh=1, fo=1, fy=1,
     a1=NCH, b1=NCH, a2=NCH, b2=NCH, s13=NCH, fx=1, s14=7, s15=8, lx=1, s16=1, s17=1,
 )
@@ -172,8 +173,8 @@
         sent(phase, ref)
 
     bar = pltpu.get_barrier_semaphore()
-    peers = [at_z(zz) for zz in zpeers] + [at_xy(*k) for k in plane] + [partner]
-    peers += [across_z(zz) for zz in zpeers]
+    peers = [dev for zz in zpeers for dev in (at_z(zz), across_z(zz))]
+    peers = peers[:6] + [at_xy(*k) for k in plane] + peers[6:] + [partner]
     for dev in peers:
         pl.semaphore_signal(bar, inc=1, device_id=dev, device_id_type=MESH)
 
@@ -421,7 +422,7 @@
         acc = acc + r.s7r[s].astype(F32)
 
     def tile_rows(d):
-        return pl.ds((d + 1) % NZ * 16, 16)
+        return pl.ds(ARRIVAL.index(d % NZ) * 16, 16)
 
     for j in range(2):
         r.mc[j, tile_rows(0), :] = acc[j * 16 : j * 16 + 16].astype(BF)
@@ -431,7 +432,8 @@
 
     def tile_on(k):
         rows = tile_rows(k)
-        late = 0 if k in NEAR_Z else 1
+        at = ARRIVAL.index(k)
+        late = next(i for i, (a, b) in enumerate(GROUPS) if a <= at < a + b)
         for d in (2, 1, 3):
             xx, yy = rem(x + d, NX), rem(y + d, NY)
             at = r.mid.at[n, rows]
@@ -465,7 +467,7 @@
         sent(k, mine_d)
     for k in (local.wg, local.wd):
         k.wait()
-    for d in (1, 7, 2, 6, 3, 5, 4):
+    for d in ARRIVAL[1:]:
         recv(p.s8, r.mc.at[:, 0:16], d - 1)
         tile_on(d)
     sent(p.s8, r.mc.at[:, 0:112])
@@ -499,7 +501,7 @@
             )
 
     ffn_chunk(n)
-    for late, rows in enumerate((pl.ds(0, 48), pl.ds(48, 80))):
+    for late, rows in enumerate(pl.ds(a * 16, b * 16) for a, b in GROUPS):
         for d in near:
             m = rem(x + d, NX) * 4 + y
             recv(p.da, r.mid.at[m, rows], d - 1 + 6 * late)
@@ -568,7 +570,7 @@
         for cols in (chunk(ch), high(ch)):
             v = jnp.dot(r.hid[...], r.wd[:, cols], preferred_element_type=F32)
             for k in range(NZ):
-                r.p3[rem(z + k + NZ - 1, NZ), :, cols] = v[k * 16 : k * 16 + 16].astype(BF)
+                r.p3[rem(z + ARRIVAL[k], NZ), :, cols] = v[k * 16 : k * 16 + 16].astype(BF)
         a1(ch)
         for d in (2, 1, 3):
             b1(ch, rem(y + d, NY))
@@ -606,7 +608,10 @@
 
     row16 = lax.broadcasted_iota(jnp.int32, (16, 128), 0)
     own_row = rem(row16, 8) == z
-    tile16 = pl.ds(pl.multiple_of(rem(xl * 4 + y - z + NZ + 1, NZ) * 16, 16), 16)
+    away = rem(xl * 4 + y - z + NZ, NZ)
+    turn = (away + 3) // 4
+    slot = turn * (2 - turn) * (2 * away - 1) + turn * (turn - 1) // 2 * (16 - 2 * away)
+    tile16 = pl.ds(pl.multiple_of(slot * 16, 16), 16)
 
     def parts(ch):
         return (ch * BA, BA), (NCH * BA + ch * BB, BB)
@@ -676,26 +681,25 @@
     local.lm.wait()
     local.tg.wait()
     wanted = jnp.broadcast_to(r.tg[...].astype(F32), (B, B)).T[:, 0:1]
-    for d in (1, 7, 2, 6, 3, 5, 4):
+    for d in ARRIVAL[1:]:
         zz = rem(z + d, NZ)
         recv(p.s14, r.fb.at[own, zz], d - 1)
         xy_send(p.s15, lambda m: r.fb.at[own, zz], r.fb.at[own, zz], d)
     sent(p.s14, r.fb.at[own, 0:7])
-    for d in (0, 1, 7, 2, 6, 3, 5, 4):
+    for d in ARRIVAL:
         zz = rem(z + d, NZ)
         recv(p.s15, r.fb.at[0:15, zz], d)
         for k in range(NP):
             at = pl.ds(pl.multiple_of(k * 128 + zz * 16, 16), 16)
             r.ff[at, :] = r.fb[k, zz].astype(F32)
+        for h in range(2):
+            to = pl.ds(pl.multiple_of(h * 64 + zz * 8, 8), 8)
+            for b in range(16):
+                r.lh[to, b * 128 : (b + 1) * 128] = r.ff[
+                    pl.ds(h * 1024 + zz * 16 + b, 8, stride=128), :
+                ]
     sent(p.s15, r.fb.at[0:15])
-    for b in range(16):
-        rows = [
-            r.ff[pl.ds(h * 1024 + zz * 16 + b, 8, stride=128), :]
-            for h in range(2)
-            for zz in range(NZ)
-        ]
-        r.lh[:, b * 128 : (b + 1) * 128] = jnp.concatenate(rows, axis=0).astype(BF)
-    r.lp[...] = jnp.dot(r.lh[...], r.lm[...], preferred_element_type=F32)
+    r.lp[...] = jnp.dot(r.lh[...].astype(BF), r.lm[...], preferred_element_type=F32)
     send(p.lx, r.lp, r.lr, partner)
     done(p.lx, r.lr)
     mean_f = r.lp[...] + r.lr[...]

time: 106 us -> 105 us (level); the launches traced: 104 us -> 105 us
  no operation moved by 1% of the time
where the time goes in v9:
time: 105 us
  Pallas kernels  104 us (99%)
    pallas_call x1, Pallas kernels, body(): pl.pallas_call(functools.partial(kernel, list(args)), out_shape=[VM(k.sha...  103 us

profile of v9, /device:TPU:32, one launch (start us, length us, event | category | flops | bytes accessed | tf_op | source)
XLA Modules:
  0.0 104.6 jit_solution(7526435349942260095)
XLA Ops:
  0.6 103.3 %step.1 = (bf16[128,512]{1,0:T(8,128)(2,1)S(1)}, f32[1,128]{1,0:T(1,128)S(1)}) custom-call(bf16[2,4096]{1,0:T(2,128)(2,1)} %refs_0_.1, bf16[2,512,2048]{2,1,0:T(8,128)(2,1)} %refs_1_.1, s32[128]{0:T(128)} %refs_2_.1, s32[1,128]{1,0:T(1,128)} %bitcast.8, f32[3,4096]{1,0:T(4,128)} %refs_4_.1, bf16[48,4096]{1,0:T(8,128)(2,1)} %bitcast.6, ...), custom_call_target="tpu_custom_call" | custom-call | tf_op jit(solution)/shard_map/step/pallas_call | solution.py:758
  104.0 0.7 result.1

commit v10 on v9

--- a/solution.py
+++ b/solution.py
@@ -19,6 +19,7 @@
 B = 128
 QN = 384
 ZORDER = (4, 3, 5, 2, 6, 1, 7)
+FAR_Z = (3, 5, 4)
 ARRIVAL = (0, 1, 7, 2, 6, 3, 5, 4)
 GROUPS = ((0, 3), (3, 2), (5, 3))
 NCH, CA, CB = 4, 512, 512
@@ -96,7 +97,7 @@
 PHASES = dict(
     wq=1, wqf=1, wo=1, s1=1, s2=1, s3=1, s4=1, s5=1, s6=1, s7=1, s8=7, da=18, db=9, dg=9,
     xg=2, xd=2, fg=2, fd=2, xh=2, fi=1, fh=1, fo=1, fy=1,
-    a1=NCH, b1=NCH, a2=NCH, b2=NCH, s13=NCH, fx=1, s14=7, s15=8, lx=1, s16=1, s17=1,
+    a1=NCH, b1=NCH, a2=NCH, b2=NCH, s13=NCH, fx=1, s14=7, s15=8, pz=8, lx=1, s16=1, s17=1,
 )
 LS = dict(ls=DMA((16,)))
 OUTS = dict(
@@ -527,13 +528,10 @@
 
     lax.fori_loop(0, 3, line_step, 0)
 
-    def diag_step(i, carry):
-        m = rem(x + 1 + i // 3, NX) * 4 + rem(y + 1 + i % 3, NY)
-        recv(p.dg, r.mid.at[m], i)
+    for dx, dy in sorted(((a, b) for a in near for b in near), key=lambda k: k.count(2)):
+        m = rem(x + dx, NX) * 4 + rem(y + dy, NY)
+        recv(p.dg, r.mid.at[m], (dx - 1) * 3 + dy - 1)
         ffn_chunk(m)
-        return carry
-
-    lax.fori_loop(0, 9, diag_step, 0)
     scale = lax.rsqrt(jnp.sum(r.ssq[...], axis=1, keepdims=True) * (1.0 / D) + 1e-5)
 
     def by_member(k):
@@ -675,20 +673,27 @@
     send(p.fx, r.fs.at[half(1 - c)], r.fr, partner)
     done(p.fx, r.fr)
     r.fb[own, z] = ((r.fs[half(c), :] + r.fr[...]) * 0.25).astype(BF)
-    for d in ZORDER:
+    for d in FAR_Z:
         send(p.s14, r.fb.at[own, z], r.fb.at[own, z], at_z(rem(z + d, NZ)), 7 - d)
     xy_send(p.s15, lambda m: r.fb.at[own, z], r.fb.at[own, z], 0)
     local.lm.wait()
     local.tg.wait()
     wanted = jnp.broadcast_to(r.tg[...].astype(F32), (B, B)).T[:, 0:1]
-    for d in ARRIVAL[1:]:
+    for d in FAR_Z:
         zz = rem(z + d, NZ)
         recv(p.s14, r.fb.at[own, zz], d - 1)
         xy_send(p.s15, lambda m: r.fb.at[own, zz], r.fb.at[own, zz], d)
-    sent(p.s14, r.fb.at[own, 0:7])
+    sent(p.s14, r.fb.at[own, 0:3])
+    recv(p.s15, r.fb.at[0:15, z], 0)
+    for d in (2, 6, 1, 7):
+        send(p.pz, r.fb.at[:, z], r.fb.at[:, z], at_z(rem(z + d, NZ)), 8 - d)
+    sent(p.pz, r.fb.at[:, 0:4])
     for d in ARRIVAL:
         zz = rem(z + d, NZ)
-        recv(p.s15, r.fb.at[0:15, zz], d)
+        if d in FAR_Z:
+            recv(p.s15, r.fb.at[0:15, zz], d)
+        elif d:
+            recv(p.pz, r.fb.at[:, zz], d)
         for k in range(NP):
             at = pl.ds(pl.multiple_of(k * 128 + zz * 16, 16), 16)
             r.ff[at, :] = r.fb[k, zz].astype(F32)
@@ -698,7 +703,7 @@
                 r.lh[to, b * 128 : (b + 1) * 128] = r.ff[
                     pl.ds(h * 1024 + zz * 16 + b, 8, stride=128), :
                 ]
-    sent(p.s15, r.fb.at[0:15])
+    sent(p.s15, r.fb.at[0:15, 0:4])
     r.lp[...] = jnp.dot(r.lh[...].astype(BF), r.lm[...], preferred_element_type=F32)
     send(p.lx, r.lp, r.lr, partner)
     done(p.lx, r.lr)

time: 105 us -> 105 us (level); the launches traced: 105 us -> 103 us
  Pallas kernels: 104 us -> 102 us
    pallas_call x1, Pallas kernels: 103 us -> 102 us  [body(): pl.pallas_call(functools.partial(kernel, list(args)), out_shape=[VM(k.sha...]
where the time goes in v10:
time: 105 us; the launch traced here: 103 us
  Pallas kernels  102 us (97%)
    pallas_call x1, Pallas kernels, body(): pl.pallas_call(functools.partial(kernel, list(args)), out_shape=[VM(k.sha...  102 us

profile of v10, /device:TPU:32, one launch (start us, length us, event | category | flops | bytes accessed | tf_op | source)
XLA Modules:
  0.0 103.1 jit_solution(7038625242905229979)
XLA Ops:
  0.6 101.7 %step.1 = (bf16[128,512]{1,0:T(8,128)(2,1)S(1)}, f32[1,128]{1,0:T(1,128)S(1)}) custom-call(bf16[2,4096]{1,0:T(2,128)(2,1)} %refs_0_.1, bf16[2,512,2048]{2,1,0:T(8,128)(2,1)} %refs_1_.1, s32[128]{0:T(128)} %refs_2_.1, s32[1,128]{1,0:T(1,128)} %bitcast.8, f32[3,4096]{1,0:T(4,128)} %refs_4_.1, bf16[48,4096]{1,0:T(8,128)(2,1)} %bitcast.6, ...), custom_call_target="tpu_custom_call" | custom-call | tf_op jit(solution)/shard_map/step/pallas_call | solution.py:763
  102.4 0.7 result.1
